TPU v7x, 256 devices: a whole 4x4x8 slice. The times are simulated.
256 devices in a mesh: obs: 64 (over z, y, core), rep: 4 (over x).
Axes of the slice: x: 4, y: 4, z: 8, core: 2. Of those that a mesh axis runs over, the one named last changes fastest.
Arguments:
- jacobians: float32 [18, 8388608], P(None, ('obs', 'rep')), may hold values from -3 to 3
- residuals: float32 [2, 8388608], P(None, ('obs', 'rep')), may hold values from -6 to 6
- camera_local: int32 [8388608], P(('obs', 'rep')), may hold values from 0 to 1023
- bucket_counts: int32 [256, 64], P(('obs', 'rep')), may hold values from 1 to 512, as said below
- camera_map: int32 [65536], replicated, may hold values from 0 to 65535, each once
Outputs:
- gradient: float32 [9, 65536], replicated
- camera_blocks: float32 [81, 65536], P(None, 'obs')
Inputs may be any that keep to these rules, and one draw needn't show every extreme that they name: bucket_counts[s, d] counts the leading live slots of bucket d of source block s; exactly one destination d has all 512 slots live from every source block, and every other bucket has at most 256 live slots. A slot in bucket d names camera slot d * 1024 + camera_local. `camera_map`: each camera id appears once.
All inputs are finite; a program needn't handle non-finite values.
Results may differ from a plain program's by a relative error of at most 0.0003.
Values sent between devices are 32-bit elements; how exact they have to be, the bound alone decides.
No kernel may reach another device: no remote copies, remote signals or barrier semaphores. Data moves between devices by JAX's collectives and lax.ppermute only.
A program may use at most 192 MiB of HBM per device.

v0:
```python
import math

import jax
import jax.numpy as jnp
from jax import lax
from jax.sharding import Mesh
from jax.sharding import PartitionSpec as P

CAM_DEV = 1024
OBS = ("obs_0", "obs_1", "obs_2")
OBS_REP = ("obs_0", "obs_1", "obs_2", "rep")


def sent_together(arrays, axis, split_dim, concat_dim, along):
    widths = [a.shape[along] for a in arrays]
    both = jnp.concatenate(arrays, axis=along)
    filled = lax.all_to_all(both, axis, split_axis=split_dim, concat_axis=concat_dim, tiled=True)
    return tuple(jnp.split(filled, [sum(widths[:k]) for k in range(1, len(widths))], axis=along))


def split_up(shard, dim, count):
    shape = shard.shape
    pieces = shard.reshape(*shape[:dim], count, shape[dim] // count, *shape[dim + 1 :])
    return jnp.moveaxis(pieces, dim, 0)


def summed_on_arrival(shard, axis, dim):
    pieces = split_up(shard, dim, lax.axis_size(axis))
    arrived = lax.all_to_all(pieces, axis, split_axis=0, concat_axis=0, tiled=True)
    return arrived.sum(axis=0)


def side_by_side(arrays, axis, dim, along):
    both = jnp.concatenate(arrays, axis=along)
    filled, at, finished = (summed_on_arrival(both, axis, dim), 0, [])
    for a in arrays:
        finished.append(lax.slice_in_dim(filled, at, at + a.shape[along], axis=along))
        at += a.shape[along]
    return tuple(finished)


def in_order(pieces, dim):
    shape = list(pieces.shape[1:])
    shape[dim] *= pieces.shape[0]
    return jnp.moveaxis(pieces, 0, dim).reshape(shape)


def stacked_from(shard, axes, order):
    pieces = shard[None]
    for k in order:
        pieces = lax.all_gather(pieces, axes[k], axis=0, tiled=True)
    carried = [lax.axis_size(axes[k]) for k in reversed(order)]
    pieces = pieces.reshape(*carried, *shard.shape)
    turned = sorted(range(len(order)), key=lambda place: order[len(order) - 1 - place])
    return pieces.transpose(*turned, *range(len(order), pieces.ndim)).reshape(-1, *shard.shape)


def whole_of(shard, axes, order, dim):
    return in_order(stacked_from(shard, axes, order), dim)


def sent_to_all(shard, axis):
    count = lax.axis_size(axis)
    return lax.all_to_all(
        jnp.broadcast_to(shard[None], (count, *shard.shape)), axis, 0, 0, tiled=True
    )


def gather_directly(shard, axis, dim):
    return in_order(sent_to_all(shard, axis), dim)


def observation_terms(jacobs, resids):
    leading_row = jacobs[0:9]
    trailing_row = jacobs[9:18]
    gradient_terms = leading_row * resids[0:1] + trailing_row * resids[1:2]
    block_terms = (
        leading_row[:, None] * leading_row[None, :] + trailing_row[:, None] * trailing_row[None, :]
    )
    block_terms = block_terms.reshape((81,) + leading_row.shape[1:])
    return jnp.concatenate([gradient_terms, block_terms], axis=0)


def grouped_sums(jac_flat, res_flat, ids_flat, live_flat, width):
    total = jac_flat.shape[1]
    groups = total // width
    camera_rows = lax.broadcasted_iota(jnp.int32, (CAM_DEV, 1), 0)

    def add_group(index, summed):
        start = index * width
        jac_piece = lax.dynamic_slice_in_dim(jac_flat, start, width, 1)
        res_piece = lax.dynamic_slice_in_dim(res_flat, start, width, 1)
        id_piece = lax.dynamic_slice_in_dim(ids_flat, start, width, 0)
        live_piece = lax.dynamic_slice_in_dim(live_flat, start, width, 0)[None, :]
        terms = observation_terms(jac_piece * live_piece, res_piece * live_piece)
        one_hot = (id_piece[None, :] == camera_rows).astype(jnp.float32)
        added = lax.dot_general(
            terms,
            one_hot,
            (((1,), (1,)), ((), ())),
            precision=lax.Precision.HIGHEST,
            preferred_element_type=jnp.float32,
        )
        return summed + added

    return lax.fori_loop(0, groups, add_group, jnp.zeros((90, CAM_DEV), jnp.float32))


def group_width(senders, width):
    return math.gcd(senders, max(1, 2048 // width)) * width


def local(jacobians, residuals, camera_local, bucket_counts, camera_map):
    senders = lax.axis_size(OBS)
    capacity = jacobians.shape[1] // senders
    jac_split = jacobians.reshape(18, senders, capacity)
    res_split = residuals.reshape(2, senders, capacity)
    ids_split = camera_local.reshape(1, senders, capacity)
    counts_here = bucket_counts.reshape(1, senders, 1)
    moved_jac, moved_res = sent_together((jac_split, res_split), OBS, 1, 1, 0)
    moved_ids, moved_counts = sent_together((ids_split, counts_here), OBS, 1, 1, 2)
    within = lax.broadcasted_iota(jnp.int32, (1, senders, capacity), 2)
    live_mask = (within < moved_counts).astype(jnp.float32)
    summed = grouped_sums(
        moved_jac.reshape(18, senders * capacity),
        moved_res.reshape(2, senders * capacity),
        moved_ids.reshape(senders * capacity),
        live_mask.reshape(senders * capacity),
        group_width(senders, capacity),
    )
    grad_part = summed[:9]
    block_part = summed[9:]
    grad_share, block_share = side_by_side((grad_part, block_part), "rep", 1, 0)
    grad_slots = whole_of(grad_share, OBS_REP, (0, 1, 3, 2), 1)
    blocks_out = gather_directly(block_share, "rep", 1)
    gradient = (
        jnp.zeros(grad_slots.shape, jnp.float32)
        .at[:, camera_map]
        .set(grad_slots, unique_indices=True)
    )
    return (gradient, blocks_out)


def solution(mesh):
    split = Mesh(
        mesh.devices.reshape(8, 4, 2, mesh.shape["rep"]), ("obs_0", "obs_1", "obs_2", "rep")
    )
    return jax.shard_map(
        local,
        mesh=split,
        in_specs=(P(None, OBS_REP), P(None, OBS_REP), P(OBS_REP), P(OBS_REP, None), P()),
        out_specs=(P(), P(None, OBS)),
        check_vma=False,
    )
```

profile of v0, /device:TPU:1, one launch (start us, length us, event | category | flops | bytes accessed | tf_op | source)
XLA Modules:
  0.0 553.7 jit_solution(11730834584020948406)
XLA Ops:
  9.7 13.1 %all-to-all-start.1 = ((s32[1,64,513]{2,0,1:T(1,128)}), s32[1,64,513]{2,0,1:T(1,128)S(1)}, u32[]{:S(2)}, u32[]{:S(2)}) async-start(s32[1,64,513]{2,0,1:T(1,128)} %copy.22), calls=%async_computation.1 | async-start | bytes 327680 | tf_op jit(solution)/shard_map/all_to_all | solution.py:17
  22.8 3.7 copy.30
  34.5 6.9 %all-to-all-start = ((f32[20,64,512]{2,0,1:T(8,128)}), f32[20,64,512]{2,0,1:T(8,128)S(1)}, u32[]{:S(2)}, u32[]{:S(2)}) async-start(f32[20,64,512]{2,0,1:T(8,128)} %copy.19), calls=%async_computation | async-start | bytes 6291456 | tf_op jit(solution)/shard_map/all_to_all | solution.py:17
  43.8 70.0 %all-to-all-done = f32[20,64,512]{2,0,1:T(8,128)S(1)} async-done(((f32[20,64,512]{2,0,1:T(8,128)}), f32[20,64,512]{2,0,1:T(8,128)S(1)}, u32[]{:S(2)}, u32[]{:S(2)}) %all-to-all-start) | async-done | bytes 2621472 | tf_op jit(solution)/shard_map/all_to_all | solution.py:17
  119.3 118.1 %while.14 = (s32[]{:T(128)}, f32[90,1024]{1,0:T(8,128)}, f32[18,32768]{1,0:T(8,128)}, f32[32768]{0:T(1024)}, f32[2,32768]{1,0:T(2,128)S(1)}, /*index=5*/s32[3276...) while((s32[]{:T(128)}, f32[90,1024]{1,0:T(8,128)}, f32[18,32768]{1,0:T(8,128)}, ...), condition=%wide.region_1.0_spmd.clone, body=%wide.region_0.0_spmd.clone.sunk | while | flops 2267983872 | bytes 7364837 | solution.py:106
  121.4 4.6 fusion.17
  128.8 4.6 fusion.17
  136.1 4.6 fusion.17
  143.5 4.6 fusion.17
  150.9 4.6 fusion.17
  158.3 4.6 fusion.17
  165.6 4.6 fusion.17
  173.0 4.6 fusion.17
  180.4 4.6 fusion.17
  187.8 4.6 fusion.17
  195.2 4.6 fusion.17
  202.5 4.6 fusion.17
  209.9 4.6 fusion.17
  217.3 4.6 fusion.17
  224.7 4.6 fusion.17
  232.0 4.6 fusion.17
  238.6 10.0 %all_to_all.20 = f32[4,90,256]{2,1,0:T(8,128)S(1)} all-to-all(f32[4,90,256]{2,1,0:T(8,128)S(1)} %copy.23), channel_id=1, replica_groups=mesh['obs_0'=8,'obs_1'=4,'obs_2'=2,'rep'=4] {'rep'}, dimensions={0} | all-to-all | bytes 737280 | tf_op jit(solution)/shard_map/all_to_all | solution.py:29
  248.7 21.8 %all-gather.1 = f32[8,9,256]{2,1,0:T(8,128)S(1)} all-gather(f32[1,9,256]{2,1,0:T(8,128)S(1)} %slice_bitcast_fusion), channel_id=2, replica_groups=mesh['obs_0'=8,'obs_1'=4,'obs_2'=2,'rep'=4] {'obs_0'}, dimensions={0}, use_global_device_ids=true | all-gather | bytes 82944 | tf_op jit(solution)/shard_map/all_gather | solution.py:51
  270.6 10.2 %all_gather.13 = f32[32,9,256]{2,0,1:T(8,128)} all-gather(f32[8,9,256]{2,0,1:T(8,128)S(1)} %copy.24), channel_id=1, replica_groups=mesh['obs_0'=8,'obs_1'=4,'obs_2'=2,'rep'=4] {'obs_1'}, dimensions={0}, use_global_device_ids=true | all-gather | bytes 368640 | tf_op jit(solution)/shard_map/all_gather | solution.py:51
  280.8 28.4 %all-gather.5.cloned.1.call-done = f32[128,9,256]{2,0,1:T(8,128)} async-done(((f32[32,9,256]{2,0,1:T(8,128)}), f32[128,9,256]{2,0,1:T(8,128)}) %all-gather.5.cloned.1.call-update) | async-done | bytes 1179664 | tf_op jit(solution)/shard_map/all_gather | solution.py:51
  310.0 3.7 all-to-all-start.3
  313.7 6.0 %all-to-all-done.3 = f32[4,81,256]{2,1,0:T(8,128)S(1)} async-done(((f32[4,81,256]{2,1,0:T(8,128)}), f32[4,81,256]{2,1,0:T(8,128)S(1)}, u32[]{:S(2)}, u32[]{:S(2)}) %all-to-all-start.3) | async-done | bytes 331808 | tf_op jit(solution)/shard_map/all_to_all | solution.py:64
  320.7 10.1 %all-gather.7.cloned.1.call-done = f32[256,9,256]{2,0,1:T(8,128)} async-done(((f32[128,9,256]{2,0,1:T(8,128)}), f32[256,9,256]{2,0,1:T(8,128)}) %all-gather.7.cloned.1.call-update) | async-done | bytes 2359312 | tf_op jit(solution)/shard_map/all_gather | solution.py:51
  330.8 4.6 copy.37
  338.1 16.6 %copy.29 = f32[9,256,256]{0,2,1:T(8,128)} copy(f32[9,256,256]{2,1,0:T(8,128)S(1)} %bitcast.45) | data formatting | bytes 4718592 | tf_op jit(solution)/shard_map/reshape | solution.py:45
  354.7 172.8 %scatter_custom_fusion = f32[9,65536]{0,1:T(8,128)} fusion(s32[65536]{0:T(1024)S(1)} %compare_select_fusion, f32[65536,9]{1,0:T(8,128)} %bitcast.41, f32[]{:T(128)} %constant.34.clone.1), kind=kCustom, calls=%fused_computation.14 | custom fusion | bytes 2359808 | tf_op jit(solution)/shard_map/scatter | solution.py:139
  527.5 19.4 %copy.28 = f32[9,65536]{1,0:T(8,128)} copy(f32[9,65536]{0,1:T(8,128)} %scatter_custom_fusion) | data formatting | bytes 4718592
  (235 shorter events, 68.0 us)
Async XLA Ops:
  9.7 24.8 %all-to-all-start.1 = ((s32[1,64,513]{2,0,1:T(1,128)}), s32[1,64,513]{2,0,1:T(1,128)S(1)}, u32[]{:S(2)}, u32[]{:S(2)}) async-start(s32[1,64,513]{2,0,1:T(1,128)} %copy.22), calls=%async_computation.1 | async-start | bytes 327680 | tf_op jit(solution)/shard_map/all_to_all | solution.py:17
  26.6 1.0 copy-start.3
  34.5 7.2 %copy-start = (s32[1,64,513]{2,0,1:T(1,128)}, s32[1,64,513]{2,0,1:T(1,128)S(1)}, u32[]{:S(2)}) copy-start(s32[1,64,513]{2,0,1:T(1,128)S(1)} %all-to-all-done.1) | copy-start | bytes 393988
  34.5 79.4 %all-to-all-start = ((f32[20,64,512]{2,0,1:T(8,128)}), f32[20,64,512]{2,0,1:T(8,128)S(1)}, u32[]{:S(2)}, u32[]{:S(2)}) async-start(f32[20,64,512]{2,0,1:T(8,128)} %copy.19), calls=%async_computation | async-start | bytes 6291456 | tf_op jit(solution)/shard_map/all_to_all | solution.py:17
  41.4 267.8 %all-gather.5.cloned.1.call-start = ((), (), s32[]{:S(2)}) async-start(), calls=%async_computation.4 | async-start | bytes 1474560 | tf_op jit(solution)/shard_map/all_gather | solution.py:51
  115.6 3.6 slice-start
  119.3 2.1 copy-start.1
  125.9 0.7 copy-start.2
  126.7 2.1 copy-start.1
  133.3 0.7 copy-start.2
  134.1 2.1 copy-start.1
  140.7 0.7 copy-start.2
  141.4 2.1 copy-start.1
  148.1 0.7 copy-start.2
  148.8 2.1 copy-start.1
  155.5 0.7 copy-start.2
  156.2 2.1 copy-start.1
  162.8 0.7 copy-start.2
  163.6 2.1 copy-start.1
  170.2 0.7 copy-start.2
  171.0 2.1 copy-start.1
  178.3 2.1 copy-start.1
  185.7 2.1 copy-start.1
  193.1 2.1 copy-start.1
  200.5 2.1 copy-start.1
  207.8 2.1 copy-start.1
  215.2 2.1 copy-start.1
  222.6 2.1 copy-start.1
  230.0 2.1 copy-start.1
  237.3 76.3 %copy-start.4 = (s32[65536]{0:T(1024)S(1)}, s32[65536]{0:T(1024)}, u32[]{:S(2)}) copy-start(s32[65536]{0:T(1024)} %param.11) | copy-start | bytes 786436
  280.8 50.0 %all-gather.7.cloned.1.call-start = ((), (), s32[]{:S(2)}) async-start(), calls=%async_computation.5 | async-start | bytes 3538944 | tf_op jit(solution)/shard_map/all_gather | solution.py:51
  310.0 9.7 %all-to-all-start.3 = ((f32[4,81,256]{2,1,0:T(8,128)}), f32[4,81,256]{2,1,0:T(8,128)S(1)}, u32[]{:S(2)}, u32[]{:S(2)}) async-start(f32[4,81,256]{2,1,0:T(8,128)} %broadcast_in_dim.40), calls=%async_computation.3 | async-start | bytes 720896 | tf_op jit(solution)/shard_map/all_to_all | solution.py:64
  (9 other events, 6.7 us)
Sparse Core Ops, SparseCore 0:
  280.9 28.2 all-gather.4
  311.0 19.7 all-gather.6
where the time goes:
time: 555 us; the launch traced here: 554 us
  local copies, waits for them, and re-layouts  262 us (47%)
  waiting for transfers between devices  118 us (21%)
  matrix products  72.9 us (13%)
  blocking collectives  42 us (8%)
  starting transfers between devices  24 us (4%)
  other arithmetic  19.5 us (4%)
  between operations  14.2 us (3%)
    scatter x1, local copies, waits for them, and re-layouts, local(): gradient = jnp.zeros(grad_slots.shape, jnp.float32).at[:, camera_map].set...  173 us
    all_to_all x2, waiting for transfers between devices, sent_together(): lax.all_to_all(both, axis, split_axis=split_dim, concat_axis=concat_dim,...  73.4 us
    dot_general x16, matrix products, add_group(): lax.dot_general(terms, one_hot, (((1,), (1,)), ((), ())), precision=lax.P...  72.9 us
    all_gather x2, waiting for transfers between devices, stacked_from(): pieces = lax.all_gather(pieces, axes[k], axis=0, tiled=True)  38.4 us
    all_gather x2, blocking collectives, stacked_from(): pieces = lax.all_gather(pieces, axes[k], axis=0, tiled=True)  32 us
    unnamed x16, local copies, waits for them, and re-layouts  28.7 us
    all_to_all x2, starting transfers between devices, sent_together(): lax.all_to_all(both, axis, split_axis=split_dim, concat_axis=concat_dim,...  20.1 us
    reshape x1, local copies, waits for them, and re-layouts, in_order(): return jnp.moveaxis(pieces, 0, dim).reshape(shape)  16.6 us
  transfers between devices with their start and end apart: 5, of which 5 were waited for; matrix products, arithmetic and copies ran while one was open for 2% of the time, Pallas kernels for 0%

commit v1 on v0

v1 whole, which is shorter than its diff:
```python
import jax
import jax.numpy as jnp
from jax import lax
from jax.experimental import pallas as pl
from jax.experimental.pallas import tpu as pltpu
from jax.sharding import Mesh
from jax.sharding import PartitionSpec as P

CAM_DEV = 1024
HALF = 256
LANES = 128
SPAN = 256
QUARTERS = CAM_DEV // SPAN
CAMS = 9
PAIRS = 45
TERMS = 56
VALUES = 21
BLOCK = 28
HOT_ROWS = 7
OBS = ("z", "y", "c")
PLANE = ("y", "c", "x")
ALL = ("z", "y", "c", "x")
F32 = jnp.float32
BF16 = jnp.bfloat16
VMEM = pl.BlockSpec(memory_space=pltpu.VMEM)
SMEM = pl.BlockSpec(memory_space=pltpu.SMEM)


def two_pieces(x):
    upper = x.astype(BF16).astype(F32)
    return jnp.concatenate([upper, x - upper], axis=0).astype(BF16)


def kept_where(x, row, value):
    rows, lanes = x.shape
    kept = jnp.broadcast_to(row, (16, lanes)) == value
    kept = jnp.where(kept, 1.0, 0.0).astype(BF16)
    return (x.reshape(rows // 16, 16, lanes) * kept[None]).reshape(rows, lanes)


def one_hot(row):
    lanes = row.shape[1]
    spread = lax.broadcasted_iota(jnp.int32, (SPAN, lanes), 0) == row
    return jnp.where(spread, 1.0, 0.0).astype(BF16)


def product(left, right):
    return lax.dot_general(left, right, (((1,), (1,)), ((), ())), preferred_element_type=F32)


def set_operands(left_ref, right_ref, x, ids, parts, at):
    pieces = two_pieces(x)
    rows = pieces.shape[0]
    upper, lower = jnp.right_shift(ids, 8), jnp.bitwise_and(ids, SPAN - 1)
    for part in range(parts):
        left_ref[part * rows : (part + 1) * rows, at : at + LANES] = kept_where(pieces, upper, part)
    right_ref[:, at : at + LANES] = one_hot(lower)


def pack_body(counts_ref, jac_ref, res_ref, cam_ref, out_ref, terms_ref, left_ref, right_ref):
    targets = out_ref.shape[0]
    capacity = jac_ref.shape[1] // targets

    def send(target, hot):
        count = counts_ref[0, target]
        for half in range(2):
            at = pl.multiple_of(target * capacity + half * LANES, LANES)
            here = pl.ds(at, LANES)
            live = lax.broadcasted_iota(jnp.int32, (1, LANES), 1) + half * LANES < count
            row = half * BLOCK
            out_ref[target, row : row + 18, :] = jnp.where(live, jac_ref[:, here], 0.0)
            out_ref[target, row + 18 : row + 20, :] = jnp.where(live, res_ref[:, here], 0.0)
            out_ref[target, row + 20 : row + 21, :] = cam_ref[:, here].astype(F32)
        return jnp.where(count > HALF, target, hot)

    hot = lax.fori_loop(0, targets, send, 0)
    for half in range(2):
        at = pl.multiple_of(hot * capacity + HALF + half * LANES, LANES)
        here = pl.ds(at, LANES)
        count = counts_ref[0, hot]
        live = lax.broadcasted_iota(jnp.int32, (1, LANES), 1) + HALF + half * LANES < count
        jac = jnp.where(live, jac_ref[:, here], 0.0)
        res = jnp.where(live, res_ref[:, here], 0.0)
        ids = cam_ref[:, here]
        first, second = jac[:CAMS], jac[CAMS:]
        for turn in range(5):
            around = first if turn == 0 else jnp.concatenate([first[turn:], first[:turn]], axis=0)
            beside = second if turn == 0 else jnp.concatenate([second[turn:], second[:turn]], axis=0)
            terms_ref[CAMS * turn : CAMS * (turn + 1), :] = first * around + second * beside
        terms_ref[PAIRS : PAIRS + CAMS, :] = first * res[0:1] + second * res[1:2]
        terms_ref[PAIRS + CAMS : TERMS, :] = jnp.zeros((TERMS - PAIRS - CAMS, LANES), F32)
        set_operands(left_ref, right_ref, terms_ref[...], ids, QUARTERS, half * LANES)
    summed = product(left_ref[...], right_ref[...])
    for share in range(targets):
        rows, column = HOT_ROWS * (share // 8), LANES * (share % 8)
        start = 2 * TERMS * (column // SPAN) + rows
        lanes = slice(column % SPAN, column % SPAN + LANES)
        piece = (
            summed[start : start + HOT_ROWS, lanes]
            + summed[start + TERMS : start + TERMS + HOT_ROWS, lanes]
        )
        out_ref[share, VALUES : VALUES + 4, :] = piece[:4]
        out_ref[share, BLOCK + VALUES : BLOCK + VALUES + 3, :] = piece[4:]


def packed(jacobians, residuals, cameras, counts, targets):
    return pl.pallas_call(
        pack_body,
        out_shape=jax.ShapeDtypeStruct((targets, 2 * BLOCK, LANES), F32),
        in_specs=[SMEM, VMEM, VMEM, VMEM],
        out_specs=VMEM,
        scratch_shapes=[
            pltpu.VMEM((TERMS, LANES), F32),
            pltpu.VMEM((2 * TERMS * QUARTERS, 2 * LANES), BF16),
            pltpu.VMEM((SPAN, 2 * LANES), BF16),
        ],
        name="pack",
    )(counts, jacobians, residuals, cameras)


def hot_body(arrived_ref, out_ref):
    arrived = arrived_ref[...]
    out_ref[0:4, :] = arrived[:, VALUES : VALUES + 4, :].sum(axis=0)
    out_ref[4:7, :] = arrived[:, BLOCK + VALUES : BLOCK + VALUES + 3, :].sum(axis=0)


def hot_share(arrived):
    return pl.pallas_call(
        hot_body,
        out_shape=jax.ShapeDtypeStruct((HOT_ROWS, LANES), F32),
        in_specs=[VMEM],
        out_specs=VMEM,
        name="hot",
    )(arrived)


def sums_body(arrived_ref, out_ref, terms_ref, left_ref, right_ref, acc_ref):
    step = pl.program_id(0)

    @pl.when(step == 0)
    def _():
        acc_ref[...] = jnp.zeros_like(acc_ref)
        terms_ref[...] = jnp.zeros_like(terms_ref)

    value = [arrived_ref[pl.ds(row, 8, stride=BLOCK), :] for row in range(VALUES)]
    for turn in range(5):
        for k in range(CAMS):
            other = (k + turn) % CAMS
            term = value[k] * value[other] + value[CAMS + k] * value[CAMS + other]
            terms_ref[pl.ds(CAMS * turn + k, 8, stride=TERMS), :] = term
    for k in range(CAMS):
        term = value[k] * value[18] + value[CAMS + k] * value[19]
        terms_ref[pl.ds(PAIRS + k, 8, stride=TERMS), :] = term
    ids = value[20].astype(jnp.int32)
    for group in range(8):
        x = terms_ref[group * TERMS : (group + 1) * TERMS, :]
        row = ids[group : group + 1, :]
        set_operands(left_ref, right_ref, x, row, QUARTERS, group * LANES)
    acc_ref[...] += product(left_ref[...], right_ref[...])

    @pl.when(step == pl.num_programs(0) - 1)
    def _():
        for part in range(QUARTERS):
            at = 2 * TERMS * part
            out_ref[part] = acc_ref[at : at + TERMS, :] + acc_ref[at + TERMS : at + 2 * TERMS, :]


def camera_sums(arrived):
    rows = arrived.shape[0]
    depth = 8 * LANES
    return pl.pallas_call(
        sums_body,
        grid=(rows // (8 * BLOCK),),
        out_shape=jax.ShapeDtypeStruct((QUARTERS, TERMS, SPAN), F32),
        in_specs=[pl.BlockSpec((8 * BLOCK, LANES), lambda i: (i, 0))],
        out_specs=pl.BlockSpec((QUARTERS, TERMS, SPAN), lambda i: (0, 0, 0)),
        scratch_shapes=[
            pltpu.VMEM((8 * TERMS, LANES), F32),
            pltpu.VMEM((2 * TERMS * QUARTERS, depth), BF16),
            pltpu.VMEM((SPAN, depth), BF16),
            pltpu.VMEM((2 * TERMS * QUARTERS, SPAN), F32),
        ],
        cost_estimate=pl.CostEstimate(
            flops=2 * 2 * TERMS * CAM_DEV * 128 * rows // BLOCK, transcendentals=0, bytes_accessed=rows * 512
        ),
        name="sums",
    )(arrived)


def add_body(own_ref, summed_ref, hot_ref, out_ref):
    own = own_ref[0, 0]
    for part in range(QUARTERS):
        for share in range(2):
            for group in range(8):
                rows = slice(HOT_ROWS * group, HOT_ROWS * (group + 1))
                lanes = slice(share * LANES, (share + 1) * LANES)
                piece = jnp.where(own > 0, hot_ref[group * 8 + part * 2 + share], 0.0)
                out_ref[part, rows, lanes] = summed_ref[part, rows, lanes] + piece


def with_hot(summed, hot, own):
    return pl.pallas_call(
        add_body,
        out_shape=jax.ShapeDtypeStruct(summed.shape, F32),
        in_specs=[SMEM, VMEM, VMEM],
        out_specs=VMEM,
        name="add",
    )(own, summed, hot)


def place_body(first_ref, slots_ref, ids_ref, out_ref, left_ref, right_ref, acc_ref):
    sources = slots_ref.shape[0]
    ranges = out_ref.shape[0]
    first = first_ref[0, 0]
    acc_ref[...] = jnp.zeros_like(acc_ref)

    def add(step, carry):
        for inner in range(4):
            source = step * 4 + inner
            for half in range(2):
                x = slots_ref[source, half * CAMS : (half + 1) * CAMS, :]
                x = jnp.concatenate([x, jnp.zeros((16 - CAMS, LANES), F32)], axis=0)
                ids = ids_ref[source, half : half + 1, :] - first
                at = (inner * 2 + half) * LANES
                set_operands(left_ref, right_ref, x, ids, ranges, at)
        acc_ref[...] += product(left_ref[...], right_ref[...])
        return carry

    lax.fori_loop(0, sources // 4, add, 0)
    for part in range(ranges):
        at = 32 * part
        both = acc_ref[at : at + CAMS, :] + acc_ref[at + 16 : at + 16 + CAMS, :]
        out_ref[part, :CAMS, :] = both[:, :LANES]
        out_ref[part, CAMS:, :] = both[:, LANES:]


def placed(slots, ids, first, ranges):
    depth = 8 * LANES
    return pl.pallas_call(
        place_body,
        out_shape=jax.ShapeDtypeStruct((ranges, 2 * CAMS, LANES), F32),
        in_specs=[SMEM, VMEM, VMEM],
        out_specs=VMEM,
        scratch_shapes=[
            pltpu.VMEM((32 * ranges, depth), BF16),
            pltpu.VMEM((SPAN, depth), BF16),
            pltpu.VMEM((32 * ranges, SPAN), F32),
        ],
        name="place",
    )(first, slots, ids)


def blocks_body(shares_ref, out_ref):
    for k in range(CAMS):
        for l in range(CAMS):
            ahead, behind = (l - k) % CAMS, (k - l) % CAMS
            row = CAMS * ahead + k if ahead <= 4 else CAMS * behind + l
            for part in range(QUARTERS):
                lanes = slice(part * SPAN, (part + 1) * SPAN)
                at = k * CAMS + l
                out_ref[at : at + 1, lanes] = shares_ref[part, row : row + 1, :]


def whole_blocks(shares):
    return pl.pallas_call(
        blocks_body,
        out_shape=jax.ShapeDtypeStruct((CAMS * CAMS, CAM_DEV), F32),
        in_specs=[VMEM],
        out_specs=VMEM,
        name="blocks",
    )(shares)


def order_body(rows_ref, out_ref):
    groups = rows_ref.shape[0] // (16 * CAMS)
    for ends in range(groups):
        x, y, c = ends % 4, ends // 4 % 4, ends // 16
        for tile in range(16):
            source = (ends * 16 + tile) * CAMS
            at = (((y * 2 + c) * 4 + x) * 16 + tile) * LANES
            out_ref[:, at : at + LANES] = rows_ref[source : source + CAMS, :]


def ordered(rows):
    return pl.pallas_call(
        order_body,
        out_shape=jax.ShapeDtypeStruct((CAMS, rows.shape[0] // CAMS * LANES), F32),
        in_specs=[VMEM],
        out_specs=VMEM,
        name="order",
    )(rows)


def exchanged(pieces, axes):
    return lax.all_to_all(pieces, axes, 0, 0, tiled=True)


def from_all(share, axes):
    count = lax.axis_size(axes)
    return exchanged(jnp.broadcast_to(share[None], (count, *share.shape)), axes)


def local(jacobians, residuals, camera_local, bucket_counts, camera_map):
    targets = lax.axis_size(OBS)
    levels = lax.axis_size("z")
    cameras = camera_local.reshape(1, -1)
    sent = packed(jacobians, residuals, cameras, bucket_counts, targets)
    arrived = exchanged(sent, OBS)
    hot = from_all(hot_share(arrived), OBS)
    summed = camera_sums(arrived.reshape(targets * 2 * BLOCK, LANES))
    own = jnp.argmax(bucket_counts[0]) == lax.axis_index(OBS)
    summed = with_hot(summed, hot, own.astype(jnp.int32).reshape(1, 1))
    share = exchanged(summed, "x").sum(axis=0)
    blocks = whole_blocks(from_all(share[:48], "x"))
    slots = share[PAIRS : PAIRS + CAMS]
    slots = jnp.concatenate([slots[:, :LANES], slots[:, LANES:]], axis=0)
    slots = from_all(slots, PLANE)
    plane = slots.shape[0] * SPAN
    ids = lax.dynamic_slice_in_dim(camera_map, lax.axis_index("z") * plane, plane)
    first = lax.axis_index(PLANE) * levels * SPAN
    part = placed(slots, ids.reshape(-1, 2, LANES), first.reshape(1, 1), levels)
    part = exchanged(part, "z").sum(axis=0)
    part = from_all(part, "z")
    part = from_all(part.reshape(-1, LANES), ("y", "x"))
    part = from_all(part.reshape(-1, LANES), "c")
    gradient = ordered(part.reshape(-1, LANES))
    return gradient, blocks


def solution(mesh):
    split = Mesh(mesh.devices.reshape(8, 4, 2, mesh.shape["rep"]), ALL)
    return jax.shard_map(
        local,
        mesh=split,
        in_specs=(P(None, ALL), P(None, ALL), P(ALL), P(ALL, None), P()),
        out_specs=(P(), P(None, OBS)),
        check_vma=False,
    )
```

time: 555 us -> 195 us (0.35)
  local copies, waits for them, and re-layouts: 262 us -> 7.6 us
  waiting for transfers between devices: 118 us -> 34.3 us
  matrix products: 72.9 us -> 0 us
  blocking collectives: 42 us -> 92.9 us
  Pallas kernels: 0 us -> 33.1 us
  other arithmetic: 19.5 us -> 0.7 us
  between operations: 14.2 us -> 1.33 us
    scatter x1 -> x0, local copies, waits for them, and re-layouts: 173 us -> none  [local(): gradient = jnp.zeros(grad_slots.shape, jnp.float32).at[:, camera_map].set...]
    all_to_all x1 -> x4, blocking collectives: 10 us -> 92.9 us  [exchanged(): return lax.all_to_all(pieces, axes, 0, 0, tiled=True)]
    dot_general x16 -> x0, matrix products: 72.9 us -> none  [add_group(): lax.dot_general(terms, one_hot, (((1,), (1,)), ((), ())), precision=lax.P...]
    all_to_all x3 -> x5, waiting for transfers between devices: 79.4 us -> 34.3 us  [exchanged(): return lax.all_to_all(pieces, axes, 0, 0, tiled=True)]
    all_gather x2 -> x0, waiting for transfers between devices: 38.4 us -> none  [stacked_from(): pieces = lax.all_gather(pieces, axes[k], axis=0, tiled=True)]
    pallas_call x0 -> x7, Pallas kernels: none -> 33.1 us  [the longest x1 13.6 us: camera_sums(): pl.pallas_call(sums_body, grid=(rows // (8 * BLOCK),), out_shape=jax.Shap...]
    all_gather x2 -> x0, blocking collectives: 32 us -> none  [stacked_from(): pieces = lax.all_gather(pieces, axes[k], axis=0, tiled=True)]
    unnamed x16 -> x8, local copies, waits for them, and re-layouts: 28.7 us -> 1.46 us
  transfers between devices with their start and end apart: 5 -> 5, of which waited for: 5 -> 4; matrix products, arithmetic and copies ran while one was open for 2% -> 1% of each run, Pallas kernels for 0% -> 8%
where the time goes in v1:
time: 195 us; the launch traced here: 194 us
  blocking collectives  92.9 us (48%)
  waiting for transfers between devices  34.3 us (18%)
  Pallas kernels  33.1 us (17%)
  starting transfers between devices  24.1 us (12%)
  local copies, waits for them, and re-layouts  7.6 us (4%)
    all_to_all x4, blocking collectives, exchanged(): return lax.all_to_all(pieces, axes, 0, 0, tiled=True)  92.9 us
    all_to_all x5, waiting for transfers between devices, exchanged(): return lax.all_to_all(pieces, axes, 0, 0, tiled=True)  34.3 us
    all_to_all x5, starting transfers between devices, exchanged(): return lax.all_to_all(pieces, axes, 0, 0, tiled=True)  24.1 us
    pallas_call x1, Pallas kernels, camera_sums(): pl.pallas_call(sums_body, grid=(rows // (8 * BLOCK),), out_shape=jax.Shap...  13.6 us
    pallas_call x1, Pallas kernels, placed(): pl.pallas_call(place_body, out_shape=jax.ShapeDtypeStruct((ranges, 2 * CA...  5.47 us
    broadcast_in_dim x7, local copies, waits for them, and re-layouts, from_all(): return exchanged(jnp.broadcast_to(share[None], (count, *share.shape)), axes)  4.77 us
    pallas_call x1, Pallas kernels, packed(): pl.pallas_call(pack_body, out_shape=jax.ShapeDtypeStruct((targets, 2 * BL...  4.29 us
    pallas_call x1, Pallas kernels, ordered(): pl.pallas_call(order_body, out_shape=jax.ShapeDtypeStruct((CAMS, rows.sha...  3.95 us
  transfers between devices with their start and end apart: 5, of which 4 were waited for; matrix products, arithmetic and copies ran while one was open for 1% of the time, Pallas kernels for 8%

profile of v1, /device:TPU:1, one launch (start us, length us, event | category | flops | bytes accessed | tf_op | source)
XLA Modules:
  0.0 194.0 jit_solution(921435896092930880)
XLA Ops:
  0.6 4.3 %pack.1 = f32[64,56,128]{2,1,0:T(8,128)} custom-call(s32[1,64]{1,0:T(1,128)} %counts_ref.1, f32[18,32768]{1,0:T(8,128)} %jac_ref.1, f32[2,32768]{1,0:T(2,128)} %res_ref.1, s32[1,32768]{1,0:T(1,128)} %bitcast.12), custom_call_target="tpu_custom_call" | custom-call | tf_op jit(solution)/shard_map/pack/pallas_call | solution.py:107
  4.9 57.8 %all_to_all.45.arrived_ref = f32[64,56,128]{2,1,0:T(8,128)} all-to-all(f32[64,56,128]{2,1,0:T(8,128)} %pack.1), channel_id=1, replica_groups=mesh['z'=8,'y'=4,'c'=2,'x'=4] {'z','y','c'}, dimensions={0} | all-to-all | bytes 3670016 | tf_op jit(solution)/shard_map/all_to_all | solution.py:295
  62.7 2.2 %hot.1 = f32[7,128]{1,0:T(8,128)} custom-call(f32[64,56,128]{2,1,0:T(8,128)} %all_to_all.45.arrived_ref), custom_call_target="tpu_custom_call" | custom-call | tf_op jit(solution)/shard_map/hot/pallas_call | solution.py:128
  64.9 1.4 broadcast_in_dim.16
  66.3 6.6 %all-to-all-start.1 = ((f32[64,7,128]{2,1,0:T(8,128)}), f32[64,7,128]{2,1,0:T(8,128)S(1)}, u32[]{:S(2)}, u32[]{:S(2)}) async-start(f32[64,7,128]{2,1,0:T(8,128)} %broadcast_in_dim.16), calls=%async_computation.1 | async-start | bytes 524288 | tf_op jit(solution)/shard_map/all_to_all | solution.py:295
  73.0 0.7 bitcast_reduce_fusion
  74.2 13.6 %sums.1.summed_ref = f32[4,56,256]{2,1,0:T(8,128)} custom-call(f32[3584,128]{1,0:T(8,128)} %bitcast.10), custom_call_target="tpu_custom_call" | custom-call | flops 3758096384 | bytes 1835008 | tf_op jit(solution)/shard_map/sums/pallas_call | solution.py:171
  87.8 0.0 all-to-all-done.1.hot_ref
  87.8 0.7 copy-done.1
  88.5 1.8 add.21
  90.3 9.5 %all_to_all.46 = f32[4,56,256]{2,1,0:T(8,128)S(1)} all-to-all(f32[4,56,256]{2,1,0:T(8,128)} %add.21), channel_id=1, replica_groups=mesh['z'=8,'y'=4,'c'=2,'x'=4] {'x'}, dimensions={0} | all-to-all | bytes 458752 | tf_op jit(solution)/shard_map/all_to_all | solution.py:295
  99.9 0.8 broadcast_in_dim.17
  100.6 7.0 %all-to-all-start.3 = ((f32[32,18,128]{2,1,0:T(8,128)}), f32[32,18,128]{2,1,0:T(8,128)S(1)}, u32[]{:S(2)}, u32[]{:S(2)}) async-start(f32[32,18,128]{2,1,0:T(8,128)} %broadcast_in_dim.17), calls=%async_computation.3 | async-start | bytes 786432 | tf_op jit(solution)/shard_map/all_to_all | solution.py:295
  107.6 1.4 dynamic_slice.3
  109.0 8.8 %all-to-all-done.3.slots_ref = f32[32,18,128]{2,1,0:T(8,128)S(1)} async-done(((f32[32,18,128]{2,1,0:T(8,128)}), f32[32,18,128]{2,1,0:T(8,128)S(1)}, u32[]{:S(2)}, u32[]{:S(2)}) %all-to-all-start.3) | async-done | bytes 294944 | tf_op jit(solution)/shard_map/all_to_all | solution.py:295
  117.8 0.7 copy-done
  118.5 5.5 %place.1 = f32[8,18,128]{2,1,0:T(8,128)} custom-call(s32[1,1]{1,0:T(1,128)} %bitcast.first_ref, f32[32,18,128]{2,1,0:T(8,128)} %copy-done, s32[32,2,128]{2,1,0:T(2,128)} %bitcast.13), custom_call_target="tpu_custom_call" | custom-call | tf_op jit(solution)/shard_map/place/pallas_call | solution.py:239
  124.0 13.9 %all_to_all.47 = f32[8,18,128]{2,1,0:T(8,128)S(1)} all-to-all(f32[8,18,128]{2,1,0:T(8,128)} %place.1), channel_id=1, replica_groups=mesh['z'=8,'y'=4,'c'=2,'x'=4] {'z'}, dimensions={0} | all-to-all | bytes 147456 | tf_op jit(solution)/shard_map/all_to_all | solution.py:295
  138.0 0.6 broadcast_in_dim.18
  138.6 3.4 %all-to-all-start.5 = ((f32[8,18,128]{2,1,0:T(8,128)}), f32[8,18,128]{2,1,0:T(8,128)S(1)}, u32[]{:S(2)}, u32[]{:S(2)}) async-start(f32[8,18,128]{2,1,0:T(8,128)} %broadcast_in_dim.18), calls=%async_computation.5 | async-start | bytes 196608 | tf_op jit(solution)/shard_map/all_to_all | solution.py:295
  142.0 7.6 %all-to-all-done.5 = f32[8,18,128]{2,1,0:T(8,128)S(1)} async-done(((f32[8,18,128]{2,1,0:T(8,128)}), f32[8,18,128]{2,1,0:T(8,128)S(1)}, u32[]{:S(2)}, u32[]{:S(2)}) %all-to-all-start.5) | async-done | bytes 73760 | tf_op jit(solution)/shard_map/all_to_all | solution.py:295
  149.6 0.7 broadcast_in_dim.45
  150.3 3.4 %all-to-all-start.8 = ((f32[4,48,256]{2,1,0:T(8,128)}), f32[4,48,256]{2,1,0:T(8,128)S(1)}, u32[]{:S(2)}, u32[]{:S(2)}) async-start(f32[4,48,256]{2,1,0:T(8,128)} %broadcast_in_dim.45), calls=%async_computation.8 | async-start | bytes 393216 | tf_op jit(solution)/shard_map/all_to_all | solution.py:295
  153.6 5.1 %all-to-all-done.8.shares_ref = f32[4,48,256]{2,1,0:T(8,128)S(1)} async-done(((f32[4,48,256]{2,1,0:T(8,128)}), f32[4,48,256]{2,1,0:T(8,128)S(1)}, u32[]{:S(2)}, u32[]{:S(2)}) %all-to-all-start.8) | async-done | bytes 196640 | tf_op jit(solution)/shard_map/all_to_all | solution.py:295
  158.8 1.1 broadcast_in_dim.20
  159.9 3.7 %all-to-all-start.6 = ((f32[16,144,128]{2,1,0:T(8,128)}), f32[16,144,128]{2,1,0:T(8,128)S(1)}, u32[]{:S(2)}, u32[]{:S(2)}) async-start(f32[16,144,128]{2,1,0:T(8,128)} %broadcast_in_dim.20), calls=%async_computation.6 | async-start | bytes 2359296 | tf_op jit(solution)/shard_map/all_to_all | solution.py:295
  163.6 0.0 copy-done.2
  163.6 1.8 blocks.1
  165.4 12.8 %all-to-all-done.6 = f32[16,144,128]{2,1,0:T(8,128)S(1)} async-done(((f32[16,144,128]{2,1,0:T(8,128)}), f32[16,144,128]{2,1,0:T(8,128)S(1)}, u32[]{:S(2)}, u32[]{:S(2)}) %all-to-all-start.6) | async-done | bytes 1179680 | tf_op jit(solution)/shard_map/all_to_all | solution.py:295
  178.2 0.2 broadcast_in_dim.44
  178.3 11.7 %all_to_all.48 = f32[2,2304,128]{2,1,0:T(8,128)} all-to-all(f32[2,2304,128]{2,1,0:T(8,128)S(1)} %broadcast_in_dim.44), channel_id=1, replica_groups=mesh['z'=8,'y'=4,'c'=2,'x'=4] {'c'}, dimensions={0} | all-to-all | bytes 4718592 | tf_op jit(solution)/shard_map/all_to_all | solution.py:295
  190.1 3.9 %order.1 = f32[9,65536]{1,0:T(8,128)} custom-call(f32[4608,128]{1,0:T(8,128)} %bitcast.9), custom_call_target="tpu_custom_call" | custom-call | tf_op jit(solution)/shard_map/order/pallas_call | solution.py:285
  (11 shorter events, 0.1 us)
Async XLA Ops:
  4.9 68.0 %copy-start.3 = (s32[1,64]{1,0:T(1,128)S(1)}, s32[1,64]{1,0:T(1,128)}, u32[]{:S(2)}) copy-start(s32[1,64]{1,0:T(1,128)} %counts_ref.1) | copy-start | bytes 772
  66.3 21.5 %all-to-all-start.1 = ((f32[64,7,128]{2,1,0:T(8,128)}), f32[64,7,128]{2,1,0:T(8,128)S(1)}, u32[]{:S(2)}, u32[]{:S(2)}) async-start(f32[64,7,128]{2,1,0:T(8,128)} %broadcast_in_dim.16), calls=%async_computation.1 | async-start | bytes 524288 | tf_op jit(solution)/shard_map/all_to_all | solution.py:295
  87.8 0.7 copy-start.1
  100.6 17.1 %all-to-all-start.3 = ((f32[32,18,128]{2,1,0:T(8,128)}), f32[32,18,128]{2,1,0:T(8,128)S(1)}, u32[]{:S(2)}, u32[]{:S(2)}) async-start(f32[32,18,128]{2,1,0:T(8,128)} %broadcast_in_dim.17), calls=%async_computation.3 | async-start | bytes 786432 | tf_op jit(solution)/shard_map/all_to_all | solution.py:295
  117.8 0.7 copy-start
  138.6 11.0 %all-to-all-start.5 = ((f32[8,18,128]{2,1,0:T(8,128)}), f32[8,18,128]{2,1,0:T(8,128)S(1)}, u32[]{:S(2)}, u32[]{:S(2)}) async-start(f32[8,18,128]{2,1,0:T(8,128)} %broadcast_in_dim.18), calls=%async_computation.5 | async-start | bytes 196608 | tf_op jit(solution)/shard_map/all_to_all | solution.py:295
  150.3 8.5 %all-to-all-start.8 = ((f32[4,48,256]{2,1,0:T(8,128)}), f32[4,48,256]{2,1,0:T(8,128)S(1)}, u32[]{:S(2)}, u32[]{:S(2)}) async-start(f32[4,48,256]{2,1,0:T(8,128)} %broadcast_in_dim.45), calls=%async_computation.8 | async-start | bytes 393216 | tf_op jit(solution)/shard_map/all_to_all | solution.py:295
  158.8 4.8 %copy-start.2 = (f32[4,48,256]{2,1,0:T(8,128)}, f32[4,48,256]{2,1,0:T(8,128)S(1)}, u32[]{:S(2)}) copy-start(f32[4,48,256]{2,1,0:T(8,128)S(1)} %all-to-all-done.8.shares_ref) | copy-start | bytes 589828
  159.9 18.3 %all-to-all-start.6 = ((f32[16,144,128]{2,1,0:T(8,128)}), f32[16,144,128]{2,1,0:T(8,128)S(1)}, u32[]{:S(2)}, u32[]{:S(2)}) async-start(f32[16,144,128]{2,1,0:T(8,128)} %broadcast_in_dim.20), calls=%async_computation.6 | async-start | bytes 2359296 | tf_op jit(solution)/shard_map/all_to_all | solution.py:295

commit v2 on v1

v2 whole, which is shorter than its diff:
```python
import jax
import jax.numpy as jnp
from jax import lax
from jax.experimental import pallas as pl
from jax.experimental.pallas import tpu as pltpu
from jax.sharding import Mesh
from jax.sharding import PartitionSpec as P

CAM_DEV = 1024
HALF = 256
LANES = 128
SPAN = 256
QUARTERS = CAM_DEV // SPAN
CAMS = 9
PAIRS = 45
TERMS = 56
VALUES = 21
BLOCK = 26
HOT_ROWS = 14
SHARE_ROWS = 128
OBS = ("z", "y", "c")
PLANE = ("y", "c", "x")
ALL = ("z", "y", "c", "x")
F32 = jnp.float32
BF16 = jnp.bfloat16
VMEM = pl.BlockSpec(memory_space=pltpu.VMEM)
SMEM = pl.BlockSpec(memory_space=pltpu.SMEM)


def two_pieces(x):
    upper = x.astype(BF16).astype(F32)
    return jnp.concatenate([upper, x - upper], axis=0).astype(BF16)


def kept_where(x, row, value):
    rows, lanes = x.shape
    kept = jnp.broadcast_to(row, (16, lanes)) == value
    kept = jnp.where(kept, 1.0, 0.0).astype(BF16)
    return (x.reshape(rows // 16, 16, lanes) * kept[None]).reshape(rows, lanes)


def one_hot(row):
    lanes = row.shape[1]
    spread = lax.broadcasted_iota(jnp.int32, (SPAN, lanes), 0) == row
    return jnp.where(spread, 1.0, 0.0).astype(BF16)


def product(left, right):
    return lax.dot_general(left, right, (((1,), (1,)), ((), ())), preferred_element_type=F32)


def set_operands(left_ref, right_ref, x, ids, parts, at):
    pieces = two_pieces(x)
    rows = pieces.shape[0]
    upper, lower = jnp.right_shift(ids, 8), jnp.bitwise_and(ids, SPAN - 1)
    for part in range(parts):
        left_ref[part * rows : (part + 1) * rows, at : at + LANES] = kept_where(pieces, upper, part)
    right_ref[:, at : at + LANES] = one_hot(lower)


def hot_piece(block):
    return slice(4 * block, min(4 * block + 4, HOT_ROWS))


def pack_body(counts_ref, jac_ref, res_ref, cam_ref, out_ref, terms_ref, left_ref, right_ref):
    targets = out_ref.shape[0]
    capacity = jac_ref.shape[1] // (2 * targets)

    def send(target, hot):
        for side in range(2):
            bucket = (2 * lax.rem(target, 4) + side) * 8 + lax.div(target, 4)
            count = counts_ref[0, bucket]
            for half in range(2):
                at = pl.multiple_of(bucket * capacity + half * LANES, LANES)
                here = pl.ds(at, LANES)
                live = lax.broadcasted_iota(jnp.int32, (1, LANES), 1) + half * LANES < count
                row = (2 * side + half) * BLOCK
                out_ref[target, row : row + 18, :] = jnp.where(live, jac_ref[:, here], 0.0)
                out_ref[target, row + 18 : row + 20, :] = jnp.where(live, res_ref[:, here], 0.0)
                out_ref[target, row + 20 : row + 21, :] = cam_ref[:, here].astype(F32)
            hot = jnp.where(count > HALF, bucket, hot)
        return hot

    hot = lax.fori_loop(0, targets, send, 0)
    for half in range(2):
        at = pl.multiple_of(hot * capacity + HALF + half * LANES, LANES)
        here = pl.ds(at, LANES)
        count = counts_ref[0, hot]
        live = lax.broadcasted_iota(jnp.int32, (1, LANES), 1) + HALF + half * LANES < count
        jac = jnp.where(live, jac_ref[:, here], 0.0)
        res = jnp.where(live, res_ref[:, here], 0.0)
        ids = cam_ref[:, here]
        first, second = jac[:CAMS], jac[CAMS:]
        for turn in range(5):
            around = first if turn == 0 else jnp.concatenate([first[turn:], first[:turn]], axis=0)
            beside = second if turn == 0 else jnp.concatenate([second[turn:], second[:turn]], axis=0)
            terms_ref[CAMS * turn : CAMS * (turn + 1), :] = first * around + second * beside
        terms_ref[PAIRS : PAIRS + CAMS, :] = first * res[0:1] + second * res[1:2]
        terms_ref[PAIRS + CAMS : TERMS, :] = jnp.zeros((TERMS - PAIRS - CAMS, LANES), F32)
        set_operands(left_ref, right_ref, terms_ref[...], ids, QUARTERS, half * LANES)
    summed = product(left_ref[...], right_ref[...])
    for share in range(targets):
        rows, column = HOT_ROWS * (share // 8), LANES * (share % 8)
        start = 2 * TERMS * (column // SPAN) + rows
        lanes = slice(column % SPAN, column % SPAN + LANES)
        piece = (
            summed[start : start + HOT_ROWS, lanes]
            + summed[start + TERMS : start + TERMS + HOT_ROWS, lanes]
        )
        for block in range(4):
            part = piece[hot_piece(block)]
            row = block * BLOCK + VALUES
            out_ref[share, row : row + part.shape[0], :] = part


def packed(jacobians, residuals, cameras, counts, targets):
    return pl.pallas_call(
        pack_body,
        out_shape=jax.ShapeDtypeStruct((targets, 4 * BLOCK, LANES), F32),
        in_specs=[SMEM, VMEM, VMEM, VMEM],
        out_specs=VMEM,
        scratch_shapes=[
            pltpu.VMEM((TERMS, LANES), F32),
            pltpu.VMEM((2 * TERMS * QUARTERS, 2 * LANES), BF16),
            pltpu.VMEM((SPAN, 2 * LANES), BF16),
        ],
        name="pack",
    )(counts, jacobians, residuals, cameras)


def sums_body(arrived_ref, out_ref, terms_ref, left_ref, right_ref, acc_ref, hot_ref):
    step = pl.program_id(0)

    @pl.when(step == 0)
    def _():
        acc_ref[...] = jnp.zeros_like(acc_ref)
        terms_ref[...] = jnp.zeros_like(terms_ref)
        hot_ref[...] = jnp.zeros_like(hot_ref)

    for pair in range(2):
        start = pair * 8 * BLOCK
        value = [arrived_ref[pl.ds(start + row, 8, stride=BLOCK), :] for row in range(VALUES)]
        for turn in range(5):
            for k in range(CAMS):
                other = (k + turn) % CAMS
                term = value[k] * value[other] + value[CAMS + k] * value[CAMS + other]
                terms_ref[pair, pl.ds(CAMS * turn + k, 8, stride=TERMS), :] = term
        for k in range(CAMS):
            term = value[k] * value[18] + value[CAMS + k] * value[19]
            terms_ref[pair, pl.ds(PAIRS + k, 8, stride=TERMS), :] = term
        ids = value[20].astype(jnp.int32)
        for group in range(8):
            x = terms_ref[pair, group * TERMS : (group + 1) * TERMS, :]
            side, half = group % 4 // 2, group % 2
            at = ((pair * 2 + group // 4) * 2 + half) * LANES
            row = ids[group : group + 1, :]
            set_operands(left_ref.at[side], right_ref.at[side], x, row, QUARTERS, at)
    for source in range(4):
        for block in range(4):
            part = hot_piece(block)
            row = (source * 4 + block) * BLOCK + VALUES
            hot_ref[part, :] += arrived_ref[row : row + part.stop - part.start, :]
    for side in range(2):
        acc_ref[side] += product(left_ref[side], right_ref[side])

    @pl.when(step == pl.num_programs(0) - 1)
    def _():
        for side in range(2):
            for part in range(QUARTERS):
                at = 2 * TERMS * part
                both = acc_ref[side, at : at + TERMS, :] + acc_ref[side, at + TERMS : at + 2 * TERMS, :]
                level = side * QUARTERS + part
                out_ref[level, :TERMS, :] = both[:, :LANES]
                out_ref[level, TERMS : 2 * TERMS, :] = both[:, LANES:]
                out_ref[level, 2 * TERMS :, :] = hot_ref[...]


def camera_sums(arrived):
    rows = arrived.shape[0]
    depth = 8 * LANES
    out = (2 * QUARTERS, SHARE_ROWS, LANES)
    return pl.pallas_call(
        sums_body,
        grid=(rows // (16 * BLOCK),),
        out_shape=jax.ShapeDtypeStruct(out, F32),
        in_specs=[pl.BlockSpec((16 * BLOCK, LANES), lambda i: (i, 0))],
        out_specs=pl.BlockSpec(out, lambda i: (0, 0, 0)),
        scratch_shapes=[
            pltpu.VMEM((2, 8 * TERMS, LANES), F32),
            pltpu.VMEM((2, 2 * TERMS * QUARTERS, depth), BF16),
            pltpu.VMEM((2, SPAN, depth), BF16),
            pltpu.VMEM((2, 2 * TERMS * QUARTERS, SPAN), F32),
            pltpu.VMEM((SHARE_ROWS - 2 * TERMS, LANES), F32),
        ],
        cost_estimate=pl.CostEstimate(
            flops=2 * 2 * TERMS * CAM_DEV * 128 * rows // BLOCK, transcendentals=0, bytes_accessed=rows * 512
        ),
        name="sums",
    )(arrived)


def place_body(first_ref, slots_ref, ids_ref, out_ref, left_ref, right_ref, acc_ref):
    sources = slots_ref.shape[0]
    ranges = out_ref.shape[0]
    first = first_ref[0, 0]
    acc_ref[...] = jnp.zeros_like(acc_ref)

    def set_group(x, ids, group):
        x = jnp.concatenate([x, jnp.zeros((16 - CAMS, LANES), F32)], axis=0)
        set_operands(left_ref, right_ref, x, ids - first, ranges, group * LANES)

    def add(step, carry):
        for group in range(8):
            source, half = step * 4 + group // 2, group % 2
            x = slots_ref[source, half * CAMS : (half + 1) * CAMS, :]
            set_group(x, ids_ref[source, half : half + 1, :], group)
        acc_ref[...] += product(left_ref[...], right_ref[...])
        return carry

    lax.fori_loop(0, sources // 4, add, 0)
    row = 2 * CAMS + PAIRS % HOT_ROWS
    for group in range(8):
        x = slots_ref[PAIRS // HOT_ROWS * 8 + group, row : row + CAMS, :]
        set_group(x, ids_ref[sources + group // 2, group % 2 : group % 2 + 1, :], group)
    acc_ref[...] += product(left_ref[...], right_ref[...])
    for part in range(ranges):
        at = 32 * part
        both = acc_ref[at : at + CAMS, :] + acc_ref[at + 16 : at + 16 + CAMS, :]
        out_ref[part, :CAMS, :] = both[:, :LANES]
        out_ref[part, CAMS:, :] = both[:, LANES:]


def placed(slots, ids, first, ranges):
    depth = 8 * LANES
    return pl.pallas_call(
        place_body,
        out_shape=jax.ShapeDtypeStruct((ranges, 2 * CAMS, LANES), F32),
        in_specs=[SMEM, VMEM, VMEM],
        out_specs=VMEM,
        scratch_shapes=[
            pltpu.VMEM((32 * ranges, depth), BF16),
            pltpu.VMEM((SPAN, depth), BF16),
            pltpu.VMEM((32 * ranges, SPAN), F32),
        ],
        name="place",
    )(first, slots, ids)


def blocks_body(place_ref, one_ref, two_ref, three_ref, four_ref, slots_ref, out_ref, rows_ref):
    column, own = place_ref[0, 0], place_ref[0, 1]
    for turn, share_ref in enumerate((one_ref, two_ref, three_ref, four_ref)):
        part = lax.rem(column - turn + QUARTERS, QUARTERS)
        for half in range(2):
            for group in range(4):
                at = HOT_ROWS * group
                hot = slots_ref[group * 8 + part * 2 + half, 2 * CAMS : 2 * CAMS + HOT_ROWS, :]
                share = share_ref[half * TERMS + at : half * TERMS + at + HOT_ROWS, :]
                rows_ref[at : at + HOT_ROWS, :] = share + jnp.where(own > 0, hot, 0.0)
            lanes = pl.ds(pl.multiple_of((part * 2 + half) * LANES, LANES), LANES)
            for k in range(CAMS):
                for l in range(CAMS):
                    ahead, behind = (l - k) % CAMS, (k - l) % CAMS
                    row = CAMS * ahead + k if ahead <= 4 else CAMS * behind + l
                    at = k * CAMS + l
                    out_ref[at : at + 1, lanes] = rows_ref[row : row + 1, :]


def whole_blocks(place, shares, slots):
    return pl.pallas_call(
        blocks_body,
        out_shape=jax.ShapeDtypeStruct((CAMS * CAMS, CAM_DEV), F32),
        in_specs=[SMEM] + [VMEM] * 5,
        out_specs=VMEM,
        scratch_shapes=[pltpu.VMEM((TERMS, LANES), F32)],
        name="blocks",
    )(place, *shares, slots)


def order_body(core_ref, own_ref, other_ref, out_ref):
    for turn, rows_ref in enumerate((own_ref, other_ref)):
        core = jnp.bitwise_xor(core_ref[0, 0], turn)
        for ends in range(rows_ref.shape[0] // (16 * CAMS)):
            x, y = ends % 4, ends // 4
            for tile in range(16):
                source = (ends * 16 + tile) * CAMS
                at = pl.multiple_of((((y * 2 + core) * 4 + x) * 16 + tile) * LANES, LANES)
                out_ref[:, pl.ds(at, LANES)] = rows_ref[source : source + CAMS, :]


def ordered(core, own, other):
    return pl.pallas_call(
        order_body,
        out_shape=jax.ShapeDtypeStruct((CAMS, 2 * own.shape[0] // CAMS * LANES), F32),
        in_specs=[SMEM, VMEM, VMEM],
        out_specs=VMEM,
        name="order",
    )(core, own, other)


def exchanged(pieces, axes):
    return lax.all_to_all(pieces, axes, 0, 0, tiled=True)


def from_all(share, axes):
    count = lax.axis_size(axes)
    return exchanged(jnp.broadcast_to(share[None], (count, *share.shape)), axes)


def to_owner(share, turn):
    pairs = []
    for level in range(8):
        for column in range(4):
            target = (2 * column + level // 4) * 4 + (level % 4 + turn) % 4
            pairs.append((level * 4 + column, target))
    return lax.ppermute(share, ("z", "x"), pairs)


def local(jacobians, residuals, camera_local, bucket_counts, camera_map):
    targets = lax.axis_size(PLANE)
    levels = lax.axis_size("z")
    level, core = lax.axis_index("z"), lax.axis_index("c")
    hot = jnp.argmax(bucket_counts[0])
    ids = camera_map.reshape(4, 2, 4, 2, QUARTERS, SPAN)
    ids = lax.dynamic_slice(ids, (0, level // 4, 0, 0, level % 4, 0), (4, 1, 4, 2, 1, SPAN))
    ids = ids.reshape(4, 4, 2, SPAN).transpose(1, 2, 0, 3).reshape(targets, 2, LANES)
    hot_ids = lax.dynamic_slice_in_dim(camera_map, hot * CAM_DEV, CAM_DEV)
    hot_ids = jnp.where(level == 0, hot_ids, -1).reshape(-1, 2, LANES)
    ids = jnp.concatenate([ids, hot_ids], axis=0)

    cameras = camera_local.reshape(1, -1)
    sent = packed(jacobians, residuals, cameras, bucket_counts, targets)
    arrived = exchanged(sent, PLANE)
    summed = camera_sums(arrived.reshape(-1, LANES))
    share = exchanged(summed, "z").sum(axis=0)
    shares = [to_owner(share[: 2 * TERMS], turn) for turn in range(4)]
    slots = [share[PAIRS : PAIRS + CAMS], share[TERMS + PAIRS : TERMS + PAIRS + CAMS]]
    slots.append(share[2 * TERMS : 2 * TERMS + HOT_ROWS])
    slots = from_all(jnp.concatenate(slots, axis=0), PLANE)
    own = (hot == lax.axis_index(OBS)).astype(jnp.int32)
    blocks = whole_blocks(jnp.stack([lax.axis_index("x"), own]).reshape(1, 2), shares, slots)
    first = lax.axis_index(PLANE) * levels * SPAN
    part = placed(slots, ids, first.reshape(1, 1), levels)
    part = exchanged(part, "z").sum(axis=0)
    part = from_all(part, "z")
    part = from_all(part.reshape(-1, LANES), ("y", "x")).reshape(-1, LANES)
    other = lax.ppermute(part, "c", [(0, 1), (1, 0)])
    gradient = ordered(core.reshape(1, 1), part, other)
    return gradient, blocks


def solution(mesh):
    split = Mesh(mesh.devices.reshape(8, 4, 2, mesh.shape["rep"]), ALL)
    return jax.shard_map(
        local,
        mesh=split,
        in_specs=(P(None, ALL), P(None, ALL), P(ALL), P(ALL, None), P()),
        out_specs=(P(), P(None, OBS)),
        check_vma=False,
    )
```

time: 195 us -> 175 us (0.90)
  blocking collectives: 92.9 us -> 72.6 us
  waiting for transfers between devices: 34.3 us -> 41.7 us
  Pallas kernels: 33.1 us -> 27.4 us
  local copies, waits for them, and re-layouts: 7.6 us -> 4.3 us
    all_to_all x4, blocking collectives: 92.9 us -> 72.6 us  [exchanged(): return lax.all_to_all(pieces, axes, 0, 0, tiled=True)]
    ppermute x0 -> x5, waiting for transfers between devices: none -> 14.4 us  [the longest x4 14.4 us: to_owner(): return lax.ppermute(share, ('z', 'x'), pairs)]
    all_to_all x5 -> x2, starting transfers between devices: 24.1 us -> 12.4 us  [exchanged(): return lax.all_to_all(pieces, axes, 0, 0, tiled=True)]
    ppermute x0 -> x5, starting transfers between devices: none -> 10.9 us  [the longest x4 7.22 us: to_owner(): return lax.ppermute(share, ('z', 'x'), pairs)]
    all_to_all x5 -> x2, waiting for transfers between devices: 34.3 us -> 27.3 us  [exchanged(): return lax.all_to_all(pieces, axes, 0, 0, tiled=True)]
    pallas_call x5 -> x3, Pallas kernels: 25.9 us -> 19.2 us  [the longest x1 10.8 us: camera_sums(): pl.pallas_call(sums_body, grid=(rows // (16 * BLOCK),), out_shape=jax.Sha...]
    broadcast_in_dim x7 -> x4, local copies, waits for them, and re-layouts: 4.77 us -> 0.95 us  [from_all(): return exchanged(jnp.broadcast_to(share[None], (count, *share.shape)), axes)]
  transfers between devices with their start and end apart: 5 -> 7, of which waited for: 4 -> 3; matrix products, arithmetic and copies ran while one was open for 1% -> 1% of each run, Pallas kernels for 8% -> 1%
where the time goes in v2:
time: 175 us; the launch traced here: 173 us
  blocking collectives  72.6 us (41%)
  waiting for transfers between devices  41.7 us (24%)
  Pallas kernels  27.4 us (16%)
  starting transfers between devices  23.3 us (13%)
  local copies, waits for them, and re-layouts  4.3 us (2%)
  between operations  1.99 us (1%)
  other arithmetic  1.97 us (1%)
    all_to_all x4, blocking collectives, exchanged(): return lax.all_to_all(pieces, axes, 0, 0, tiled=True)  72.6 us
    all_to_all x2, waiting for transfers between devices, exchanged(): return lax.all_to_all(pieces, axes, 0, 0, tiled=True)  27.3 us
    ppermute x4, waiting for transfers between devices, to_owner(): return lax.ppermute(share, ('z', 'x'), pairs)  14.4 us
    all_to_all x2, starting transfers between devices, exchanged(): return lax.all_to_all(pieces, axes, 0, 0, tiled=True)  12.4 us
    pallas_call x1, Pallas kernels, camera_sums(): pl.pallas_call(sums_body, grid=(rows // (16 * BLOCK),), out_shape=jax.Sha...  10.8 us
    ppermute x4, starting transfers between devices, to_owner(): return lax.ppermute(share, ('z', 'x'), pairs)  7.22 us
    pallas_call x1, Pallas kernels, placed(): pl.pallas_call(place_body, out_shape=jax.ShapeDtypeStruct((ranges, 2 * CA...  5.96 us
    pallas_call x1, Pallas kernels, ordered(): pl.pallas_call(order_body, out_shape=jax.ShapeDtypeStruct((CAMS, 2 * own....  4.34 us
  transfers between devices with their start and end apart: 7, of which 3 were waited for; matrix products, arithmetic and copies ran while one was open for 1% of the time, Pallas kernels for 1%

profile of v2, /device:TPU:1, one launch (start us, length us, event | category | flops | bytes accessed | tf_op | source)
XLA Modules:
  0.0 173.3 jit_solution(2998145550000964578)
XLA Ops:
  0.6 4.1 %pack.1 = f32[32,104,128]{2,1,0:T(8,128)} custom-call(s32[1,64]{1,0:T(1,128)} %counts_ref.1, f32[18,32768]{1,0:T(8,128)} %jac_ref.1, f32[2,32768]{1,0:T(2,128)} %res_ref.1, s32[1,32768]{1,0:T(1,128)} %bitcast.20), custom_call_target="tpu_custom_call" | custom-call | tf_op jit(solution)/shard_map/pack/pallas_call | solution.py:117
  4.7 32.5 %all_to_all.30 = f32[32,104,128]{2,1,0:T(8,128)} all-to-all(f32[32,104,128]{2,1,0:T(8,128)} %pack.1), channel_id=1, replica_groups=mesh['z'=8,'y'=4,'c'=2,'x'=4] {'y','c','x'}, dimensions={0} | all-to-all | bytes 3407872 | tf_op jit(solution)/shard_map/all_to_all | solution.py:301
  37.2 10.8 %sums.1 = f32[8,128,128]{2,1,0:T(8,128)} custom-call(f32[3328,128]{1,0:T(8,128)} %bitcast.19), custom_call_target="tpu_custom_call" | custom-call | flops 3758096384 | bytes 1703936 | tf_op jit(solution)/shard_map/sums/pallas_call | solution.py:182
  48.0 8.3 %all-to-all-start.1 = ((f32[8,128,128]{2,1,0:T(8,128)}), f32[8,128,128]{2,1,0:T(8,128)S(1)}, u32[]{:S(2)}, u32[]{:S(2)}) async-start(f32[8,128,128]{2,1,0:T(8,128)} %sums.1), calls=%async_computation.1 | async-start | bytes 1048576 | tf_op jit(solution)/shard_map/all_to_all | solution.py:301
  56.4 18.0 %all-to-all-done.1 = f32[8,128,128]{2,1,0:T(8,128)S(1)} async-done(((f32[8,128,128]{2,1,0:T(8,128)}), f32[8,128,128]{2,1,0:T(8,128)S(1)}, u32[]{:S(2)}, u32[]{:S(2)}) %all-to-all-start.1) | async-done | bytes 524320 | tf_op jit(solution)/shard_map/all_to_all | solution.py:301
  74.4 0.9 broadcast_in_dim.12
  75.2 4.1 %all-to-all-start.2 = ((f32[32,32,128]{2,1,0:T(8,128)}), f32[32,32,128]{2,1,0:T(8,128)S(1)}, u32[]{:S(2)}, u32[]{:S(2)}) async-start(f32[32,32,128]{2,1,0:T(8,128)} %broadcast_in_dim.12), calls=%async_computation.2 | async-start | bytes 1048576 | tf_op jit(solution)/shard_map/all_to_all | solution.py:301
  79.3 0.6 bitcast_reduce_fusion
  80.6 0.1 reshape.41
  80.9 0.6 pad_add_fusion.ids_ref
  81.5 9.4 %all-to-all-done.2.slots_ref = f32[32,32,128]{2,1,0:T(8,128)S(1)} async-done(((f32[32,32,128]{2,1,0:T(8,128)}), f32[32,32,128]{2,1,0:T(8,128)S(1)}, u32[]{:S(2)}, u32[]{:S(2)}) %all-to-all-start.2) | async-done | bytes 524320 | tf_op jit(solution)/shard_map/all_to_all | solution.py:301
  90.8 0.8 copy-done
  91.6 6.0 %place.1 = f32[8,18,128]{2,1,0:T(8,128)} custom-call(s32[1,1]{1,0:T(1,128)} %bitcast.1.first_ref, f32[32,32,128]{2,1,0:T(8,128)} %copy-done, s32[36,2,128]{2,1,0:T(2,128)} %pad_add_fusion.ids_ref), custom_call_target="tpu_custom_call" | custom-call | tf_op jit(solution)/shard_map/place/pallas_call | solution.py:235
  97.6 10.7 %all_to_all.31 = f32[8,18,128]{2,1,0:T(8,128)S(1)} all-to-all(f32[8,18,128]{2,1,0:T(8,128)} %place.1), channel_id=1, replica_groups=mesh['z'=8,'y'=4,'c'=2,'x'=4] {'z'}, dimensions={0} | all-to-all | bytes 147456 | tf_op jit(solution)/shard_map/all_to_all | solution.py:301
  108.4 10.1 %all_to_all.32 = f32[8,18,128]{2,1,0:T(8,128)S(1)} all-to-all(f32[8,18,128]{2,1,0:T(8,128)S(1)} %broadcast_in_dim.25), channel_id=1, replica_groups=mesh['z'=8,'y'=4,'c'=2,'x'=4] {'z'}, dimensions={0} | all-to-all | bytes 147456 | tf_op jit(solution)/shard_map/all_to_all | solution.py:301
  118.4 0.1 broadcast_in_dim.27
  118.5 19.3 %all_to_all.33 = f32[16,144,128]{2,1,0:T(8,128)S(1)} all-to-all(f32[16,144,128]{2,1,0:T(8,128)S(1)} %broadcast_in_dim.27), channel_id=1, replica_groups=mesh['z'=8,'y'=4,'c'=2,'x'=4] {'y','x'}, dimensions={0} | all-to-all | bytes 2359296 | tf_op jit(solution)/shard_map/all_to_all | solution.py:301
  137.8 3.7 %collective-permute-start = (f32[2304,128]{1,0:T(8,128)S(1)}, f32[2304,128]{1,0:T(8,128)S(1)}, u32[]{:S(2)}, u32[]{:S(2)}) collective-permute-start(f32[2304,128]{1,0:T(8,128)S(1)} %bitcast.17), channel_id=1, source_target_pairs={{0,4},{4,0},{1,5},{5,1},{2,6},{6,2},{3,7},{7,3},{8,12},{12,8},{9,1... | collective-permute-start | bytes 3538952 | tf_op jit(solution)/shard_map/ppermute | solution.py:346
  142.1 2.6 %collective-permute-start.4 = (f32[112,128]{1,0:T(8,128)S(1)}, f32[112,128]{1,0:T(8,128)S(1)}, u32[]{:S(2)}, u32[]{:S(2)}) collective-permute-start(f32[112,128]{1,0:T(8,128)S(1)} %slice.22), channel_id=1, source_target_pairs={{0,3},{1,67},{2,131},{3,195},{32,0},{33,64},{34,128},{35,192},{64,... | collective-permute-start | bytes 172040 | tf_op jit(solution)/shard_map/ppermute | solution.py:315
  144.7 2.1 %collective-permute-start.3 = (f32[112,128]{1,0:T(8,128)S(1)}, f32[112,128]{1,0:T(8,128)S(1)}, u32[]{:S(2)}, u32[]{:S(2)}) collective-permute-start(f32[112,128]{1,0:T(8,128)S(1)} %slice.22), channel_id=1, source_target_pairs={{0,2},{1,66},{2,130},{3,194},{32,3},{33,67},{34,131},{35,195},{64,... | collective-permute-start | bytes 172040 | tf_op jit(solution)/shard_map/ppermute | solution.py:315
  146.8 1.9 %collective-permute-start.2 = (f32[112,128]{1,0:T(8,128)S(1)}, f32[112,128]{1,0:T(8,128)S(1)}, u32[]{:S(2)}, u32[]{:S(2)}) collective-permute-start(f32[112,128]{1,0:T(8,128)S(1)} %slice.22), channel_id=1, source_target_pairs={{0,1},{1,65},{2,129},{3,193},{32,2},{33,66},{34,130},{35,194},{64,... | collective-permute-start | bytes 172040 | tf_op jit(solution)/shard_map/ppermute | solution.py:315
  148.7 0.7 collective-permute-start.1
  149.4 0.7 add_bitcast_fusion.place_ref
  150.0 0.0 collective-permute-done.4.four_ref
  150.0 14.4 %collective-permute-done.3.three_ref = f32[112,128]{1,0:T(8,128)S(1)} collective-permute-done((f32[112,128]{1,0:T(8,128)S(1)}, f32[112,128]{1,0:T(8,128)S(1)}, u32[]{:S(2)}, u32[]{:S(2)}) %collective-permute-start.3) | collective-permute-done | bytes 57376 | tf_op jit(solution)/shard_map/ppermute | solution.py:315
  164.4 0.6 copy-done.5
  165.0 0.0 copy-done.6
  165.1 0.6 copy-done.7
  165.7 2.2 %blocks.1 = f32[81,1024]{1,0:T(8,128)} custom-call(s32[1,2]{1,0:T(1,128)} %add_bitcast_fusion.place_ref, f32[112,128]{1,0:T(8,128)} %copy-done.7, f32[112,128]{1,0:T(8,128)} %copy-done.6, f32[112,128]{1,0:T(8,128)} %copy-done.5, f32[112,128]{1,0:T(8,128)} %copy-done.4, f32[32,32,128]{2,1,0:T(8,128)} %copy-done), custom_call_target="tpu_custom_call" | custom-call | tf_op jit(solution)/shard_map/blocks/pallas_call | solution.py:269
  167.9 0.0 collective-permute-done.other_ref
  167.9 1.0 copy-done.2
  168.9 4.3 %order.1 = f32[9,65536]{1,0:T(8,128)} custom-call(s32[1,1]{1,0:T(1,128)} %bitcast.core_ref, f32[2304,128]{1,0:T(8,128)} %bitcast.18, f32[2304,128]{1,0:T(8,128)} %copy-done.2), custom_call_target="tpu_custom_call" | custom-call | tf_op jit(solution)/shard_map/order/pallas_call | solution.py:291
  (28 shorter events, 0.2 us)
Async XLA Ops:
  48.0 31.3 %copy-start.8 = (s32[1,64]{1,0:T(1,128)S(1)}, s32[1,64]{1,0:T(1,128)}, u32[]{:S(2)}) copy-start(s32[1,64]{1,0:T(1,128)} %counts_ref.1) | copy-start | bytes 772
  48.0 32.5 %copy-start.3 = (s32[65536]{0:T(1024)S(1)}, s32[65536]{0:T(1024)}, u32[]{:S(2)}) copy-start(s32[65536]{0:T(1024)} %param.9) | copy-start | bytes 786436
  48.0 26.3 %all-to-all-start.1 = ((f32[8,128,128]{2,1,0:T(8,128)}), f32[8,128,128]{2,1,0:T(8,128)S(1)}, u32[]{:S(2)}, u32[]{:S(2)}) async-start(f32[8,128,128]{2,1,0:T(8,128)} %sums.1), calls=%async_computation.1 | async-start | bytes 1048576 | tf_op jit(solution)/shard_map/all_to_all | solution.py:301
  75.2 15.6 %all-to-all-start.2 = ((f32[32,32,128]{2,1,0:T(8,128)}), f32[32,32,128]{2,1,0:T(8,128)S(1)}, u32[]{:S(2)}, u32[]{:S(2)}) async-start(f32[32,32,128]{2,1,0:T(8,128)} %broadcast_in_dim.12), calls=%async_computation.2 | async-start | bytes 1048576 | tf_op jit(solution)/shard_map/all_to_all | solution.py:301
  90.8 0.8 copy-start
  137.8 30.0 %copy-start.1 = (f32[16,144,128]{2,1,0:T(8,128)}, f32[16,144,128]{2,1,0:T(8,128)S(1)}, u32[]{:S(2)}) copy-start(f32[16,144,128]{2,1,0:T(8,128)S(1)} %all_to_all.33) | copy-start | bytes 3538948
  137.8 30.0 %collective-permute-start = (f32[2304,128]{1,0:T(8,128)S(1)}, f32[2304,128]{1,0:T(8,128)S(1)}, u32[]{:S(2)}, u32[]{:S(2)}) collective-permute-start(f32[2304,128]{1,0:T(8,128)S(1)} %bitcast.17), channel_id=1, source_target_pairs={{0,4},{4,0},{1,5},{5,1},{2,6},{6,2},{3,7},{7,3},{8,12},{12,8},{9,1... | collective-permute-start | bytes 3538952 | tf_op jit(solution)/shard_map/ppermute | solution.py:346
  142.1 7.9 %collective-permute-start.4 = (f32[112,128]{1,0:T(8,128)S(1)}, f32[112,128]{1,0:T(8,128)S(1)}, u32[]{:S(2)}, u32[]{:S(2)}) collective-permute-start(f32[112,128]{1,0:T(8,128)S(1)} %slice.22), channel_id=1, source_target_pairs={{0,3},{1,67},{2,131},{3,195},{32,0},{33,64},{34,128},{35,192},{64,... | collective-permute-start | bytes 172040 | tf_op jit(solution)/shard_map/ppermute | solution.py:315
  144.7 19.7 %collective-permute-start.3 = (f32[112,128]{1,0:T(8,128)S(1)}, f32[112,128]{1,0:T(8,128)S(1)}, u32[]{:S(2)}, u32[]{:S(2)}) collective-permute-start(f32[112,128]{1,0:T(8,128)S(1)} %slice.22), channel_id=1, source_target_pairs={{0,2},{1,66},{2,130},{3,194},{32,3},{33,67},{34,131},{35,195},{64,... | collective-permute-start | bytes 172040 | tf_op jit(solution)/shard_map/ppermute | solution.py:315
  146.8 17.6 %collective-permute-start.2 = (f32[112,128]{1,0:T(8,128)S(1)}, f32[112,128]{1,0:T(8,128)S(1)}, u32[]{:S(2)}, u32[]{:S(2)}) collective-permute-start(f32[112,128]{1,0:T(8,128)S(1)} %slice.22), channel_id=1, source_target_pairs={{0,1},{1,65},{2,129},{3,193},{32,2},{33,66},{34,130},{35,194},{64,... | collective-permute-start | bytes 172040 | tf_op jit(solution)/shard_map/ppermute | solution.py:315
  148.7 15.7 %collective-permute-start.1 = (f32[112,128]{1,0:T(8,128)S(1)}, f32[112,128]{1,0:T(8,128)S(1)}, u32[]{:S(2)}, u32[]{:S(2)}) collective-permute-start(f32[112,128]{1,0:T(8,128)S(1)} %slice.22), channel_id=1, source_target_pairs={{0,0},{1,64},{2,128},{3,192},{32,1},{33,65},{34,129},{35,193},{64,... | collective-permute-start | bytes 172040 | tf_op jit(solution)/shard_map/ppermute | solution.py:315
  150.0 14.4 %copy-start.4 = (f32[112,128]{1,0:T(8,128)}, f32[112,128]{1,0:T(8,128)S(1)}, u32[]{:S(2)}) copy-start(f32[112,128]{1,0:T(8,128)S(1)} %collective-permute-done.4.four_ref) | copy-start | bytes 172036
  164.4 0.6 copy-start.5
  164.4 0.6 copy-start.6
  165.1 0.6 copy-start.7
  167.9 1.1 copy-start.2

commit v3 on v2

--- a/solution.py
+++ b/solution.py
@@ -17,7 +17,9 @@
 VALUES = 21
 BLOCK = 26
 HOT_ROWS = 14
-SHARE_ROWS = 128
+EXTRA_ROWS = 16
+GRAD_ROWS = 2 * CAMS + HOT_ROWS
+BLOCK_ROWS = 48
 OBS = ("z", "y", "c")
 PLANE = ("y", "c", "x")
 ALL = ("z", "y", "c", "x")
@@ -170,15 +172,18 @@
                 at = 2 * TERMS * part
                 both = acc_ref[side, at : at + TERMS, :] + acc_ref[side, at + TERMS : at + 2 * TERMS, :]
                 level = side * QUARTERS + part
-                out_ref[level, :TERMS, :] = both[:, :LANES]
-                out_ref[level, TERMS : 2 * TERMS, :] = both[:, LANES:]
-                out_ref[level, 2 * TERMS :, :] = hot_ref[...]
+                for half in range(2):
+                    lanes = slice(half * LANES, (half + 1) * LANES)
+                    at = GRAD_ROWS + half * BLOCK_ROWS
+                    out_ref[level, at : at + BLOCK_ROWS, :] = both[:BLOCK_ROWS, lanes]
+                    out_ref[level, half * CAMS : (half + 1) * CAMS, :] = both[PAIRS : PAIRS + CAMS, lanes]
+                out_ref[level, 2 * CAMS : GRAD_ROWS, :] = hot_ref[:HOT_ROWS]
 
 
 def camera_sums(arrived):
     rows = arrived.shape[0]
     depth = 8 * LANES
-    out = (2 * QUARTERS, SHARE_ROWS, LANES)
+    out = (2 * QUARTERS, GRAD_ROWS + 2 * BLOCK_ROWS, LANES)
     return pl.pallas_call(
         sums_body,
         grid=(rows // (16 * BLOCK),),
@@ -190,7 +195,7 @@
             pltpu.VMEM((2, 2 * TERMS * QUARTERS, depth), BF16),
             pltpu.VMEM((2, SPAN, depth), BF16),
             pltpu.VMEM((2, 2 * TERMS * QUARTERS, SPAN), F32),
-            pltpu.VMEM((SHARE_ROWS - 2 * TERMS, LANES), F32),
+            pltpu.VMEM((EXTRA_ROWS, LANES), F32),
         ],
         cost_estimate=pl.CostEstimate(
             flops=2 * 2 * TERMS * CAM_DEV * 128 * rows // BLOCK, transcendentals=0, bytes_accessed=rows * 512
@@ -252,10 +257,10 @@
         part = lax.rem(column - turn + QUARTERS, QUARTERS)
         for half in range(2):
             for group in range(4):
-                at = HOT_ROWS * group
-                hot = slots_ref[group * 8 + part * 2 + half, 2 * CAMS : 2 * CAMS + HOT_ROWS, :]
-                share = share_ref[half * TERMS + at : half * TERMS + at + HOT_ROWS, :]
-                rows_ref[at : at + HOT_ROWS, :] = share + jnp.where(own > 0, hot, 0.0)
+                start, stop = HOT_ROWS * group, min(HOT_ROWS * (group + 1), PAIRS)
+                hot = slots_ref[group * 8 + part * 2 + half, 2 * CAMS : 2 * CAMS + stop - start, :]
+                share = share_ref[half * BLOCK_ROWS + start : half * BLOCK_ROWS + stop, :]
+                rows_ref[start:stop, :] = share + jnp.where(own > 0, hot, 0.0)
             lanes = pl.ds(pl.multiple_of((part * 2 + half) * LANES, LANES), LANES)
             for k in range(CAMS):
                 for l in range(CAMS):
@@ -271,7 +276,7 @@
         out_shape=jax.ShapeDtypeStruct((CAMS * CAMS, CAM_DEV), F32),
         in_specs=[SMEM] + [VMEM] * 5,
         out_specs=VMEM,
-        scratch_shapes=[pltpu.VMEM((TERMS, LANES), F32)],
+        scratch_shapes=[pltpu.VMEM((BLOCK_ROWS, LANES), F32)],
         name="blocks",
     )(place, *shares, slots)
 
@@ -306,13 +311,17 @@
     return exchanged(jnp.broadcast_to(share[None], (count, *share.shape)), axes)
 
 
-def to_owner(share, turn):
+def to_owner(share):
     pairs = []
     for level in range(8):
         for column in range(4):
-            target = (2 * column + level // 4) * 4 + (level % 4 + turn) % 4
-            pairs.append((level * 4 + column, target))
+            pairs.append((level * 4 + column, (2 * column + level // 4) * 4 + level % 4))
     return lax.ppermute(share, ("z", "x"), pairs)
+
+
+def turned(share, turn):
+    count = lax.axis_size("x")
+    return lax.ppermute(share, "x", [(k, (k + turn) % count) for k in range(count)])
 
 
 def local(jacobians, residuals, camera_local, bucket_counts, camera_map):
@@ -330,18 +339,18 @@
     cameras = camera_local.reshape(1, -1)
     sent = packed(jacobians, residuals, cameras, bucket_counts, targets)
     arrived = exchanged(sent, PLANE)
-    summed = camera_sums(arrived.reshape(-1, LANES))
-    share = exchanged(summed, "z").sum(axis=0)
-    shares = [to_owner(share[: 2 * TERMS], turn) for turn in range(4)]
-    slots = [share[PAIRS : PAIRS + CAMS], share[TERMS + PAIRS : TERMS + PAIRS + CAMS]]
-    slots.append(share[2 * TERMS : 2 * TERMS + HOT_ROWS])
-    slots = from_all(jnp.concatenate(slots, axis=0), PLANE)
-    own = (hot == lax.axis_index(OBS)).astype(jnp.int32)
-    blocks = whole_blocks(jnp.stack([lax.axis_index("x"), own]).reshape(1, 2), shares, slots)
+    share = exchanged(camera_sums(arrived.reshape(-1, LANES)), "z").sum(axis=0)
+    squares = to_owner(share[GRAD_ROWS:])
+    slots = from_all(share[:GRAD_ROWS], PLANE)
+    slots, squares = lax.optimization_barrier((slots, squares))
+    shares = [squares] + [turned(squares, turn) for turn in range(1, QUARTERS)]
     first = lax.axis_index(PLANE) * levels * SPAN
     part = placed(slots, ids, first.reshape(1, 1), levels)
     part = exchanged(part, "z").sum(axis=0)
+    part, shares = lax.optimization_barrier((part, shares))
     part = from_all(part, "z")
+    own = (hot == lax.axis_index(OBS)).astype(jnp.int32)
+    blocks = whole_blocks(jnp.stack([lax.axis_index("x"), own]).reshape(1, 2), shares, slots)
     part = from_all(part.reshape(-1, LANES), ("y", "x")).reshape(-1, LANES)
     other = lax.ppermute(part, "c", [(0, 1), (1, 0)])
     gradient = ordered(core.reshape(1, 1), part, other)

time: 175 us -> 157 us (0.90)
  waiting for transfers between devices: 41.7 us -> 30.1 us
  blocking collectives: 72.6 us -> 64.9 us
  starting transfers between devices: 23.3 us -> 27.1 us
    ppermute x4 -> x1, waiting for transfers between devices: 14.4 us -> 0.01 us  [to_owner(): return lax.ppermute(share, ('z', 'x'), pairs)]
    all_to_all x4 -> x3, blocking collectives: 72.6 us -> 64.9 us  [exchanged(): return lax.all_to_all(pieces, axes, 0, 0, tiled=True)]
    ppermute x4 -> x1, starting transfers between devices: 7.22 us -> 0.66 us  [to_owner(): return lax.ppermute(share, ('z', 'x'), pairs)]
    ppermute x0 -> x3, starting transfers between devices: none -> 5.37 us  [turned(): lax.ppermute(share, 'x', [(k, (k + turn) % count) for k in range(count)])]
    all_to_all x2 -> x3, starting transfers between devices: 12.4 us -> 15.7 us  [exchanged(): return lax.all_to_all(pieces, axes, 0, 0, tiled=True)]
    all_to_all x2 -> x3, waiting for transfers between devices: 27.3 us -> 28.6 us  [exchanged(): return lax.all_to_all(pieces, axes, 0, 0, tiled=True)]
  transfers between devices with their start and end apart: 7 -> 8, of which waited for: 3 -> 4; matrix products, arithmetic and copies ran while one was open for 1% -> 1% of each run, Pallas kernels for 1% -> 1%
where the time goes in v3:
time: 157 us
  blocking collectives  64.9 us (41%)
  waiting for transfers between devices  30.1 us (19%)
  Pallas kernels  27.4 us (17%)
  starting transfers between devices  27.1 us (17%)
  local copies, waits for them, and re-layouts  3.03 us (2%)
  between operations  2.11 us (1%)
  other arithmetic  2.04 us (1%)
    all_to_all x3, blocking collectives, exchanged(): return lax.all_to_all(pieces, axes, 0, 0, tiled=True)  64.9 us
    all_to_all x3, waiting for transfers between devices, exchanged(): return lax.all_to_all(pieces, axes, 0, 0, tiled=True)  28.6 us
    all_to_all x3, starting transfers between devices, exchanged(): return lax.all_to_all(pieces, axes, 0, 0, tiled=True)  15.7 us
    pallas_call x1, Pallas kernels, camera_sums(): pl.pallas_call(sums_body, grid=(rows // (16 * BLOCK),), out_shape=jax.Sha...  10.8 us
    pallas_call x1, Pallas kernels, placed(): pl.pallas_call(place_body, out_shape=jax.ShapeDtypeStruct((ranges, 2 * CA...  5.96 us
    ppermute x3, starting transfers between devices, turned(): lax.ppermute(share, 'x', [(k, (k + turn) % count) for k in range(count)])  5.37 us
    ppermute x1, starting transfers between devices, local(): other = lax.ppermute(part, 'c', [(0, 1), (1, 0)])  5.29 us
    pallas_call x1, Pallas kernels, ordered(): pl.pallas_call(order_body, out_shape=jax.ShapeDtypeStruct((CAMS, 2 * own....  4.34 us
  transfers between devices with their start and end apart: 8, of which 4 were waited for; matrix products, arithmetic and copies ran while one was open for 1% of the time, Pallas kernels for 1%

profile of v3, /device:TPU:1, one launch (start us, length us, event | category | flops | bytes accessed | tf_op | source)
XLA Modules:
  0.0 156.6 jit_solution(5198966347389452738)
XLA Ops:
  0.6 4.1 %pack.1 = f32[32,104,128]{2,1,0:T(8,128)} custom-call(s32[1,64]{1,0:T(1,128)} %counts_ref.1, f32[18,32768]{1,0:T(8,128)} %jac_ref.1, f32[2,32768]{1,0:T(2,128)} %res_ref.1, s32[1,32768]{1,0:T(1,128)} %bitcast.20), custom_call_target="tpu_custom_call" | custom-call | tf_op jit(solution)/shard_map/pack/pallas_call | solution.py:119
  4.7 32.5 %all_to_all.30 = f32[32,104,128]{2,1,0:T(8,128)} all-to-all(f32[32,104,128]{2,1,0:T(8,128)} %pack.1), channel_id=1, replica_groups=mesh['z'=8,'y'=4,'c'=2,'x'=4] {'y','c','x'}, dimensions={0} | all-to-all | bytes 3407872 | tf_op jit(solution)/shard_map/all_to_all | solution.py:306
  37.2 10.8 %sums.1 = f32[8,128,128]{2,1,0:T(8,128)} custom-call(f32[3328,128]{1,0:T(8,128)} %bitcast.19), custom_call_target="tpu_custom_call" | custom-call | flops 3758096384 | bytes 1703936 | tf_op jit(solution)/shard_map/sums/pallas_call | solution.py:187
  48.1 8.3 %all-to-all-start.1 = ((f32[8,128,128]{2,1,0:T(8,128)}), f32[8,128,128]{2,1,0:T(8,128)S(1)}, u32[]{:S(2)}, u32[]{:S(2)}) async-start(f32[8,128,128]{2,1,0:T(8,128)} %sums.1), calls=%async_computation.1 | async-start | bytes 1048576 | tf_op jit(solution)/shard_map/all_to_all | solution.py:306
  56.4 18.0 %all-to-all-done.1 = f32[8,128,128]{2,1,0:T(8,128)S(1)} async-done(((f32[8,128,128]{2,1,0:T(8,128)}), f32[8,128,128]{2,1,0:T(8,128)S(1)}, u32[]{:S(2)}, u32[]{:S(2)}) %all-to-all-start.1) | async-done | bytes 524320 | tf_op jit(solution)/shard_map/all_to_all | solution.py:306
  74.4 0.9 broadcast_in_dim.12
  75.2 4.1 %all-to-all-start.2 = ((f32[32,32,128]{2,1,0:T(8,128)}), f32[32,32,128]{2,1,0:T(8,128)S(1)}, u32[]{:S(2)}, u32[]{:S(2)}) async-start(f32[32,32,128]{2,1,0:T(8,128)} %broadcast_in_dim.12), calls=%async_computation.2 | async-start | bytes 1048576 | tf_op jit(solution)/shard_map/all_to_all | solution.py:306
  79.3 0.7 bitcast_reduce_fusion
  80.7 0.1 reshape.41
  81.0 0.7 collective-permute-start
  81.7 0.6 pad_add_fusion.ids_ref
  82.3 0.0 collective-permute-done.one_ref
  82.3 8.5 %all-to-all-done.2.slots_ref = f32[32,32,128]{2,1,0:T(8,128)S(1)} async-done(((f32[32,32,128]{2,1,0:T(8,128)}), f32[32,32,128]{2,1,0:T(8,128)S(1)}, u32[]{:S(2)}, u32[]{:S(2)}) %all-to-all-start.2) | async-done | bytes 524320 | tf_op jit(solution)/shard_map/all_to_all | solution.py:306
  90.8 0.8 copy-done.1
  91.6 6.0 %place.1 = f32[8,18,128]{2,1,0:T(8,128)} custom-call(s32[1,1]{1,0:T(1,128)} %bitcast.1.first_ref, f32[32,32,128]{2,1,0:T(8,128)} %copy-done.1, s32[36,2,128]{2,1,0:T(2,128)} %pad_add_fusion.ids_ref), custom_call_target="tpu_custom_call" | custom-call | tf_op jit(solution)/shard_map/place/pallas_call | solution.py:240
  97.6 3.4 %all-to-all-start.3 = ((f32[8,18,128]{2,1,0:T(8,128)}), f32[8,18,128]{2,1,0:T(8,128)S(1)}, u32[]{:S(2)}, u32[]{:S(2)}) async-start(f32[8,18,128]{2,1,0:T(8,128)} %place.1), calls=%async_computation.3 | async-start | bytes 196608 | tf_op jit(solution)/shard_map/all_to_all | solution.py:306
  100.9 1.8 %collective-permute-start.3 = (f32[96,128]{1,0:T(8,128)S(1)}, f32[96,128]{1,0:T(8,128)S(1)}, u32[]{:S(2)}, u32[]{:S(2)}) collective-permute-start(f32[96,128]{1,0:T(8,128)S(1)} %collective-permute-done.one_ref), channel_id=1, source_target_pairs={{0,3},{1,0},{2,1},{3,2},{4,7},{5,4},{6,5},{7,6},{8,11},{9,8},{10,9... | collective-permute-start | bytes 147464 | tf_op jit(solution)/shard_map/ppermute | solution.py:324
  102.8 2.8 %collective-permute-start.2 = (f32[96,128]{1,0:T(8,128)S(1)}, f32[96,128]{1,0:T(8,128)S(1)}, u32[]{:S(2)}, u32[]{:S(2)}) collective-permute-start(f32[96,128]{1,0:T(8,128)S(1)} %collective-permute-done.one_ref), channel_id=1, source_target_pairs={{0,2},{1,3},{2,0},{3,1},{4,6},{5,7},{6,4},{7,5},{8,10},{9,11},{10,... | collective-permute-start | bytes 147464 | tf_op jit(solution)/shard_map/ppermute | solution.py:324
  105.5 0.8 collective-permute-start.1
  106.3 2.1 %all-to-all-done.3 = f32[8,18,128]{2,1,0:T(8,128)S(1)} async-done(((f32[8,18,128]{2,1,0:T(8,128)}), f32[8,18,128]{2,1,0:T(8,128)S(1)}, u32[]{:S(2)}, u32[]{:S(2)}) %all-to-all-start.3) | async-done | bytes 73760 | tf_op jit(solution)/shard_map/all_to_all | solution.py:306
  108.4 0.0 collective-permute-done.3.four_ref
  108.5 0.0 collective-permute-done.2.three_ref
  108.5 1.5 collective-permute-done.1.two_ref
  110.0 13.5 %all_to_all.31 = f32[8,18,128]{2,1,0:T(8,128)S(1)} all-to-all(f32[8,18,128]{2,1,0:T(8,128)S(1)} %broadcast_in_dim.25), channel_id=1, replica_groups=mesh['z'=8,'y'=4,'c'=2,'x'=4] {'z'}, dimensions={0} | all-to-all | bytes 147456 | tf_op jit(solution)/shard_map/all_to_all | solution.py:306
  123.5 0.1 broadcast_in_dim.27
  123.6 18.9 %all_to_all.32 = f32[16,144,128]{2,1,0:T(8,128)S(1)} all-to-all(f32[16,144,128]{2,1,0:T(8,128)S(1)} %broadcast_in_dim.27), channel_id=1, replica_groups=mesh['z'=8,'y'=4,'c'=2,'x'=4] {'y','x'}, dimensions={0} | all-to-all | bytes 2359296 | tf_op jit(solution)/shard_map/all_to_all | solution.py:306
  142.5 5.3 %collective-permute-start.4 = (f32[2304,128]{1,0:T(8,128)S(1)}, f32[2304,128]{1,0:T(8,128)S(1)}, u32[]{:S(2)}, u32[]{:S(2)}) collective-permute-start(f32[2304,128]{1,0:T(8,128)S(1)} %bitcast.17), channel_id=1, source_target_pairs={{0,4},{4,0},{1,5},{5,1},{2,6},{6,2},{3,7},{7,3},{8,12},{12,8},{9,1... | collective-permute-start | bytes 3538952 | tf_op jit(solution)/shard_map/ppermute | solution.py:355
  148.4 0.7 add_bitcast_fusion.place_ref
  149.1 2.1 %blocks.1 = f32[81,1024]{1,0:T(8,128)} custom-call(s32[1,2]{1,0:T(1,128)} %add_bitcast_fusion.place_ref, f32[96,128]{1,0:T(8,128)} %copy-done.4, f32[96,128]{1,0:T(8,128)} %copy-done.7, f32[96,128]{1,0:T(8,128)} %copy-done.6, f32[96,128]{1,0:T(8,128)} %copy-done.5, f32[32,32,128]{2,1,0:T(8,128)} %copy-done.1), custom_call_target="tpu_custom_call" | custom-call | tf_op jit(solution)/shard_map/blocks/pallas_call | solution.py:274
  151.2 0.0 collective-permute-done.4.other_ref
  151.2 1.0 copy-done.2
  152.3 4.3 %order.1 = f32[9,65536]{1,0:T(8,128)} custom-call(s32[1,1]{1,0:T(1,128)} %bitcast.core_ref, f32[2304,128]{1,0:T(8,128)} %bitcast.18, f32[2304,128]{1,0:T(8,128)} %copy-done.2), custom_call_target="tpu_custom_call" | custom-call | tf_op jit(solution)/shard_map/order/pallas_call | solution.py:296
  (27 shorter events, 0.2 us)
Async XLA Ops:
  48.0 31.2 %copy-start.8 = (s32[1,64]{1,0:T(1,128)S(1)}, s32[1,64]{1,0:T(1,128)}, u32[]{:S(2)}) copy-start(s32[1,64]{1,0:T(1,128)} %counts_ref.1) | copy-start | bytes 772
  48.0 32.6 %copy-start.3 = (s32[65536]{0:T(1024)S(1)}, s32[65536]{0:T(1024)}, u32[]{:S(2)}) copy-start(s32[65536]{0:T(1024)} %param.9) | copy-start | bytes 786436
  48.1 26.3 %all-to-all-start.1 = ((f32[8,128,128]{2,1,0:T(8,128)}), f32[8,128,128]{2,1,0:T(8,128)S(1)}, u32[]{:S(2)}, u32[]{:S(2)}) async-start(f32[8,128,128]{2,1,0:T(8,128)} %sums.1), calls=%async_computation.1 | async-start | bytes 1048576 | tf_op jit(solution)/shard_map/all_to_all | solution.py:306
  75.2 15.6 %all-to-all-start.2 = ((f32[32,32,128]{2,1,0:T(8,128)}), f32[32,32,128]{2,1,0:T(8,128)S(1)}, u32[]{:S(2)}, u32[]{:S(2)}) async-start(f32[32,32,128]{2,1,0:T(8,128)} %broadcast_in_dim.12), calls=%async_computation.2 | async-start | bytes 1048576 | tf_op jit(solution)/shard_map/all_to_all | solution.py:306
  81.0 1.3 collective-permute-start
  82.3 66.8 %copy-start.4 = (f32[96,128]{1,0:T(8,128)}, f32[96,128]{1,0:T(8,128)S(1)}, u32[]{:S(2)}) copy-start(f32[96,128]{1,0:T(8,128)S(1)} %collective-permute-done.one_ref) | copy-start | bytes 147460
  90.8 0.8 copy-start.1
  97.6 10.9 %all-to-all-start.3 = ((f32[8,18,128]{2,1,0:T(8,128)}), f32[8,18,128]{2,1,0:T(8,128)S(1)}, u32[]{:S(2)}, u32[]{:S(2)}) async-start(f32[8,18,128]{2,1,0:T(8,128)} %place.1), calls=%async_computation.3 | async-start | bytes 196608 | tf_op jit(solution)/shard_map/all_to_all | solution.py:306
  100.9 7.5 %collective-permute-start.3 = (f32[96,128]{1,0:T(8,128)S(1)}, f32[96,128]{1,0:T(8,128)S(1)}, u32[]{:S(2)}, u32[]{:S(2)}) collective-permute-start(f32[96,128]{1,0:T(8,128)S(1)} %collective-permute-done.one_ref), channel_id=1, source_target_pairs={{0,3},{1,0},{2,1},{3,2},{4,7},{5,4},{6,5},{7,6},{8,11},{9,8},{10,9... | collective-permute-start | bytes 147464 | tf_op jit(solution)/shard_map/ppermute | solution.py:324
  102.8 5.7 %collective-permute-start.2 = (f32[96,128]{1,0:T(8,128)S(1)}, f32[96,128]{1,0:T(8,128)S(1)}, u32[]{:S(2)}, u32[]{:S(2)}) collective-permute-start(f32[96,128]{1,0:T(8,128)S(1)} %collective-permute-done.one_ref), channel_id=1, source_target_pairs={{0,2},{1,3},{2,0},{3,1},{4,6},{5,7},{6,4},{7,5},{8,10},{9,11},{10,... | collective-permute-start | bytes 147464 | tf_op jit(solution)/shard_map/ppermute | solution.py:324
  105.5 4.4 %collective-permute-start.1 = (f32[96,128]{1,0:T(8,128)S(1)}, f32[96,128]{1,0:T(8,128)S(1)}, u32[]{:S(2)}, u32[]{:S(2)}) collective-permute-start(f32[96,128]{1,0:T(8,128)S(1)} %collective-permute-done.one_ref), channel_id=1, source_target_pairs={{0,1},{1,2},{2,3},{3,0},{4,5},{5,6},{6,7},{7,4},{8,9},{9,10},{10,1... | collective-permute-start | bytes 147464 | tf_op jit(solution)/shard_map/ppermute | solution.py:324
  108.5 34.0 %copy-start.5 = (f32[96,128]{1,0:T(8,128)}, f32[96,128]{1,0:T(8,128)S(1)}, u32[]{:S(2)}) copy-start(f32[96,128]{1,0:T(8,128)S(1)} %collective-permute-done.3.four_ref) | copy-start | bytes 147460
  108.5 34.0 %copy-start.6 = (f32[96,128]{1,0:T(8,128)}, f32[96,128]{1,0:T(8,128)S(1)}, u32[]{:S(2)}) copy-start(f32[96,128]{1,0:T(8,128)S(1)} %collective-permute-done.2.three_ref) | copy-start | bytes 147460
  110.0 32.5 %copy-start.7 = (f32[96,128]{1,0:T(8,128)}, f32[96,128]{1,0:T(8,128)S(1)}, u32[]{:S(2)}) copy-start(f32[96,128]{1,0:T(8,128)S(1)} %collective-permute-done.1.two_ref) | copy-start | bytes 147460
  142.5 8.8 %copy-start = (f32[16,144,128]{2,1,0:T(8,128)}, f32[16,144,128]{2,1,0:T(8,128)S(1)}, u32[]{:S(2)}) copy-start(f32[16,144,128]{2,1,0:T(8,128)S(1)} %all_to_all.32) | copy-start | bytes 3538948
  142.5 8.7 %collective-permute-start.4 = (f32[2304,128]{1,0:T(8,128)S(1)}, f32[2304,128]{1,0:T(8,128)S(1)}, u32[]{:S(2)}, u32[]{:S(2)}) collective-permute-start(f32[2304,128]{1,0:T(8,128)S(1)} %bitcast.17), channel_id=1, source_target_pairs={{0,4},{4,0},{1,5},{5,1},{2,6},{6,2},{3,7},{7,3},{8,12},{12,8},{9,1... | collective-permute-start | bytes 3538952 | tf_op jit(solution)/shard_map/ppermute | solution.py:355
  151.2 1.0 copy-start.2

commit v4 on v3

--- a/solution.py
+++ b/solution.py
@@ -20,6 +20,7 @@
 EXTRA_ROWS = 16
 GRAD_ROWS = 2 * CAMS + HOT_ROWS
 BLOCK_ROWS = 48
+PAIRS_PER_STEP = 4
 OBS = ("z", "y", "c")
 PLANE = ("y", "c", "x")
 ALL = ("z", "y", "c", "x")
@@ -27,6 +28,10 @@
 BF16 = jnp.bfloat16
 VMEM = pl.BlockSpec(memory_space=pltpu.VMEM)
 SMEM = pl.BlockSpec(memory_space=pltpu.SMEM)
+
+
+def near(x):
+    return pltpu.with_memory_space_constraint(x, pltpu.VMEM)
 
 
 def two_pieces(x):
@@ -139,7 +144,7 @@
         terms_ref[...] = jnp.zeros_like(terms_ref)
         hot_ref[...] = jnp.zeros_like(hot_ref)
 
-    for pair in range(2):
+    for pair in range(PAIRS_PER_STEP):
         start = pair * 8 * BLOCK
         value = [arrived_ref[pl.ds(start + row, 8, stride=BLOCK), :] for row in range(VALUES)]
         for turn in range(5):
@@ -153,17 +158,17 @@
         ids = value[20].astype(jnp.int32)
         for group in range(8):
             x = terms_ref[pair, group * TERMS : (group + 1) * TERMS, :]
-            side, half = group % 4 // 2, group % 2
-            at = ((pair * 2 + group // 4) * 2 + half) * LANES
+            side = group % 4 // 2
+            at = (group // 4 * 2 + group % 2) * LANES
             row = ids[group : group + 1, :]
-            set_operands(left_ref.at[side], right_ref.at[side], x, row, QUARTERS, at)
-    for source in range(4):
-        for block in range(4):
-            part = hot_piece(block)
-            row = (source * 4 + block) * BLOCK + VALUES
-            hot_ref[part, :] += arrived_ref[row : row + part.stop - part.start, :]
-    for side in range(2):
-        acc_ref[side] += product(left_ref[side], right_ref[side])
+            set_operands(left_ref.at[pair, side], right_ref.at[pair, side], x, row, QUARTERS, at)
+        for source in range(2):
+            for block in range(4):
+                part = hot_piece(block)
+                row = start + (source * 4 + block) * BLOCK + VALUES
+                hot_ref[part, :] += arrived_ref[row : row + part.stop - part.start, :]
+        for side in range(2):
+            acc_ref[side] += product(left_ref[pair, side], right_ref[pair, side])
 
     @pl.when(step == pl.num_programs(0) - 1)
     def _():
@@ -182,18 +187,19 @@
 
 def camera_sums(arrived):
     rows = arrived.shape[0]
-    depth = 8 * LANES
+    depth = 4 * LANES
+    step = 8 * BLOCK * PAIRS_PER_STEP
     out = (2 * QUARTERS, GRAD_ROWS + 2 * BLOCK_ROWS, LANES)
     return pl.pallas_call(
         sums_body,
-        grid=(rows // (16 * BLOCK),),
+        grid=(rows // step,),
         out_shape=jax.ShapeDtypeStruct(out, F32),
-        in_specs=[pl.BlockSpec((16 * BLOCK, LANES), lambda i: (i, 0))],
+        in_specs=[pl.BlockSpec((step, LANES), lambda i: (i, 0))],
         out_specs=pl.BlockSpec(out, lambda i: (0, 0, 0)),
         scratch_shapes=[
-            pltpu.VMEM((2, 8 * TERMS, LANES), F32),
-            pltpu.VMEM((2, 2 * TERMS * QUARTERS, depth), BF16),
-            pltpu.VMEM((2, SPAN, depth), BF16),
+            pltpu.VMEM((PAIRS_PER_STEP, 8 * TERMS, LANES), F32),
+            pltpu.VMEM((PAIRS_PER_STEP, 2, 2 * TERMS * QUARTERS, depth), BF16),
+            pltpu.VMEM((PAIRS_PER_STEP, 2, SPAN, depth), BF16),
             pltpu.VMEM((2, 2 * TERMS * QUARTERS, SPAN), F32),
             pltpu.VMEM((EXTRA_ROWS, LANES), F32),
         ],
@@ -204,30 +210,28 @@
     )(arrived)
 
 
-def place_body(first_ref, slots_ref, ids_ref, out_ref, left_ref, right_ref, acc_ref):
+def place_body(slots_ref, codes_ref, out_ref, left_ref, right_ref, acc_ref):
     sources = slots_ref.shape[0]
     ranges = out_ref.shape[0]
-    first = first_ref[0, 0]
-    acc_ref[...] = jnp.zeros_like(acc_ref)
-
-    def set_group(x, ids, group):
-        x = jnp.concatenate([x, jnp.zeros((16 - CAMS, LANES), F32)], axis=0)
-        set_operands(left_ref, right_ref, x, ids - first, ranges, group * LANES)
-
-    def add(step, carry):
+    blank = jnp.zeros((16 - CAMS, LANES), F32)
+
+    def set_group(x, codes, chunk, group):
+        x = jnp.concatenate([x, blank], axis=0)
+        set_operands(left_ref.at[chunk], right_ref.at[chunk], x, codes, ranges, group * LANES)
+
+    for chunk in range(sources // 4):
         for group in range(8):
-            source, half = step * 4 + group // 2, group % 2
+            source, half = chunk * 4 + group // 2, group % 2
             x = slots_ref[source, half * CAMS : (half + 1) * CAMS, :]
-            set_group(x, ids_ref[source, half : half + 1, :], group)
-        acc_ref[...] += product(left_ref[...], right_ref[...])
-        return carry
-
-    lax.fori_loop(0, sources // 4, add, 0)
+            set_group(x, codes_ref[source, half : half + 1, :], chunk, group)
+        summed = product(left_ref[chunk], right_ref[chunk])
+        acc_ref[...] = summed if chunk == 0 else acc_ref[...] + summed
     row = 2 * CAMS + PAIRS % HOT_ROWS
-    for group in range(8):
-        x = slots_ref[PAIRS // HOT_ROWS * 8 + group, row : row + CAMS, :]
-        set_group(x, ids_ref[sources + group // 2, group % 2 : group % 2 + 1, :], group)
-    acc_ref[...] += product(left_ref[...], right_ref[...])
+    for group in range(4):
+        x = slots_ref[PAIRS // HOT_ROWS * 4 + group, row : row + CAMS, :]
+        set_group(x, codes_ref[sources + group // 2, group % 2 : group % 2 + 1, :], sources // 4, group)
+    depth = 4 * LANES
+    acc_ref[...] += product(left_ref[sources // 4, :, :depth], right_ref[sources // 4, :, :depth])
     for part in range(ranges):
         at = 32 * part
         both = acc_ref[at : at + CAMS, :] + acc_ref[at + 16 : at + 16 + CAMS, :]
@@ -235,30 +239,34 @@
         out_ref[part, CAMS:, :] = both[:, LANES:]
 
 
-def placed(slots, ids, first, ranges):
+def placed(slots, codes, ranges):
     depth = 8 * LANES
+    chunks = slots.shape[0] // 4 + 1
     return pl.pallas_call(
         place_body,
         out_shape=jax.ShapeDtypeStruct((ranges, 2 * CAMS, LANES), F32),
-        in_specs=[SMEM, VMEM, VMEM],
+        in_specs=[VMEM, VMEM],
         out_specs=VMEM,
         scratch_shapes=[
-            pltpu.VMEM((32 * ranges, depth), BF16),
-            pltpu.VMEM((SPAN, depth), BF16),
+            pltpu.VMEM((chunks, 32 * ranges, depth), BF16),
+            pltpu.VMEM((chunks, SPAN, depth), BF16),
             pltpu.VMEM((32 * ranges, SPAN), F32),
         ],
         name="place",
-    )(first, slots, ids)
-
-
-def blocks_body(place_ref, one_ref, two_ref, three_ref, four_ref, slots_ref, out_ref, rows_ref):
-    column, own = place_ref[0, 0], place_ref[0, 1]
+    )(near(slots), near(codes))
+
+
+def blocks_body(place_ref, one_ref, two_ref, three_ref, four_ref, hot_ref, other_ref, out_ref, rows_ref):
+    column, core, own = place_ref[0, 0], place_ref[0, 1], place_ref[0, 2]
     for turn, share_ref in enumerate((one_ref, two_ref, three_ref, four_ref)):
         part = lax.rem(column - turn + QUARTERS, QUARTERS)
         for half in range(2):
             for group in range(4):
                 start, stop = HOT_ROWS * group, min(HOT_ROWS * (group + 1), PAIRS)
-                hot = slots_ref[group * 8 + part * 2 + half, 2 * CAMS : 2 * CAMS + stop - start, :]
+                source = group * 4 + lax.rem(part, 2) * 2 + half
+                here = hot_ref[source, : stop - start, :]
+                there = other_ref[source, : stop - start, :]
+                hot = jnp.where(lax.div(part, 2) == core, here, there)
                 share = share_ref[half * BLOCK_ROWS + start : half * BLOCK_ROWS + stop, :]
                 rows_ref[start:stop, :] = share + jnp.where(own > 0, hot, 0.0)
             lanes = pl.ds(pl.multiple_of((part * 2 + half) * LANES, LANES), LANES)
@@ -270,36 +278,51 @@
                     out_ref[at : at + 1, lanes] = rows_ref[row : row + 1, :]
 
 
-def whole_blocks(place, shares, slots):
+def whole_blocks(place, shares, hot, other):
     return pl.pallas_call(
         blocks_body,
         out_shape=jax.ShapeDtypeStruct((CAMS * CAMS, CAM_DEV), F32),
-        in_specs=[SMEM] + [VMEM] * 5,
+        in_specs=[SMEM] + [VMEM] * 6,
         out_specs=VMEM,
         scratch_shapes=[pltpu.VMEM((BLOCK_ROWS, LANES), F32)],
         name="blocks",
-    )(place, *shares, slots)
-
-
-def order_body(core_ref, own_ref, other_ref, out_ref):
-    for turn, rows_ref in enumerate((own_ref, other_ref)):
-        core = jnp.bitwise_xor(core_ref[0, 0], turn)
-        for ends in range(rows_ref.shape[0] // (16 * CAMS)):
-            x, y = ends % 4, ends // 4
-            for tile in range(16):
-                source = (ends * 16 + tile) * CAMS
-                at = pl.multiple_of((((y * 2 + core) * 4 + x) * 16 + tile) * LANES, LANES)
-                out_ref[:, pl.ds(at, LANES)] = rows_ref[source : source + CAMS, :]
-
-
-def ordered(core, own, other):
+    )(place, *[near(x) for x in (*shares, hot, other)])
+
+
+def order_body(core_ref, rows_ref, *refs):
+    out_ref = refs[-1]
+    tiles = rows_ref.shape[1] // CAMS
+    ends = out_ref.shape[1] // (tiles * LANES)
+    for end in range(ends):
+        source = pl.program_id(0) * ends + end
+        for tile in range(tiles):
+            at = (end * tiles + tile) * LANES
+            out_ref[:, at : at + LANES] = rows_ref[source, tile * CAMS : (tile + 1) * CAMS, :]
+
+
+def ordered(core, rows, before=None):
+    ends, depth, lanes = rows.shape
+    steps = 4
+    width = ends // steps * depth // CAMS * lanes
+    whole = jax.ShapeDtypeStruct((CAMS, 2 * steps * width), F32)
+    in_specs = [VMEM]
+    operands, aliases = [core, near(rows)], {}
+    if before is not None:
+        in_specs.append(pl.BlockSpec(memory_space=pl.ANY))
+        operands.append(before)
+        aliases = {2: 0}
     return pl.pallas_call(
         order_body,
-        out_shape=jax.ShapeDtypeStruct((CAMS, 2 * own.shape[0] // CAMS * LANES), F32),
-        in_specs=[SMEM, VMEM, VMEM],
-        out_specs=VMEM,
+        grid_spec=pltpu.PrefetchScalarGridSpec(
+            num_scalar_prefetch=1,
+            grid=(steps,),
+            in_specs=in_specs,
+            out_specs=pl.BlockSpec((CAMS, width), lambda i, core: (0, core[0] * steps + i)),
+        ),
+        out_shape=whole,
+        input_output_aliases=aliases,
         name="order",
-    )(core, own, other)
+    )(*operands)
 
 
 def exchanged(pieces, axes):
@@ -324,36 +347,46 @@
     return lax.ppermute(share, "x", [(k, (k + turn) % count) for k in range(count)])
 
 
+def swapped(mine):
+    return lax.ppermute(mine, "c", [(0, 1), (1, 0)])
+
+
 def local(jacobians, residuals, camera_local, bucket_counts, camera_map):
     targets = lax.axis_size(PLANE)
-    levels = lax.axis_size("z")
     level, core = lax.axis_index("z"), lax.axis_index("c")
     hot = jnp.argmax(bucket_counts[0])
     ids = camera_map.reshape(4, 2, 4, 2, QUARTERS, SPAN)
-    ids = lax.dynamic_slice(ids, (0, level // 4, 0, 0, level % 4, 0), (4, 1, 4, 2, 1, SPAN))
-    ids = ids.reshape(4, 4, 2, SPAN).transpose(1, 2, 0, 3).reshape(targets, 2, LANES)
-    hot_ids = lax.dynamic_slice_in_dim(camera_map, hot * CAM_DEV, CAM_DEV)
+    ids = lax.dynamic_slice(ids, (0, level // 4, 0, core, level % 4, 0), (4, 1, 4, 1, 1, SPAN))
+    ids = ids.reshape(4, 4, SPAN).transpose(1, 0, 2).reshape(-1, 2, LANES)
+    hot_ids = lax.dynamic_slice_in_dim(camera_map, hot * CAM_DEV + core * 4 * LANES, 4 * LANES)
     hot_ids = jnp.where(level == 0, hot_ids, -1).reshape(-1, 2, LANES)
     ids = jnp.concatenate([ids, hot_ids], axis=0)
+    here = jnp.bitwise_and(jnp.right_shift(ids, 11), 15) == lax.axis_index(("y", "x"))
+    codes = jnp.right_shift(ids, 15) * 8 * SPAN + jnp.bitwise_and(ids, 8 * SPAN - 1)
+    codes = jnp.where(here & (ids >= 0), codes, -SPAN)
 
     cameras = camera_local.reshape(1, -1)
     sent = packed(jacobians, residuals, cameras, bucket_counts, targets)
     arrived = exchanged(sent, PLANE)
     share = exchanged(camera_sums(arrived.reshape(-1, LANES)), "z").sum(axis=0)
     squares = to_owner(share[GRAD_ROWS:])
-    slots = from_all(share[:GRAD_ROWS], PLANE)
+    slots = from_all(share[:GRAD_ROWS], ("y", "x"))
     slots, squares = lax.optimization_barrier((slots, squares))
     shares = [squares] + [turned(squares, turn) for turn in range(1, QUARTERS)]
-    first = lax.axis_index(PLANE) * levels * SPAN
-    part = placed(slots, ids, first.reshape(1, 1), levels)
-    part = exchanged(part, "z").sum(axis=0)
-    part, shares = lax.optimization_barrier((part, shares))
+    part = placed(slots, codes, 16)
+    own_hot = slots[:, 2 * CAMS :]
+    other_hot = swapped(own_hot)
+    part = exchanged(part, ("c", "z")).sum(axis=0)
+    part, shares, other_hot = lax.optimization_barrier((part, shares, other_hot))
     part = from_all(part, "z")
     own = (hot == lax.axis_index(OBS)).astype(jnp.int32)
-    blocks = whole_blocks(jnp.stack([lax.axis_index("x"), own]).reshape(1, 2), shares, slots)
-    part = from_all(part.reshape(-1, LANES), ("y", "x")).reshape(-1, LANES)
-    other = lax.ppermute(part, "c", [(0, 1), (1, 0)])
-    gradient = ordered(core.reshape(1, 1), part, other)
+    place = jnp.stack([lax.axis_index("x"), core, own]).reshape(1, 3)
+    blocks = whole_blocks(place, shares, own_hot, other_hot)
+    part = from_all(part.reshape(-1, LANES), ("y", "x"))
+    part, blocks = lax.optimization_barrier((part, blocks))
+    other = swapped(part)
+    gradient = ordered(core.reshape(1), part)
+    gradient = ordered((1 - core).reshape(1), other, gradient)
     return gradient, blocks
 
 

time: 157 us -> 149 us (0.949)
  blocking collectives: 64.9 us -> 46.8 us
  waiting for transfers between devices: 30.1 us -> 41.8 us
  Pallas kernels: 27.4 us -> 21.3 us
  starting transfers between devices: 27.1 us -> 32.8 us
    all_to_all x3 -> x2, blocking collectives: 64.9 us -> 46.8 us  [exchanged(): return lax.all_to_all(pieces, axes, 0, 0, tiled=True)]
    all_to_all x3 -> x4, waiting for transfers between devices: 28.6 us -> 40.7 us  [exchanged(): return lax.all_to_all(pieces, axes, 0, 0, tiled=True)]
    all_to_all x3 -> x4, starting transfers between devices: 15.7 us -> 23.6 us  [exchanged(): return lax.all_to_all(pieces, axes, 0, 0, tiled=True)]
    pallas_call x1, Pallas kernels: 5.96 us -> 2.96 us  [placed(): pl.pallas_call(place_body, out_shape=jax.ShapeDtypeStruct((ranges, 2 * CA...]
    pallas_call x2 -> x3, Pallas kernels: 15.2 us -> 12.6 us  [the longest x1 8.97 us: camera_sums(): pl.pallas_call(sums_body, grid=(rows // step,), out_shape=jax.ShapeDtypeS...]
    unnamed x19 -> x4, local copies, waits for them, and re-layouts: 1.87 us -> 0.01 us
    ppermute x1 -> x2, starting transfers between devices: 5.29 us -> 4.05 us  [swapped(): return lax.ppermute(mine, 'c', [(0, 1), (1, 0)])]
  transfers between devices with their start and end apart: 8 -> 10, of which waited for: 4 -> 6; matrix products, arithmetic and copies ran while one was open for 1% -> 1% of each run, Pallas kernels for 1% -> 2%
where the time goes in v4:
time: 149 us; the launch traced here: 148 us
  blocking collectives  46.8 us (31%)
  waiting for transfers between devices  41.8 us (28%)
  starting transfers between devices  32.8 us (22%)
  Pallas kernels  21.3 us (14%)
  between operations  2.08 us (1%)
  local copies, waits for them, and re-layouts  2.04 us (1%)
    all_to_all x2, blocking collectives, exchanged(): return lax.all_to_all(pieces, axes, 0, 0, tiled=True)  46.8 us
    all_to_all x4, waiting for transfers between devices, exchanged(): return lax.all_to_all(pieces, axes, 0, 0, tiled=True)  40.7 us
    all_to_all x4, starting transfers between devices, exchanged(): return lax.all_to_all(pieces, axes, 0, 0, tiled=True)  23.6 us
    pallas_call x1, Pallas kernels, camera_sums(): pl.pallas_call(sums_body, grid=(rows // step,), out_shape=jax.ShapeDtypeS...  8.97 us
    ppermute x3, starting transfers between devices, turned(): lax.ppermute(share, 'x', [(k, (k + turn) % count) for k in range(count)])  4.46 us
    pallas_call x1, Pallas kernels, packed(): pl.pallas_call(pack_body, out_shape=jax.ShapeDtypeStruct((targets, 4 * BL...  4.09 us
    ppermute x2, starting transfers between devices, swapped(): return lax.ppermute(mine, 'c', [(0, 1), (1, 0)])  4.05 us
    pallas_call x2, Pallas kernels, ordered(): pl.pallas_call(order_body, grid_spec=pltpu.PrefetchScalarGridSpec(num_sca...  3.65 us
  transfers between devices with their start and end apart: 10, of which 6 were waited for; matrix products, arithmetic and copies ran while one was open for 1% of the time, Pallas kernels for 2%

profile of v4, /device:TPU:1, one launch (start us, length us, event | category | flops | bytes accessed | tf_op | source)
XLA Modules:
  0.0 148.3 jit_solution(672030569745432751)
XLA Ops:
  0.6 4.1 %pack.1 = f32[32,104,128]{2,1,0:T(8,128)} custom-call(s32[1,64]{1,0:T(1,128)} %counts_ref.1, f32[18,32768]{1,0:T(8,128)} %jac_ref.1, f32[2,32768]{1,0:T(2,128)} %res_ref.1, s32[1,32768]{1,0:T(1,128)} %bitcast.18), custom_call_target="tpu_custom_call" | custom-call | tf_op jit(solution)/shard_map/pack/pallas_call | solution.py:124
  4.7 32.5 %all_to_all.30 = f32[32,104,128]{2,1,0:T(8,128)} all-to-all(f32[32,104,128]{2,1,0:T(8,128)} %pack.1), channel_id=1, replica_groups=mesh['z'=8,'y'=4,'c'=2,'x'=4] {'y','c','x'}, dimensions={0} | all-to-all | bytes 3407872 | tf_op jit(solution)/shard_map/all_to_all | solution.py:329
  37.2 9.0 %sums.1 = f32[8,128,128]{2,1,0:T(8,128)} custom-call(f32[3328,128]{1,0:T(8,128)} %bitcast.17), custom_call_target="tpu_custom_call" | custom-call | flops 3758096384 | bytes 1703936 | tf_op jit(solution)/shard_map/sums/pallas_call | solution.py:193
  46.2 8.2 %all-to-all-start.1 = ((f32[8,128,128]{2,1,0:T(8,128)}), f32[8,128,128]{2,1,0:T(8,128)S(1)}, u32[]{:S(2)}, u32[]{:S(2)}) async-start(f32[8,128,128]{2,1,0:T(8,128)} %sums.1), calls=%async_computation.1 | async-start | bytes 1048576 | tf_op jit(solution)/shard_map/all_to_all | solution.py:329
  54.4 0.1 reshape.35
  54.6 0.7 bitcast_reduce_fusion
  55.2 17.1 %all-to-all-done.1 = f32[8,128,128]{2,1,0:T(8,128)S(1)} async-done(((f32[8,128,128]{2,1,0:T(8,128)}), f32[8,128,128]{2,1,0:T(8,128)S(1)}, u32[]{:S(2)}, u32[]{:S(2)}) %all-to-all-start.1) | async-done | bytes 524320 | tf_op jit(solution)/shard_map/all_to_all | solution.py:329
  72.4 0.7 broadcast_in_dim.27
  73.1 3.5 %all-to-all-start.2 = ((f32[16,32,128]{2,1,0:T(8,128)}), f32[16,32,128]{2,1,0:T(8,128)S(1)}, u32[]{:S(2)}, u32[]{:S(2)}) async-start(f32[16,32,128]{2,1,0:T(8,128)} %broadcast_in_dim.27), calls=%async_computation.2 | async-start | bytes 524288 | tf_op jit(solution)/shard_map/all_to_all | solution.py:329
  77.4 0.1 dynamic-slice_select_fusion
  77.5 0.7 collective-permute-start
  78.2 0.0 collective-permute-done.one_ref
  78.2 6.7 %all-to-all-done.2.slots_ref = f32[16,32,128]{2,1,0:T(8,128)S(1)} async-done(((f32[16,32,128]{2,1,0:T(8,128)}), f32[16,32,128]{2,1,0:T(8,128)S(1)}, u32[]{:S(2)}, u32[]{:S(2)}) %all-to-all-start.2) | async-done | bytes 262176 | tf_op jit(solution)/shard_map/all_to_all | solution.py:329
  84.9 3.0 %place.1 = f32[16,18,128]{2,1,0:T(8,128)} custom-call(f32[16,32,128]{2,1,0:T(8,128)S(1)} %all-to-all-done.2.slots_ref, s32[18,2,128]{2,1,0:T(2,128)S(1)} %and_select_fusion.codes_ref), custom_call_target="tpu_custom_call" | custom-call | tf_op jit(solution)/shard_map/place/pallas_call | solution.py:245
  87.9 7.2 %all-to-all-start.3 = ((f32[16,18,128]{2,1,0:T(8,128)}), f32[16,18,128]{2,1,0:T(8,128)S(1)}, u32[]{:S(2)}, u32[]{:S(2)}) async-start(f32[16,18,128]{2,1,0:T(8,128)} %place.1), calls=%async_computation.3 | async-start | bytes 393216 | tf_op jit(solution)/shard_map/all_to_all | solution.py:329
  95.1 0.2 collective-permute-start.4
  95.3 2.3 %collective-permute-start.3 = (f32[96,128]{1,0:T(8,128)S(1)}, f32[96,128]{1,0:T(8,128)S(1)}, u32[]{:S(2)}, u32[]{:S(2)}) collective-permute-start(f32[96,128]{1,0:T(8,128)S(1)} %collective-permute-done.one_ref), channel_id=1, source_target_pairs={{0,3},{1,0},{2,1},{3,2},{4,7},{5,4},{6,5},{7,6},{8,11},{9,8},{10,9... | collective-permute-start | bytes 147464 | tf_op jit(solution)/shard_map/ppermute | solution.py:347
  97.6 1.3 collective-permute-start.2
  98.9 0.8 collective-permute-start.1
  99.7 3.6 %all-to-all-done.3 = f32[16,18,128]{2,1,0:T(8,128)S(1)} async-done(((f32[16,18,128]{2,1,0:T(8,128)}), f32[16,18,128]{2,1,0:T(8,128)S(1)}, u32[]{:S(2)}, u32[]{:S(2)}) %all-to-all-start.3) | async-done | bytes 147488 | tf_op jit(solution)/shard_map/all_to_all | solution.py:329
  103.4 0.0 collective-permute-done.2.three_ref
  103.4 0.5 collective-permute-done.1.two_ref
  103.9 14.3 %all_to_all.31 = f32[8,18,128]{2,1,0:T(8,128)S(1)} all-to-all(f32[8,18,128]{2,1,0:T(8,128)S(1)} %broadcast_in_dim.30), channel_id=1, replica_groups=mesh['z'=8,'y'=4,'c'=2,'x'=4] {'z'}, dimensions={0} | all-to-all | bytes 147456 | tf_op jit(solution)/shard_map/all_to_all | solution.py:329
  118.2 1.1 broadcast_in_dim.32
  119.3 4.7 %all-to-all-start.5 = ((f32[16,144,128]{2,1,0:T(8,128)}), f32[16,144,128]{2,1,0:T(8,128)S(1)}, u32[]{:S(2)}, u32[]{:S(2)}) async-start(f32[16,144,128]{2,1,0:T(8,128)} %broadcast_in_dim.32), calls=%async_computation.5 | async-start | bytes 2359296 | tf_op jit(solution)/shard_map/all_to_all | solution.py:329
  124.6 0.6 add_bitcast_fusion.place_ref
  125.2 1.6 %blocks.1 = f32[81,1024]{1,0:T(8,128)} custom-call(s32[1,3]{1,0:T(1,128)} %add_bitcast_fusion.place_ref, f32[96,128]{1,0:T(8,128)S(1)} %collective-permute-done.one_ref, f32[96,128]{1,0:T(8,128)S(1)} %collective-permute-done.1.two_ref, f32[96,128]{1,0:T(8,128)S(1)} %collective-permute-done.2.three_ref, f32[96,128]{1,0:T(8,128)S(1)} %collective-permute-done.3.four_ref, ...), custom_call_target="tpu_custom_call" | custom-call | tf_op jit(solution)/shard_map/blocks/pallas_call | solution.py:282
  126.9 13.2 %all-to-all-done.5.rows_ref = f32[16,144,128]{2,1,0:T(8,128)S(1)} async-done(((f32[16,144,128]{2,1,0:T(8,128)}), f32[16,144,128]{2,1,0:T(8,128)S(1)}, u32[]{:S(2)}, u32[]{:S(2)}) %all-to-all-start.5) | async-done | bytes 1179680 | tf_op jit(solution)/shard_map/all_to_all | solution.py:329
  140.1 3.9 %collective-permute-start.5 = (f32[16,144,128]{2,1,0:T(8,128)S(1)}, f32[16,144,128]{2,1,0:T(8,128)S(1)}, u32[]{:S(2)}, u32[]{:S(2)}) collective-permute-start(f32[16,144,128]{2,1,0:T(8,128)S(1)} %all-to-all-done.5.rows_ref), channel_id=1, source_target_pairs={{0,4},{4,0},{1,5},{5,1},{2,6},{6,2},{3,7},{7,3},{8,12},{12,8},{9,1... | collective-permute-start | bytes 3538952 | tf_op jit(solution)/shard_map/ppermute | solution.py:351
  144.0 1.8 %order.2.refs_0_ = f32[9,65536]{1,0:T(8,128)} custom-call(s32[1]{0:T(128)} %bitcast.7.core_ref, f32[16,144,128]{2,1,0:T(8,128)S(1)} %all-to-all-done.5.rows_ref), custom_call_target="tpu_custom_call" | custom-call | tf_op jit(solution)/shard_map/order/pallas_call | solution.py:314
  145.8 0.6 collective-permute-done.5.rows_ref
  146.5 1.8 %order.3 = f32[9,65536]{1,0:T(8,128)} custom-call(s32[1]{0:T(128)} %bitcast.core_ref, f32[16,144,128]{2,1,0:T(8,128)S(1)} %collective-permute-done.5.rows_ref, f32[9,65536]{1,0:T(8,128)} %order.2.refs_0_), custom_call_target="tpu_custom_call", output_to_operand_aliasing={{}: (2, {})} | custom-call | tf_op jit(solution)/shard_map/order/pallas_call | solution.py:314
  (17 shorter events, 0.2 us)
Async XLA Ops:
  37.2 17.2 %copy-start = (s32[65536]{0:T(1024)S(1)}, s32[65536]{0:T(1024)}, u32[]{:S(2)}) copy-start(s32[65536]{0:T(1024)} %param.9) | copy-start | bytes 786436
  37.2 17.3 %copy-start.1 = (s32[1,64]{1,0:T(1,128)S(1)}, s32[1,64]{1,0:T(1,128)}, u32[]{:S(2)}) copy-start(s32[1,64]{1,0:T(1,128)} %counts_ref.1) | copy-start | bytes 772
  46.2 26.1 %all-to-all-start.1 = ((f32[8,128,128]{2,1,0:T(8,128)}), f32[8,128,128]{2,1,0:T(8,128)S(1)}, u32[]{:S(2)}, u32[]{:S(2)}) async-start(f32[8,128,128]{2,1,0:T(8,128)} %sums.1), calls=%async_computation.1 | async-start | bytes 1048576 | tf_op jit(solution)/shard_map/all_to_all | solution.py:329
  73.1 11.8 %all-to-all-start.2 = ((f32[16,32,128]{2,1,0:T(8,128)}), f32[16,32,128]{2,1,0:T(8,128)S(1)}, u32[]{:S(2)}, u32[]{:S(2)}) async-start(f32[16,32,128]{2,1,0:T(8,128)} %broadcast_in_dim.27), calls=%async_computation.2 | async-start | bytes 524288 | tf_op jit(solution)/shard_map/all_to_all | solution.py:329
  77.5 0.7 collective-permute-start
  87.9 15.5 %all-to-all-start.3 = ((f32[16,18,128]{2,1,0:T(8,128)}), f32[16,18,128]{2,1,0:T(8,128)S(1)}, u32[]{:S(2)}, u32[]{:S(2)}) async-start(f32[16,18,128]{2,1,0:T(8,128)} %place.1), calls=%async_computation.3 | async-start | bytes 393216 | tf_op jit(solution)/shard_map/all_to_all | solution.py:329
  95.1 8.8 %collective-permute-start.4 = (f32[16,14,128]{2,1,0:T(8,128)S(1)}, f32[16,14,128]{2,1,0:T(8,128)S(1)}, u32[]{:S(2)}, u32[]{:S(2)}) collective-permute-start(f32[16,14,128]{2,1,0:T(8,128)S(1)} %slice.11.hot_ref), channel_id=1, source_target_pairs={{0,4},{4,0},{1,5},{5,1},{2,6},{6,2},{3,7},{7,3},{8,12},{12,8},{9,1... | collective-permute-start | bytes 344072 | tf_op jit(solution)/shard_map/ppermute | solution.py:351
  95.3 8.1 %collective-permute-start.3 = (f32[96,128]{1,0:T(8,128)S(1)}, f32[96,128]{1,0:T(8,128)S(1)}, u32[]{:S(2)}, u32[]{:S(2)}) collective-permute-start(f32[96,128]{1,0:T(8,128)S(1)} %collective-permute-done.one_ref), channel_id=1, source_target_pairs={{0,3},{1,0},{2,1},{3,2},{4,7},{5,4},{6,5},{7,6},{8,11},{9,8},{10,9... | collective-permute-start | bytes 147464 | tf_op jit(solution)/shard_map/ppermute | solution.py:347
  97.6 5.8 %collective-permute-start.2 = (f32[96,128]{1,0:T(8,128)S(1)}, f32[96,128]{1,0:T(8,128)S(1)}, u32[]{:S(2)}, u32[]{:S(2)}) collective-permute-start(f32[96,128]{1,0:T(8,128)S(1)} %collective-permute-done.one_ref), channel_id=1, source_target_pairs={{0,2},{1,3},{2,0},{3,1},{4,6},{5,7},{6,4},{7,5},{8,10},{9,11},{10,... | collective-permute-start | bytes 147464 | tf_op jit(solution)/shard_map/ppermute | solution.py:347
  98.9 5.0 %collective-permute-start.1 = (f32[96,128]{1,0:T(8,128)S(1)}, f32[96,128]{1,0:T(8,128)S(1)}, u32[]{:S(2)}, u32[]{:S(2)}) collective-permute-start(f32[96,128]{1,0:T(8,128)S(1)} %collective-permute-done.one_ref), channel_id=1, source_target_pairs={{0,1},{1,2},{2,3},{3,0},{4,5},{5,6},{6,7},{7,4},{8,9},{9,10},{10,1... | collective-permute-start | bytes 147464 | tf_op jit(solution)/shard_map/ppermute | solution.py:347
  119.3 20.9 %all-to-all-start.5 = ((f32[16,144,128]{2,1,0:T(8,128)}), f32[16,144,128]{2,1,0:T(8,128)S(1)}, u32[]{:S(2)}, u32[]{:S(2)}) async-start(f32[16,144,128]{2,1,0:T(8,128)} %broadcast_in_dim.32), calls=%async_computation.5 | async-start | bytes 2359296 | tf_op jit(solution)/shard_map/all_to_all | solution.py:329
  140.1 6.3 %collective-permute-start.5 = (f32[16,144,128]{2,1,0:T(8,128)S(1)}, f32[16,144,128]{2,1,0:T(8,128)S(1)}, u32[]{:S(2)}, u32[]{:S(2)}) collective-permute-start(f32[16,144,128]{2,1,0:T(8,128)S(1)} %all-to-all-done.5.rows_ref), channel_id=1, source_target_pairs={{0,4},{4,0},{1,5},{5,1},{2,6},{6,2},{3,7},{7,3},{8,12},{12,8},{9,1... | collective-permute-start | bytes 3538952 | tf_op jit(solution)/shard_map/ppermute | solution.py:351

commit v5 on v4

v5 whole, which is shorter than its diff:
```python
import jax
import jax.numpy as jnp
from jax import lax
from jax.experimental import pallas as pl
from jax.experimental.pallas import tpu as pltpu
from jax.sharding import Mesh
from jax.sharding import PartitionSpec as P

CAM_DEV = 1024
HALF = 256
LANES = 128
SPAN = 256
QUARTERS = CAM_DEV // SPAN
CAMS = 9
PAIRS = 45
TERMS = 56
VALUES = 21
BLOCK = 28
HOT_ROWS = 7
GRAD_ROWS = 32
BLOCK_ROWS = 48
CHUNKS_PER_STEP = 4
OBS = ("zk", "zp", "y", "c")
ALL = ("zk", "zp", "y", "c", "x")
NEAR = ("zp", "y", "c", "x")
RANGE = ("zp", "y", "x")
F32 = jnp.float32
BF16 = jnp.bfloat16
VMEM = pl.BlockSpec(memory_space=pltpu.VMEM)
SMEM = pl.BlockSpec(memory_space=pltpu.SMEM)


def near(x):
    return pltpu.with_memory_space_constraint(x, pltpu.VMEM)


def two_pieces(x):
    upper = x.astype(BF16).astype(F32)
    return jnp.concatenate([upper, x - upper], axis=0).astype(BF16)


def kept_where(x, row, value):
    rows, lanes = x.shape
    kept = jnp.broadcast_to(row, (16, lanes)) == value
    kept = jnp.where(kept, 1.0, 0.0).astype(BF16)
    return (x.reshape(rows // 16, 16, lanes) * kept[None]).reshape(rows, lanes)


def one_hot(row):
    lanes = row.shape[1]
    spread = lax.broadcasted_iota(jnp.int32, (SPAN, lanes), 0) == row
    return jnp.where(spread, 1.0, 0.0).astype(BF16)


def product(left, right):
    return lax.dot_general(left, right, (((1,), (1,)), ((), ())), preferred_element_type=F32)


def set_operands(left_ref, right_ref, x, ids, parts, at):
    pieces = two_pieces(x)
    rows = pieces.shape[0]
    upper, lower = jnp.right_shift(ids, 8), jnp.bitwise_and(ids, SPAN - 1)
    for part in range(parts):
        left_ref[part * rows : (part + 1) * rows, at : at + LANES] = kept_where(pieces, upper, part)
    right_ref[:, at : at + LANES] = one_hot(lower)


def pack_body(
    counts_ref, jac_ref, res_ref, cam_ref, out_ref, kept_ref, terms_ref, left_ref, right_ref
):
    targets = out_ref.shape[0]
    capacity = jac_ref.shape[1] // 16
    step = pl.program_id(0)
    hot = jnp.int32(-1)
    for side in range(2):
        for owner in range(8):
            bucket = side * 8 + owner
            count = counts_ref[0, step * 16 + bucket]
            target = side * 32 + owner * 4 + step
            for half in range(2):
                at = bucket * capacity + half * LANES
                here = slice(at, at + LANES)
                live = lax.broadcasted_iota(jnp.int32, (1, LANES), 1) + half * LANES < count
                row = half * BLOCK
                out_ref[target, row : row + 18, :] = jnp.where(live, jac_ref[:, here], 0.0)
                out_ref[target, row + 18 : row + 20, :] = jnp.where(live, res_ref[:, here], 0.0)
                out_ref[target, row + 20 : row + 21, :] = cam_ref[:, here].astype(F32)
            hot = jnp.where(count > HALF, bucket, hot)

    @pl.when(hot >= 0)
    def _():
        count = counts_ref[0, step * 16 + hot]
        for half in range(2):
            at = pl.multiple_of(hot * capacity + HALF + half * LANES, LANES)
            here = pl.ds(at, LANES)
            live = lax.broadcasted_iota(jnp.int32, (1, LANES), 1) + HALF + half * LANES < count
            kept_ref[half, :18, :] = jnp.where(live, jac_ref[:, here], 0.0)
            kept_ref[half, 18:20, :] = jnp.where(live, res_ref[:, here], 0.0)
            kept_ref[half, 20:21, :] = cam_ref[:, here].astype(F32)

    @pl.when(step == pl.num_programs(0) - 1)
    def _():
        for half in range(2):
            kept = kept_ref[half]
            first, second = kept[:CAMS], kept[CAMS : 2 * CAMS]
            for turn in range(5):
                around = first if turn == 0 else jnp.concatenate([first[turn:], first[:turn]], axis=0)
                beside = second if turn == 0 else jnp.concatenate([second[turn:], second[:turn]], axis=0)
                terms_ref[CAMS * turn : CAMS * (turn + 1), :] = first * around + second * beside
            terms_ref[PAIRS : PAIRS + CAMS, :] = first * kept[18:19] + second * kept[19:20]
            terms_ref[PAIRS + CAMS : TERMS, :] = jnp.zeros((TERMS - PAIRS - CAMS, LANES), F32)
            ids = kept[20:21].astype(jnp.int32)
            set_operands(left_ref, right_ref, terms_ref[...], ids, QUARTERS, half * LANES)
        summed = product(left_ref[...], right_ref[...])
        for share in range(targets):
            rows, column = HOT_ROWS * (share // 8), LANES * (share % 8)
            start = 2 * TERMS * (column // SPAN) + rows
            lanes = slice(column % SPAN, column % SPAN + LANES)
            piece = (
                summed[start : start + HOT_ROWS, lanes]
                + summed[start + TERMS : start + TERMS + HOT_ROWS, lanes]
            )
            out_ref[share, VALUES : VALUES + HOT_ROWS, :] = piece


def packed(jacobians, residuals, cameras, counts, targets):
    steps = 4
    width = jacobians.shape[1] // steps
    return pl.pallas_call(
        pack_body,
        grid=(steps,),
        out_shape=pltpu.VMEM((targets, 2 * BLOCK, LANES), F32),
        in_specs=[
            SMEM,
            pl.BlockSpec((18, width), lambda i: (0, i)),
            pl.BlockSpec((2, width), lambda i: (0, i)),
            pl.BlockSpec((1, width), lambda i: (0, i)),
        ],
        out_specs=VMEM,
        scratch_shapes=[
            pltpu.VMEM((2, 24, LANES), F32),
            pltpu.VMEM((TERMS, LANES), F32),
            pltpu.VMEM((2 * TERMS * QUARTERS, 2 * LANES), BF16),
            pltpu.VMEM((SPAN, 2 * LANES), BF16),
        ],
        name="pack",
    )(counts, jacobians, residuals, cameras)


def sums_body(arrived_ref, *refs):
    out_refs, (terms_ref, left_ref, right_ref, acc_ref, hot_ref) = refs[:QUARTERS], refs[QUARTERS:]
    step = pl.program_id(0)

    @pl.when(step == 0)
    def _():
        acc_ref[...] = jnp.zeros_like(acc_ref)
        terms_ref[...] = jnp.zeros_like(terms_ref)
        hot_ref[...] = jnp.zeros_like(hot_ref)

    for chunk in range(CHUNKS_PER_STEP):
        start = chunk * 8 * BLOCK
        value = [arrived_ref[pl.ds(start + row, 8, stride=BLOCK), :] for row in range(VALUES)]
        for turn in range(5):
            for k in range(CAMS):
                other = (k + turn) % CAMS
                term = value[k] * value[other] + value[CAMS + k] * value[CAMS + other]
                terms_ref[chunk, pl.ds(CAMS * turn + k, 8, stride=TERMS), :] = term
        for k in range(CAMS):
            term = value[k] * value[18] + value[CAMS + k] * value[19]
            terms_ref[chunk, pl.ds(PAIRS + k, 8, stride=TERMS), :] = term
        ids = value[20].astype(jnp.int32)
        for group in range(8):
            x = terms_ref[chunk, group * TERMS : (group + 1) * TERMS, :]
            row = ids[group : group + 1, :]
            set_operands(left_ref.at[chunk], right_ref.at[chunk], x, row, QUARTERS, group * LANES)
        for source in range(4):
            row = start + 2 * source * BLOCK + VALUES
            hot_ref[:HOT_ROWS, :] += arrived_ref[row : row + HOT_ROWS, :]
        acc_ref[...] += product(left_ref[chunk], right_ref[chunk])

    @pl.when(step == pl.num_programs(0) - 1)
    def _():
        for turn, out_ref in enumerate(out_refs):
            part = lax.rem(lax.axis_index("zk") + turn, QUARTERS)
            upper = pl.ds(pl.multiple_of(2 * TERMS * part, 16), TERMS)
            lower = pl.ds(pl.multiple_of(2 * TERMS * part + TERMS, 8), TERMS)
            both = acc_ref[upper, :] + acc_ref[lower, :]
            for half in range(2):
                lanes = slice(half * LANES, (half + 1) * LANES)
                at = GRAD_ROWS + half * BLOCK_ROWS
                out_ref[at : at + BLOCK_ROWS, :] = both[:BLOCK_ROWS, lanes]
                out_ref[half * CAMS : (half + 1) * CAMS, :] = both[PAIRS : PAIRS + CAMS, lanes]
            out_ref[2 * CAMS : 2 * CAMS + HOT_ROWS, :] = hot_ref[:HOT_ROWS]
            rest = GRAD_ROWS - 2 * CAMS - HOT_ROWS
            out_ref[GRAD_ROWS - rest : GRAD_ROWS, :] = jnp.zeros((rest, LANES), F32)


def camera_sums(arrived):
    rows = arrived.shape[0]
    depth = 8 * LANES
    step = 8 * BLOCK * CHUNKS_PER_STEP
    out = (GRAD_ROWS + 2 * BLOCK_ROWS, LANES)
    return pl.pallas_call(
        sums_body,
        grid=(rows // step,),
        out_shape=[pltpu.VMEM(out, F32)] * QUARTERS,
        in_specs=[pl.BlockSpec((step, LANES), lambda i: (i, 0))],
        out_specs=[VMEM] * QUARTERS,
        scratch_shapes=[
            pltpu.VMEM((CHUNKS_PER_STEP, 8 * TERMS, LANES), F32),
            pltpu.VMEM((CHUNKS_PER_STEP, 2 * TERMS * QUARTERS, depth), BF16),
            pltpu.VMEM((CHUNKS_PER_STEP, SPAN, depth), BF16),
            pltpu.VMEM((2 * TERMS * QUARTERS, SPAN), F32),
            pltpu.VMEM((8, LANES), F32),
        ],
        cost_estimate=pl.CostEstimate(
            flops=2 * 2 * TERMS * CAM_DEV * 128 * rows // BLOCK, transcendentals=0, bytes_accessed=rows * 512
        ),
        name="sums",
    )(arrived)


def place_body(slots_ref, codes_ref, mine_ref, theirs_ref, left_ref, right_ref, acc_ref):
    sources = slots_ref.shape[0]
    ranges = acc_ref.shape[0] // 32
    blank = jnp.zeros((16 - CAMS, LANES), F32)

    def set_group(x, codes, chunk, group):
        x = jnp.concatenate([x, blank], axis=0)
        set_operands(left_ref.at[chunk], right_ref.at[chunk], x, codes, ranges, group * LANES)

    for chunk in range(sources // 4):
        for group in range(8):
            source, half = chunk * 4 + group // 2, group % 2
            x = slots_ref[source, half * CAMS : (half + 1) * CAMS, :]
            set_group(x, codes_ref[source, half : half + 1, :], chunk, group)
        summed = product(left_ref[chunk], right_ref[chunk])
        acc_ref[...] = summed if chunk == 0 else acc_ref[...] + summed
    split = HOT_ROWS - PAIRS % HOT_ROWS
    for group in range(4):
        source = PAIRS // HOT_ROWS * 4 + group
        x = slots_ref[source, 2 * CAMS + HOT_ROWS - split : 2 * CAMS + HOT_ROWS, :]
        rest = slots_ref[source + 4, 2 * CAMS : 3 * CAMS - split, :]
        x = jnp.concatenate([x, rest], axis=0)
        set_group(x, codes_ref[sources + group // 2, group % 2 : group % 2 + 1, :], sources // 4, group)
    depth = 4 * LANES
    acc_ref[...] += product(left_ref[sources // 4, :, :depth], right_ref[sources // 4, :, :depth])
    for flip, out_ref in enumerate((mine_ref, theirs_ref)):
        core = jnp.bitwise_xor(lax.axis_index("c"), flip)
        for part in range(QUARTERS):
            at = pl.multiple_of((core * QUARTERS + part) * 32, 32)
            both = acc_ref[pl.ds(at, CAMS), :] + acc_ref[pl.ds(at + 16, CAMS), :]
            for half in range(2):
                row = (part * 2 + half) * CAMS
                out_ref[row : row + CAMS, :] = both[:, half * LANES : (half + 1) * LANES]


def placed(slots, codes, ranges):
    depth = 8 * LANES
    chunks = slots.shape[0] // 4 + 1
    return pl.pallas_call(
        place_body,
        out_shape=[pltpu.VMEM((ranges * CAMS, LANES), F32)] * 2,
        in_specs=[VMEM, VMEM],
        out_specs=[VMEM, VMEM],
        scratch_shapes=[
            pltpu.VMEM((chunks, 32 * ranges, depth), BF16),
            pltpu.VMEM((chunks, SPAN, depth), BF16),
            pltpu.VMEM((32 * ranges, SPAN), F32),
        ],
        name="place",
    )(near(slots), near(codes))


def blocks_body(counts_ref, one_ref, two_ref, three_ref, four_ref, hot_ref, other_ref, out_ref, rows_ref):
    column, core = lax.axis_index("x"), lax.axis_index("c")
    own = jnp.where(counts_ref[0, lax.axis_index(OBS)] > HALF, 1, 0)
    for turn, share_ref in enumerate((one_ref, two_ref, three_ref, four_ref)):
        part = lax.rem(column - turn + QUARTERS, QUARTERS)
        for half in range(2):
            for group in range(TERMS // HOT_ROWS):
                start, stop = HOT_ROWS * group, min(HOT_ROWS * (group + 1), PAIRS)
                if start >= PAIRS:
                    continue
                source = group * 4 + lax.rem(part, 2) * 2 + half
                here = hot_ref[source, : stop - start, :]
                there = other_ref[source, : stop - start, :]
                hot = jnp.where(lax.div(part, 2) == core, here, there)
                share = share_ref[half * BLOCK_ROWS + start : half * BLOCK_ROWS + stop, :]
                rows_ref[start:stop, :] = share + jnp.where(own > 0, hot, 0.0)
            lanes = pl.ds(pl.multiple_of((part * 2 + half) * LANES, LANES), LANES)
            for k in range(CAMS):
                for l in range(CAMS):
                    ahead, behind = (l - k) % CAMS, (k - l) % CAMS
                    row = CAMS * ahead + k if ahead <= 4 else CAMS * behind + l
                    at = k * CAMS + l
                    out_ref[at : at + 1, lanes] = rows_ref[row : row + 1, :]


def whole_blocks(counts, shares, hot, other):
    return pl.pallas_call(
        blocks_body,
        out_shape=jax.ShapeDtypeStruct((CAMS * CAMS, CAM_DEV), F32),
        in_specs=[SMEM] + [VMEM] * 6,
        out_specs=VMEM,
        scratch_shapes=[pltpu.VMEM((BLOCK_ROWS, LANES), F32)],
        name="blocks",
    )(counts, *[near(x) for x in (*shares, hot, other)])


def order_body(core_ref, rows_ref, *refs):
    out_ref = refs[-1]
    width = SPAN * QUARTERS
    ends = out_ref.shape[1] // width
    for end in range(ends):
        source = pl.program_id(0) * ends + end
        for tile in range(width // LANES):
            at = end * width + tile * LANES
            out_ref[:, at : at + LANES] = rows_ref[source, tile * CAMS : (tile + 1) * CAMS, :]


def ordered(core, rows, before=None):
    ends, depth, lanes = rows.shape
    steps = 4
    width = ends // steps * depth // CAMS * lanes
    whole = jax.ShapeDtypeStruct((CAMS, 2 * steps * width), F32)
    in_specs = [VMEM]
    operands, aliases, flip = [core, near(rows)], {}, int(before is not None)
    if before is not None:
        in_specs.append(pl.BlockSpec(memory_space=pl.ANY))
        operands.append(before)
        aliases = {2: 0}
    return pl.pallas_call(
        order_body,
        grid_spec=pltpu.PrefetchScalarGridSpec(
            num_scalar_prefetch=1,
            grid=(steps,),
            in_specs=in_specs,
            out_specs=pl.BlockSpec((CAMS, width), lambda i, core: (0, jnp.bitwise_xor(core[0], flip) * steps + i)),
        ),
        out_shape=whole,
        input_output_aliases=aliases,
        name="order",
    )(*operands)


def exchanged(pieces, axes):
    return lax.all_to_all(pieces, axes, 0, 0, tiled=True)


def from_all(share, axes):
    count = lax.axis_size(axes)
    return exchanged(jnp.broadcast_to(share[None], (count, *share.shape)), axes)


def to_owner(share):
    pairs = [(level * 4 + column, column * 4 + level) for level in range(4) for column in range(4)]
    return lax.ppermute(share, ("zk", "x"), pairs)


def turned(share, axis, turn):
    count = lax.axis_size(axis)
    return lax.ppermute(share, axis, [(k, (k + turn) % count) for k in range(count)])


def local(jacobians, residuals, camera_local, bucket_counts, camera_map):
    targets = lax.axis_size(NEAR)
    level, core = lax.axis_index("zk"), lax.axis_index("c")
    cameras = camera_local.reshape(1, -1)
    sent = packed(jacobians, residuals, cameras, bucket_counts, targets)
    arrived = exchanged(sent, NEAR)
    camera_map, bucket_counts, arrived = lax.optimization_barrier((camera_map, bucket_counts, arrived))
    hot = jnp.argmax(bucket_counts[0])
    ids = camera_map.reshape(4, 2, 4, 2, QUARTERS, SPAN)
    ids = lax.dynamic_slice(ids, (0, 0, 0, core, level, 0), (4, 2, 4, 1, 1, SPAN))
    ids = ids.reshape(4, 8, SPAN).transpose(1, 0, 2).reshape(-1, 2, LANES)
    hot_ids = lax.dynamic_slice_in_dim(camera_map, hot * CAM_DEV + core * 4 * LANES, 4 * LANES)
    hot_ids = jnp.where(level == 0, hot_ids, -1).reshape(-1, 2, LANES)
    ids = jnp.concatenate([ids, hot_ids], axis=0)
    here = jnp.bitwise_and(jnp.right_shift(ids, 10), 31) == lax.axis_index(RANGE)
    codes = jnp.right_shift(ids, 15) * QUARTERS * SPAN + jnp.bitwise_and(ids, QUARTERS * SPAN - 1)
    codes = jnp.where(here & (ids >= 0), codes, -SPAN)
    sums = camera_sums(arrived.reshape(-1, LANES))
    share = sums[0]
    for turn in range(1, QUARTERS):
        share = share + turned(sums[turn], "zk", turn)
    squares = to_owner(share[GRAD_ROWS:])
    slots = from_all(share[:GRAD_ROWS], RANGE)
    slots, squares = lax.optimization_barrier((slots, squares))
    shares = [squares] + [turned(squares, "x", turn) for turn in range(1, QUARTERS)]
    mine, theirs = placed(slots, codes, 2 * QUARTERS)
    own_hot = slots[:, 2 * CAMS : 2 * CAMS + HOT_ROWS]
    other_hot = turned(own_hot, "c", 1)
    mine = mine + turned(theirs, "c", 1)
    part = mine
    for turn in range(1, QUARTERS):
        part = part + turned(mine, "zk", turn)
    part, shares, other_hot = lax.optimization_barrier((part, shares, other_hot))
    blocks = whole_blocks(bucket_counts, shares, own_hot, other_hot)
    part = from_all(part, RANGE)
    part, blocks = lax.optimization_barrier((part, blocks))
    other = turned(part, "c", 1)
    core = core.reshape(1)
    gradient = ordered(core, part)
    gradient = ordered(core, other, gradient)
    return gradient, blocks


def solution(mesh):
    split = Mesh(mesh.devices.reshape(4, 2, 4, 2, mesh.shape["rep"]), ALL)
    return jax.shard_map(
        local,
        mesh=split,
        in_specs=(P(None, ALL), P(None, ALL), P(ALL), P(ALL, None), P()),
        out_specs=(P(), P(None, OBS)),
        check_vma=False,
    )
```

time: 149 us -> 133 us (0.89)
  waiting for transfers between devices: 41.8 us -> 29.4 us
  blocking collectives: 46.8 us -> 35.5 us
  starting transfers between devices: 32.8 us -> 42.2 us
    ppermute x6 -> x13, starting transfers between devices: 9.15 us -> 31.3 us  [the longest x12 30.7 us: turned(): lax.ppermute(share, axis, [(k, (k + turn) % count) for k in range(count)])]
    all_to_all x4 -> x2, waiting for transfers between devices: 40.7 us -> 20.4 us  [exchanged(): return lax.all_to_all(pieces, axes, 0, 0, tiled=True)]
    all_to_all x4 -> x2, starting transfers between devices: 23.6 us -> 10.8 us  [exchanged(): return lax.all_to_all(pieces, axes, 0, 0, tiled=True)]
    all_to_all x2 -> x1, blocking collectives: 46.8 us -> 35.5 us  [exchanged(): return lax.all_to_all(pieces, axes, 0, 0, tiled=True)]
    ppermute x6 -> x13, waiting for transfers between devices: 1.13 us -> 9.05 us  [the longest x12 9.05 us: turned(): lax.ppermute(share, axis, [(k, (k + turn) % count) for k in range(count)])]
  transfers between devices with their start and end apart: 10 -> 15, of which waited for: 6 -> 8; matrix products, arithmetic and copies ran while one was open for 1% -> 1% of each run, Pallas kernels for 2% -> 3%
where the time goes in v5:
time: 133 us; the launch traced here: 132 us
  starting transfers between devices  42.2 us (32%)
  blocking collectives  35.5 us (27%)
  waiting for transfers between devices  29.4 us (22%)
  Pallas kernels  20.7 us (16%)
  local copies, waits for them, and re-layouts  2.2 us (2%)
  between operations  1.45 us (1%)
    all_to_all x1, blocking collectives, exchanged(): return lax.all_to_all(pieces, axes, 0, 0, tiled=True)  35.5 us
    ppermute x12, starting transfers between devices, turned(): lax.ppermute(share, axis, [(k, (k + turn) % count) for k in range(count)])  30.7 us
    all_to_all x2, waiting for transfers between devices, exchanged(): return lax.all_to_all(pieces, axes, 0, 0, tiled=True)  20.4 us
    all_to_all x2, starting transfers between devices, exchanged(): return lax.all_to_all(pieces, axes, 0, 0, tiled=True)  10.8 us
    pallas_call x1, Pallas kernels, camera_sums(): pl.pallas_call(sums_body, grid=(rows // step,), out_shape=[pltpu.VMEM(out...  9.36 us
    ppermute x12, waiting for transfers between devices, turned(): lax.ppermute(share, axis, [(k, (k + turn) % count) for k in range(count)])  9.05 us
    pallas_call x2, Pallas kernels, ordered(): pl.pallas_call(order_body, grid_spec=pltpu.PrefetchScalarGridSpec(num_sca...  3.65 us
    pallas_call x1, Pallas kernels, packed(): pl.pallas_call(pack_body, grid=(steps,), out_shape=pltpu.VMEM((targets, 2...  3.15 us
  transfers between devices with their start and end apart: 15, of which 8 were waited for; matrix products, arithmetic and copies ran while one was open for 1% of the time, Pallas kernels for 3%

profile of v5, /device:TPU:1, one launch (start us, length us, event | category | flops | bytes accessed | tf_op | source)
XLA Modules:
  0.0 132.4 jit_solution(14522830192282409439)
XLA Ops:
  0.6 3.2 %pack.1 = f32[64,56,128]{2,1,0:T(8,128)S(1)} custom-call(s32[1,64]{1,0:T(1,128)} %counts_ref.2, f32[18,32768]{1,0:T(8,128)} %jac_ref.1, f32[2,32768]{1,0:T(2,128)} %res_ref.1, s32[1,32768]{1,0:T(1,128)} %bitcast.10), custom_call_target="tpu_custom_call" | custom-call | tf_op jit(solution)/shard_map/pack/pallas_call | solution.py:129
  3.8 35.5 %all_to_all.15 = f32[64,56,128]{2,1,0:T(8,128)} all-to-all(f32[64,56,128]{2,1,0:T(8,128)S(1)} %pack.1), channel_id=1, replica_groups=mesh['zk'=4,'zp'=2,'y'=4,'c'=2,'x'=4] {'zp','y','c','x'}, dimensions={0} | all-to-all | bytes 3670016 | tf_op jit(solution)/shard_map/all_to_all | solution.py:348
  39.3 9.4 %sums.1 = (f32[128,128]{1,0:T(8,128)S(1)}, f32[128,128]{1,0:T(8,128)S(1)}, f32[128,128]{1,0:T(8,128)S(1)}, f32[128,128]{1,0:T(8,128)S(1)}) custom-call(f32[3584,128]{1,0:T(8,128)} %bitcast.9), custom_call_target="tpu_custom_call" | custom-call | flops 3758096384 | bytes 1835008 | tf_op jit(solution)/shard_map/sums/pallas_call | solution.py:203
  48.7 3.1 %collective-permute-start = (f32[128,128]{1,0:T(8,128)S(1)}, f32[128,128]{1,0:T(8,128)S(1)}, u32[]{:S(2)}, u32[]{:S(2)}) collective-permute-start(f32[128,128]{1,0:T(8,128)S(1)} %get-tuple-element.24), channel_id=1, source_target_pairs={{0,64},{64,128},{128,192},{192,0},{1,65},{65,129},{129,193},{193,1... | collective-permute-start | bytes 196616 | tf_op jit(solution)/shard_map/ppermute | solution.py:363
  51.7 4.2 %collective-permute-start.1 = (f32[128,128]{1,0:T(8,128)S(1)}, f32[128,128]{1,0:T(8,128)S(1)}, u32[]{:S(2)}, u32[]{:S(2)}) collective-permute-start(f32[128,128]{1,0:T(8,128)S(1)} %get-tuple-element.25), channel_id=1, source_target_pairs={{0,128},{64,192},{128,0},{192,64},{1,129},{65,193},{129,1},{193,65... | collective-permute-start | bytes 196616 | tf_op jit(solution)/shard_map/ppermute | solution.py:363
  55.9 2.4 %collective-permute-start.2 = (f32[128,128]{1,0:T(8,128)S(1)}, f32[128,128]{1,0:T(8,128)S(1)}, u32[]{:S(2)}, u32[]{:S(2)}) collective-permute-start(f32[128,128]{1,0:T(8,128)S(1)} %get-tuple-element.26), channel_id=1, source_target_pairs={{0,192},{64,0},{128,64},{192,128},{1,193},{65,1},{129,65},{193,129... | collective-permute-start | bytes 196616 | tf_op jit(solution)/shard_map/ppermute | solution.py:363
  58.3 0.4 collective-permute-done.1
  58.8 4.8 %collective-permute-done.2 = f32[128,128]{1,0:T(8,128)S(1)} collective-permute-done((f32[128,128]{1,0:T(8,128)S(1)}, f32[128,128]{1,0:T(8,128)S(1)}, u32[]{:S(2)}, u32[]{:S(2)}) %collective-permute-start.2) | collective-permute-done | bytes 65568 | tf_op jit(solution)/shard_map/ppermute | solution.py:363
  63.6 0.9 broadcast_in_dim.20
  64.4 4.1 %all-to-all-start.1 = ((f32[32,32,128]{2,1,0:T(8,128)}), f32[32,32,128]{2,1,0:T(8,128)S(1)}, u32[]{:S(2)}, u32[]{:S(2)}) async-start(f32[32,32,128]{2,1,0:T(8,128)} %broadcast_in_dim.20), calls=%async_computation.1 | async-start | bytes 1048576 | tf_op jit(solution)/shard_map/all_to_all | solution.py:348
  68.5 0.7 bitcast_reduce_fusion
  70.2 0.7 collective-permute-start.3
  70.9 7.2 %all-to-all-done.1.slots_ref = f32[32,32,128]{2,1,0:T(8,128)S(1)} async-done(((f32[32,32,128]{2,1,0:T(8,128)}), f32[32,32,128]{2,1,0:T(8,128)S(1)}, u32[]{:S(2)}, u32[]{:S(2)}) %all-to-all-start.1) | async-done | bytes 524320 | tf_op jit(solution)/shard_map/all_to_all | solution.py:348
  78.1 2.9 %place.1 = (f32[72,128]{1,0:T(8,128)S(1)}, f32[72,128]{1,0:T(8,128)S(1)}) custom-call(f32[32,32,128]{2,1,0:T(8,128)S(1)} %all-to-all-done.1.slots_ref, s32[34,2,128]{2,1,0:T(2,128)S(1)} %and_select_fusion.codes_ref), custom_call_target="tpu_custom_call" | custom-call | tf_op jit(solution)/shard_map/place/pallas_call | solution.py:261
  81.0 3.0 %collective-permute-start.4 = (f32[72,128]{1,0:T(8,128)S(1)}, f32[72,128]{1,0:T(8,128)S(1)}, u32[]{:S(2)}, u32[]{:S(2)}) collective-permute-start(f32[72,128]{1,0:T(8,128)S(1)} %get-tuple-element.32), channel_id=1, source_target_pairs={{0,4},{4,0},{1,5},{5,1},{2,6},{6,2},{3,7},{7,3},{8,12},{12,8},{9,1... | collective-permute-start | bytes 110600 | tf_op jit(solution)/shard_map/ppermute | solution.py:363
  84.0 0.9 collective-permute-done.4
  84.9 3.8 %collective-permute-start.7 = (f32[72,128]{1,0:T(8,128)S(1)}, f32[72,128]{1,0:T(8,128)S(1)}, u32[]{:S(2)}, u32[]{:S(2)}) collective-permute-start(f32[72,128]{1,0:T(8,128)S(1)} %add.52), channel_id=1, source_target_pairs={{0,192},{64,0},{128,64},{192,128},{1,193},{65,1},{129,65},{193,129... | collective-permute-start | bytes 110600 | tf_op jit(solution)/shard_map/ppermute | solution.py:363
  88.7 3.0 %collective-permute-start.6 = (f32[72,128]{1,0:T(8,128)S(1)}, f32[72,128]{1,0:T(8,128)S(1)}, u32[]{:S(2)}, u32[]{:S(2)}) collective-permute-start(f32[72,128]{1,0:T(8,128)S(1)} %add.52), channel_id=1, source_target_pairs={{0,128},{64,192},{128,0},{192,64},{1,129},{65,193},{129,1},{193,65... | collective-permute-start | bytes 110600 | tf_op jit(solution)/shard_map/ppermute | solution.py:363
  91.7 2.3 %collective-permute-start.5 = (f32[72,128]{1,0:T(8,128)S(1)}, f32[72,128]{1,0:T(8,128)S(1)}, u32[]{:S(2)}, u32[]{:S(2)}) collective-permute-start(f32[72,128]{1,0:T(8,128)S(1)} %add.52), channel_id=1, source_target_pairs={{0,64},{64,128},{128,192},{192,0},{1,65},{65,129},{129,193},{193,1... | collective-permute-start | bytes 110600 | tf_op jit(solution)/shard_map/ppermute | solution.py:363
  94.0 2.5 %collective-permute-start.10 = (f32[96,128]{1,0:T(8,128)S(1)}, f32[96,128]{1,0:T(8,128)S(1)}, u32[]{:S(2)}, u32[]{:S(2)}) collective-permute-start(f32[96,128]{1,0:T(8,128)S(1)} %collective-permute-done.3.one_ref), channel_id=1, source_target_pairs={{0,3},{1,0},{2,1},{3,2},{4,7},{5,4},{6,5},{7,6},{8,11},{9,8},{10,9... | collective-permute-start | bytes 147464 | tf_op jit(solution)/shard_map/ppermute | solution.py:363
  96.4 0.9 collective-permute-start.8
  97.3 1.5 %collective-permute-start.11 = (f32[32,7,128]{2,1,0:T(8,128)S(1)}, f32[32,7,128]{2,1,0:T(8,128)S(1)}, u32[]{:S(2)}, u32[]{:S(2)}) collective-permute-start(f32[32,7,128]{2,1,0:T(8,128)S(1)} %slice.11.hot_ref), channel_id=1, source_target_pairs={{0,4},{4,0},{1,5},{5,1},{2,6},{6,2},{3,7},{7,3},{8,12},{12,8},{9,1... | collective-permute-start | bytes 344072 | tf_op jit(solution)/shard_map/ppermute | solution.py:363
  98.8 2.2 %collective-permute-done.9.three_ref = f32[96,128]{1,0:T(8,128)S(1)} collective-permute-done((f32[96,128]{1,0:T(8,128)S(1)}, f32[96,128]{1,0:T(8,128)S(1)}, u32[]{:S(2)}, u32[]{:S(2)}) %collective-permute-start.9) | collective-permute-done | bytes 49184 | tf_op jit(solution)/shard_map/ppermute | solution.py:363
  101.0 0.1 collective-permute-done.8.two_ref
  101.1 1.1 broadcast_in_dim.23
  102.2 6.8 %all-to-all-start.2 = ((f32[32,72,128]{2,1,0:T(8,128)}), f32[32,72,128]{2,1,0:T(8,128)S(1)}, u32[]{:S(2)}, u32[]{:S(2)}) async-start(f32[32,72,128]{2,1,0:T(8,128)} %broadcast_in_dim.23), calls=%async_computation.2 | async-start | bytes 2359296 | tf_op jit(solution)/shard_map/all_to_all | solution.py:348
  109.0 1.7 %blocks.1 = f32[81,1024]{1,0:T(8,128)} custom-call(s32[1,64]{1,0:T(1,128)} %counts_ref.2, f32[96,128]{1,0:T(8,128)S(1)} %collective-permute-done.3.one_ref, f32[96,128]{1,0:T(8,128)S(1)} %collective-permute-done.8.two_ref, f32[96,128]{1,0:T(8,128)S(1)} %collective-permute-done.9.three_ref, f32[96,128]{1,0:T(8,128)S(1)} %collective-permute-done.10.four_ref, ...), custom_call_target="tpu_custom_call" | custom-call | tf_op jit(solution)/shard_map/blocks/pallas_call | solution.py:301
  110.7 13.2 %all-to-all-done.2.rows_ref = f32[32,72,128]{2,1,0:T(8,128)S(1)} async-done(((f32[32,72,128]{2,1,0:T(8,128)}), f32[32,72,128]{2,1,0:T(8,128)S(1)}, u32[]{:S(2)}, u32[]{:S(2)}) %all-to-all-start.2) | async-done | bytes 1179680 | tf_op jit(solution)/shard_map/all_to_all | solution.py:348
  123.9 4.1 %collective-permute-start.12 = (f32[32,72,128]{2,1,0:T(8,128)S(1)}, f32[32,72,128]{2,1,0:T(8,128)S(1)}, u32[]{:S(2)}, u32[]{:S(2)}) collective-permute-start(f32[32,72,128]{2,1,0:T(8,128)S(1)} %all-to-all-done.2.rows_ref), channel_id=1, source_target_pairs={{0,4},{4,0},{1,5},{5,1},{2,6},{6,2},{3,7},{7,3},{8,12},{12,8},{9,1... | collective-permute-start | bytes 3538952 | tf_op jit(solution)/shard_map/ppermute | solution.py:363
  128.1 1.8 %order.2.refs_0_ = f32[9,65536]{1,0:T(8,128)} custom-call(s32[1]{0:T(128)} %bitcast.core_ref, f32[32,72,128]{2,1,0:T(8,128)S(1)} %all-to-all-done.2.rows_ref), custom_call_target="tpu_custom_call" | custom-call | tf_op jit(solution)/shard_map/order/pallas_call | solution.py:333
  129.9 0.6 collective-permute-done.12.rows_ref
  130.5 1.8 %order.3 = f32[9,65536]{1,0:T(8,128)} custom-call(s32[1]{0:T(128)} %bitcast.core_ref, f32[32,72,128]{2,1,0:T(8,128)S(1)} %collective-permute-done.12.rows_ref, f32[9,65536]{1,0:T(8,128)} %order.2.refs_0_), custom_call_target="tpu_custom_call", output_to_operand_aliasing={{}: (2, {})} | custom-call | tf_op jit(solution)/shard_map/order/pallas_call | solution.py:333
  (24 shorter events, 0.4 us)
Async XLA Ops:
  48.6 19.8 %copy-start.1 = (s32[1,64]{1,0:T(1,128)S(1)}, s32[1,64]{1,0:T(1,128)}, u32[]{:S(2)}) copy-start(s32[1,64]{1,0:T(1,128)} %counts_ref.2) | copy-start | bytes 772
  48.6 21.2 %copy-start = (s32[65536]{0:T(1024)S(1)}, s32[65536]{0:T(1024)}, u32[]{:S(2)}) copy-start(s32[65536]{0:T(1024)} %param.9) | copy-start | bytes 786436
  48.7 9.7 %collective-permute-start = (f32[128,128]{1,0:T(8,128)S(1)}, f32[128,128]{1,0:T(8,128)S(1)}, u32[]{:S(2)}, u32[]{:S(2)}) collective-permute-start(f32[128,128]{1,0:T(8,128)S(1)} %get-tuple-element.24), channel_id=1, source_target_pairs={{0,64},{64,128},{128,192},{192,0},{1,65},{65,129},{129,193},{193,1... | collective-permute-start | bytes 196616 | tf_op jit(solution)/shard_map/ppermute | solution.py:363
  51.7 7.0 %collective-permute-start.1 = (f32[128,128]{1,0:T(8,128)S(1)}, f32[128,128]{1,0:T(8,128)S(1)}, u32[]{:S(2)}, u32[]{:S(2)}) collective-permute-start(f32[128,128]{1,0:T(8,128)S(1)} %get-tuple-element.25), channel_id=1, source_target_pairs={{0,128},{64,192},{128,0},{192,64},{1,129},{65,193},{129,1},{193,65... | collective-permute-start | bytes 196616 | tf_op jit(solution)/shard_map/ppermute | solution.py:363
  55.9 7.6 %collective-permute-start.2 = (f32[128,128]{1,0:T(8,128)S(1)}, f32[128,128]{1,0:T(8,128)S(1)}, u32[]{:S(2)}, u32[]{:S(2)}) collective-permute-start(f32[128,128]{1,0:T(8,128)S(1)} %get-tuple-element.26), channel_id=1, source_target_pairs={{0,192},{64,0},{128,64},{192,128},{1,193},{65,1},{129,65},{193,129... | collective-permute-start | bytes 196616 | tf_op jit(solution)/shard_map/ppermute | solution.py:363
  64.4 13.7 %all-to-all-start.1 = ((f32[32,32,128]{2,1,0:T(8,128)}), f32[32,32,128]{2,1,0:T(8,128)S(1)}, u32[]{:S(2)}, u32[]{:S(2)}) async-start(f32[32,32,128]{2,1,0:T(8,128)} %broadcast_in_dim.20), calls=%async_computation.1 | async-start | bytes 1048576 | tf_op jit(solution)/shard_map/all_to_all | solution.py:348
  70.2 0.7 collective-permute-start.3
  81.0 3.9 %collective-permute-start.4 = (f32[72,128]{1,0:T(8,128)S(1)}, f32[72,128]{1,0:T(8,128)S(1)}, u32[]{:S(2)}, u32[]{:S(2)}) collective-permute-start(f32[72,128]{1,0:T(8,128)S(1)} %get-tuple-element.32), channel_id=1, source_target_pairs={{0,4},{4,0},{1,5},{5,1},{2,6},{6,2},{3,7},{7,3},{8,12},{12,8},{9,1... | collective-permute-start | bytes 110600 | tf_op jit(solution)/shard_map/ppermute | solution.py:363
  84.9 11.6 %collective-permute-start.7 = (f32[72,128]{1,0:T(8,128)S(1)}, f32[72,128]{1,0:T(8,128)S(1)}, u32[]{:S(2)}, u32[]{:S(2)}) collective-permute-start(f32[72,128]{1,0:T(8,128)S(1)} %add.52), channel_id=1, source_target_pairs={{0,192},{64,0},{128,64},{192,128},{1,193},{65,1},{129,65},{193,129... | collective-permute-start | bytes 110600 | tf_op jit(solution)/shard_map/ppermute | solution.py:363
  88.7 8.6 %collective-permute-start.6 = (f32[72,128]{1,0:T(8,128)S(1)}, f32[72,128]{1,0:T(8,128)S(1)}, u32[]{:S(2)}, u32[]{:S(2)}) collective-permute-start(f32[72,128]{1,0:T(8,128)S(1)} %add.52), channel_id=1, source_target_pairs={{0,128},{64,192},{128,0},{192,64},{1,129},{65,193},{129,1},{193,65... | collective-permute-start | bytes 110600 | tf_op jit(solution)/shard_map/ppermute | solution.py:363
  91.7 7.1 %collective-permute-start.5 = (f32[72,128]{1,0:T(8,128)S(1)}, f32[72,128]{1,0:T(8,128)S(1)}, u32[]{:S(2)}, u32[]{:S(2)}) collective-permute-start(f32[72,128]{1,0:T(8,128)S(1)} %add.52), channel_id=1, source_target_pairs={{0,64},{64,128},{128,192},{192,0},{1,65},{65,129},{129,193},{193,1... | collective-permute-start | bytes 110600 | tf_op jit(solution)/shard_map/ppermute | solution.py:363
  94.0 4.8 %collective-permute-start.10 = (f32[96,128]{1,0:T(8,128)S(1)}, f32[96,128]{1,0:T(8,128)S(1)}, u32[]{:S(2)}, u32[]{:S(2)}) collective-permute-start(f32[96,128]{1,0:T(8,128)S(1)} %collective-permute-done.3.one_ref), channel_id=1, source_target_pairs={{0,3},{1,0},{2,1},{3,2},{4,7},{5,4},{6,5},{7,6},{8,11},{9,8},{10,9... | collective-permute-start | bytes 147464 | tf_op jit(solution)/shard_map/ppermute | solution.py:363
  96.4 4.5 %collective-permute-start.9 = (f32[96,128]{1,0:T(8,128)S(1)}, f32[96,128]{1,0:T(8,128)S(1)}, u32[]{:S(2)}, u32[]{:S(2)}) collective-permute-start(f32[96,128]{1,0:T(8,128)S(1)} %collective-permute-done.3.one_ref), channel_id=1, source_target_pairs={{0,2},{1,3},{2,0},{3,1},{4,6},{5,7},{6,4},{7,5},{8,10},{9,11},{10,... | collective-permute-start | bytes 147464 | tf_op jit(solution)/shard_map/ppermute | solution.py:363
  96.4 4.7 %collective-permute-start.8 = (f32[96,128]{1,0:T(8,128)S(1)}, f32[96,128]{1,0:T(8,128)S(1)}, u32[]{:S(2)}, u32[]{:S(2)}) collective-permute-start(f32[96,128]{1,0:T(8,128)S(1)} %collective-permute-done.3.one_ref), channel_id=1, source_target_pairs={{0,1},{1,2},{2,3},{3,0},{4,5},{5,6},{6,7},{7,4},{8,9},{9,10},{10,1... | collective-permute-start | bytes 147464 | tf_op jit(solution)/shard_map/ppermute | solution.py:363
  97.3 3.8 %collective-permute-start.11 = (f32[32,7,128]{2,1,0:T(8,128)S(1)}, f32[32,7,128]{2,1,0:T(8,128)S(1)}, u32[]{:S(2)}, u32[]{:S(2)}) collective-permute-start(f32[32,7,128]{2,1,0:T(8,128)S(1)} %slice.11.hot_ref), channel_id=1, source_target_pairs={{0,4},{4,0},{1,5},{5,1},{2,6},{6,2},{3,7},{7,3},{8,12},{12,8},{9,1... | collective-permute-start | bytes 344072 | tf_op jit(solution)/shard_map/ppermute | solution.py:363
  102.2 21.7 %all-to-all-start.2 = ((f32[32,72,128]{2,1,0:T(8,128)}), f32[32,72,128]{2,1,0:T(8,128)S(1)}, u32[]{:S(2)}, u32[]{:S(2)}) async-start(f32[32,72,128]{2,1,0:T(8,128)} %broadcast_in_dim.23), calls=%async_computation.2 | async-start | bytes 2359296 | tf_op jit(solution)/shard_map/all_to_all | solution.py:348
  123.9 6.6 %collective-permute-start.12 = (f32[32,72,128]{2,1,0:T(8,128)S(1)}, f32[32,72,128]{2,1,0:T(8,128)S(1)}, u32[]{:S(2)}, u32[]{:S(2)}) collective-permute-start(f32[32,72,128]{2,1,0:T(8,128)S(1)} %all-to-all-done.2.rows_ref), channel_id=1, source_target_pairs={{0,4},{4,0},{1,5},{5,1},{2,6},{6,2},{3,7},{7,3},{8,12},{12,8},{9,1... | collective-permute-start | bytes 3538952 | tf_op jit(solution)/shard_map/ppermute | solution.py:363

commit v6 on v5

--- a/solution.py
+++ b/solution.py
@@ -15,8 +15,9 @@
 PAIRS = 45
 TERMS = 56
 VALUES = 21
-BLOCK = 28
+BLOCK = 26
 HOT_ROWS = 7
+HOT_FIRST = 5
 GRAD_ROWS = 32
 BLOCK_ROWS = 48
 CHUNKS_PER_STEP = 4
@@ -68,24 +69,30 @@
 def pack_body(
     counts_ref, jac_ref, res_ref, cam_ref, out_ref, kept_ref, terms_ref, left_ref, right_ref
 ):
-    targets = out_ref.shape[0]
+    targets = out_ref.shape[0] // (2 * BLOCK)
     capacity = jac_ref.shape[1] // 16
     step = pl.program_id(0)
+    for level in range(4):
+
+        @pl.when(step == level)
+        def _():
+            for side in range(2):
+                for owner in range(8):
+                    bucket = side * 8 + owner
+                    count = counts_ref[0, level * 16 + bucket]
+                    target = side * 32 + owner * 4 + level
+                    for half in range(2):
+                        at = bucket * capacity + half * LANES
+                        here = slice(at, at + LANES)
+                        live = lax.broadcasted_iota(jnp.int32, (1, LANES), 1) + half * LANES < count
+                        row = (2 * target + half) * BLOCK
+                        out_ref[row : row + 18, :] = jnp.where(live, jac_ref[:, here], 0.0)
+                        out_ref[row + 18 : row + 20, :] = jnp.where(live, res_ref[:, here], 0.0)
+                        out_ref[row + 20 : row + 21, :] = cam_ref[:, here].astype(F32)
+
     hot = jnp.int32(-1)
-    for side in range(2):
-        for owner in range(8):
-            bucket = side * 8 + owner
-            count = counts_ref[0, step * 16 + bucket]
-            target = side * 32 + owner * 4 + step
-            for half in range(2):
-                at = bucket * capacity + half * LANES
-                here = slice(at, at + LANES)
-                live = lax.broadcasted_iota(jnp.int32, (1, LANES), 1) + half * LANES < count
-                row = half * BLOCK
-                out_ref[target, row : row + 18, :] = jnp.where(live, jac_ref[:, here], 0.0)
-                out_ref[target, row + 18 : row + 20, :] = jnp.where(live, res_ref[:, here], 0.0)
-                out_ref[target, row + 20 : row + 21, :] = cam_ref[:, here].astype(F32)
-            hot = jnp.where(count > HALF, bucket, hot)
+    for bucket in range(16):
+        hot = jnp.where(counts_ref[0, step * 16 + bucket] > HALF, bucket, hot)
 
     @pl.when(hot >= 0)
     def _():
@@ -120,7 +127,10 @@
                 summed[start : start + HOT_ROWS, lanes]
                 + summed[start + TERMS : start + TERMS + HOT_ROWS, lanes]
             )
-            out_ref[share, VALUES : VALUES + HOT_ROWS, :] = piece
+            row = 2 * share * BLOCK + VALUES
+            out_ref[row : row + HOT_FIRST, :] = piece[:HOT_FIRST]
+            row += BLOCK
+            out_ref[row : row + HOT_ROWS - HOT_FIRST, :] = piece[HOT_FIRST:]
 
 
 def packed(jacobians, residuals, cameras, counts, targets):
@@ -129,7 +139,7 @@
     return pl.pallas_call(
         pack_body,
         grid=(steps,),
-        out_shape=pltpu.VMEM((targets, 2 * BLOCK, LANES), F32),
+        out_shape=pltpu.VMEM((targets * 2 * BLOCK, LANES), F32),
         in_specs=[
             SMEM,
             pl.BlockSpec((18, width), lambda i: (0, i)),
@@ -175,7 +185,10 @@
             set_operands(left_ref.at[chunk], right_ref.at[chunk], x, row, QUARTERS, group * LANES)
         for source in range(4):
             row = start + 2 * source * BLOCK + VALUES
-            hot_ref[:HOT_ROWS, :] += arrived_ref[row : row + HOT_ROWS, :]
+            hot_ref[:HOT_FIRST, :] += arrived_ref[row : row + HOT_FIRST, :]
+            row += BLOCK
+            rest = HOT_ROWS - HOT_FIRST
+            hot_ref[HOT_FIRST:HOT_ROWS, :] += arrived_ref[row : row + rest, :]
         acc_ref[...] += product(left_ref[chunk], right_ref[chunk])
 
     @pl.when(step == pl.num_programs(0) - 1)
@@ -368,7 +381,7 @@
     level, core = lax.axis_index("zk"), lax.axis_index("c")
     cameras = camera_local.reshape(1, -1)
     sent = packed(jacobians, residuals, cameras, bucket_counts, targets)
-    arrived = exchanged(sent, NEAR)
+    arrived = exchanged(sent.reshape(targets, -1, 4, LANES), NEAR).reshape(-1, LANES)
     camera_map, bucket_counts, arrived = lax.optimization_barrier((camera_map, bucket_counts, arrived))
     hot = jnp.argmax(bucket_counts[0])
     ids = camera_map.reshape(4, 2, 4, 2, QUARTERS, SPAN)
@@ -380,7 +393,7 @@
     here = jnp.bitwise_and(jnp.right_shift(ids, 10), 31) == lax.axis_index(RANGE)
     codes = jnp.right_shift(ids, 15) * QUARTERS * SPAN + jnp.bitwise_and(ids, QUARTERS * SPAN - 1)
     codes = jnp.where(here & (ids >= 0), codes, -SPAN)
-    sums = camera_sums(arrived.reshape(-1, LANES))
+    sums = camera_sums(arrived)
     share = sums[0]
     for turn in range(1, QUARTERS):
         share = share + turned(sums[turn], "zk", turn)

time: 133 us -> 131 us (0.985)
    all_to_all x2, starting transfers between devices: 10.8 us -> 12.3 us  [exchanged(): return lax.all_to_all(pieces, axes, 0, 0, tiled=True)]
where the time goes in v6:
time: 131 us
  starting transfers between devices  43.3 us (33%)
  blocking collectives  34.2 us (26%)
  waiting for transfers between devices  28.2 us (22%)
  Pallas kernels  20.9 us (16%)
  local copies, waits for them, and re-layouts  2.2 us (2%)
  between operations  1.45 us (1%)
    all_to_all x1, blocking collectives, exchanged(): return lax.all_to_all(pieces, axes, 0, 0, tiled=True)  34.2 us
    ppermute x12, starting transfers between devices, turned(): lax.ppermute(share, axis, [(k, (k + turn) % count) for k in range(count)])  30.3 us
    all_to_all x2, waiting for transfers between devices, exchanged(): return lax.all_to_all(pieces, axes, 0, 0, tiled=True)  20.5 us
    all_to_all x2, starting transfers between devices, exchanged(): return lax.all_to_all(pieces, axes, 0, 0, tiled=True)  12.3 us
    pallas_call x1, Pallas kernels, camera_sums(): pl.pallas_call(sums_body, grid=(rows // step,), out_shape=[pltpu.VMEM(out...  9.41 us
    ppermute x12, waiting for transfers between devices, turned(): lax.ppermute(share, axis, [(k, (k + turn) % count) for k in range(count)])  7.72 us
    pallas_call x2, Pallas kernels, ordered(): pl.pallas_call(order_body, grid_spec=pltpu.PrefetchScalarGridSpec(num_sca...  3.65 us
    pallas_call x1, Pallas kernels, packed(): pl.pallas_call(pack_body, grid=(steps,), out_shape=pltpu.VMEM((targets *...  3.21 us
  transfers between devices with their start and end apart: 15, of which 8 were waited for; matrix products, arithmetic and copies ran while one was open for 1% of the time, Pallas kernels for 3%

profile of v6, /device:TPU:1, one launch (start us, length us, event | category | flops | bytes accessed | tf_op | source)
XLA Modules:
  0.0 131.1 jit_solution(11935590526749892812)
XLA Ops:
  0.6 3.2 %pack.1 = f32[3328,128]{1,0:T(8,128)S(1)} custom-call(s32[1,64]{1,0:T(1,128)} %counts_ref.2, f32[18,32768]{1,0:T(8,128)} %jac_ref.1, f32[2,32768]{1,0:T(2,128)} %res_ref.1, s32[1,32768]{1,0:T(1,128)} %bitcast.12), custom_call_target="tpu_custom_call" | custom-call | tf_op jit(solution)/shard_map/pack/pallas_call | solution.py:139
  3.9 34.2 %all_to_all.15 = f32[64,13,4,128]{3,2,1,0:T(4,128)} all-to-all(f32[64,13,4,128]{3,2,1,0:T(4,128)S(1)} %bitcast.10), channel_id=1, replica_groups=mesh['zk'=4,'zp'=2,'y'=4,'c'=2,'x'=4] {'zp','y','c','x'}, dimensions={0} | all-to-all | bytes 3407872 | tf_op jit(solution)/shard_map/all_to_all | solution.py:361
  38.0 9.4 %sums.1 = (f32[128,128]{1,0:T(8,128)S(1)}, f32[128,128]{1,0:T(8,128)S(1)}, f32[128,128]{1,0:T(8,128)S(1)}, f32[128,128]{1,0:T(8,128)S(1)}) custom-call(f32[3328,128]{1,0:T(8,128)} %bitcast.11), custom_call_target="tpu_custom_call" | custom-call | flops 3758096384 | bytes 1703936 | tf_op jit(solution)/shard_map/sums/pallas_call | solution.py:216
  47.5 3.1 %collective-permute-start = (f32[128,128]{1,0:T(8,128)S(1)}, f32[128,128]{1,0:T(8,128)S(1)}, u32[]{:S(2)}, u32[]{:S(2)}) collective-permute-start(f32[128,128]{1,0:T(8,128)S(1)} %get-tuple-element.24), channel_id=1, source_target_pairs={{0,64},{64,128},{128,192},{192,0},{1,65},{65,129},{129,193},{193,1... | collective-permute-start | bytes 196616 | tf_op jit(solution)/shard_map/ppermute | solution.py:376
  50.5 4.2 %collective-permute-start.1 = (f32[128,128]{1,0:T(8,128)S(1)}, f32[128,128]{1,0:T(8,128)S(1)}, u32[]{:S(2)}, u32[]{:S(2)}) collective-permute-start(f32[128,128]{1,0:T(8,128)S(1)} %get-tuple-element.25), channel_id=1, source_target_pairs={{0,128},{64,192},{128,0},{192,64},{1,129},{65,193},{129,1},{193,65... | collective-permute-start | bytes 196616 | tf_op jit(solution)/shard_map/ppermute | solution.py:376
  54.8 2.4 %collective-permute-start.2 = (f32[128,128]{1,0:T(8,128)S(1)}, f32[128,128]{1,0:T(8,128)S(1)}, u32[]{:S(2)}, u32[]{:S(2)}) collective-permute-start(f32[128,128]{1,0:T(8,128)S(1)} %get-tuple-element.26), channel_id=1, source_target_pairs={{0,192},{64,0},{128,64},{192,128},{1,193},{65,1},{129,65},{193,129... | collective-permute-start | bytes 196616 | tf_op jit(solution)/shard_map/ppermute | solution.py:376
  57.1 0.4 collective-permute-done.1
  57.6 3.1 %collective-permute-done.2 = f32[128,128]{1,0:T(8,128)S(1)} collective-permute-done((f32[128,128]{1,0:T(8,128)S(1)}, f32[128,128]{1,0:T(8,128)S(1)}, u32[]{:S(2)}, u32[]{:S(2)}) %collective-permute-start.2) | collective-permute-done | bytes 65568 | tf_op jit(solution)/shard_map/ppermute | solution.py:376
  60.7 0.9 broadcast_in_dim.20
  61.6 5.5 %all-to-all-start.1 = ((f32[32,32,128]{2,1,0:T(8,128)}), f32[32,32,128]{2,1,0:T(8,128)S(1)}, u32[]{:S(2)}, u32[]{:S(2)}) async-start(f32[32,32,128]{2,1,0:T(8,128)} %broadcast_in_dim.20), calls=%async_computation.1 | async-start | bytes 1048576 | tf_op jit(solution)/shard_map/all_to_all | solution.py:361
  67.2 0.7 bitcast_reduce_fusion
  68.8 0.7 collective-permute-start.3
  69.6 7.2 %all-to-all-done.1.slots_ref = f32[32,32,128]{2,1,0:T(8,128)S(1)} async-done(((f32[32,32,128]{2,1,0:T(8,128)}), f32[32,32,128]{2,1,0:T(8,128)S(1)}, u32[]{:S(2)}, u32[]{:S(2)}) %all-to-all-start.1) | async-done | bytes 524320 | tf_op jit(solution)/shard_map/all_to_all | solution.py:361
  76.8 2.9 %place.1 = (f32[72,128]{1,0:T(8,128)S(1)}, f32[72,128]{1,0:T(8,128)S(1)}) custom-call(f32[32,32,128]{2,1,0:T(8,128)S(1)} %all-to-all-done.1.slots_ref, s32[34,2,128]{2,1,0:T(2,128)S(1)} %and_select_fusion.codes_ref), custom_call_target="tpu_custom_call" | custom-call | tf_op jit(solution)/shard_map/place/pallas_call | solution.py:274
  79.7 3.0 %collective-permute-start.4 = (f32[72,128]{1,0:T(8,128)S(1)}, f32[72,128]{1,0:T(8,128)S(1)}, u32[]{:S(2)}, u32[]{:S(2)}) collective-permute-start(f32[72,128]{1,0:T(8,128)S(1)} %get-tuple-element.32), channel_id=1, source_target_pairs={{0,4},{4,0},{1,5},{5,1},{2,6},{6,2},{3,7},{7,3},{8,12},{12,8},{9,1... | collective-permute-start | bytes 110600 | tf_op jit(solution)/shard_map/ppermute | solution.py:376
  82.6 0.9 collective-permute-done.4
  83.5 3.9 %collective-permute-start.7 = (f32[72,128]{1,0:T(8,128)S(1)}, f32[72,128]{1,0:T(8,128)S(1)}, u32[]{:S(2)}, u32[]{:S(2)}) collective-permute-start(f32[72,128]{1,0:T(8,128)S(1)} %add.52), channel_id=1, source_target_pairs={{0,192},{64,0},{128,64},{192,128},{1,193},{65,1},{129,65},{193,129... | collective-permute-start | bytes 110600 | tf_op jit(solution)/shard_map/ppermute | solution.py:376
  87.4 3.0 %collective-permute-start.6 = (f32[72,128]{1,0:T(8,128)S(1)}, f32[72,128]{1,0:T(8,128)S(1)}, u32[]{:S(2)}, u32[]{:S(2)}) collective-permute-start(f32[72,128]{1,0:T(8,128)S(1)} %add.52), channel_id=1, source_target_pairs={{0,128},{64,192},{128,0},{192,64},{1,129},{65,193},{129,1},{193,65... | collective-permute-start | bytes 110600 | tf_op jit(solution)/shard_map/ppermute | solution.py:376
  90.4 2.3 %collective-permute-start.5 = (f32[72,128]{1,0:T(8,128)S(1)}, f32[72,128]{1,0:T(8,128)S(1)}, u32[]{:S(2)}, u32[]{:S(2)}) collective-permute-start(f32[72,128]{1,0:T(8,128)S(1)} %add.52), channel_id=1, source_target_pairs={{0,64},{64,128},{128,192},{192,0},{1,65},{65,129},{129,193},{193,1... | collective-permute-start | bytes 110600 | tf_op jit(solution)/shard_map/ppermute | solution.py:376
  92.7 2.4 %collective-permute-start.10 = (f32[96,128]{1,0:T(8,128)S(1)}, f32[96,128]{1,0:T(8,128)S(1)}, u32[]{:S(2)}, u32[]{:S(2)}) collective-permute-start(f32[96,128]{1,0:T(8,128)S(1)} %collective-permute-done.3.one_ref), channel_id=1, source_target_pairs={{0,3},{1,0},{2,1},{3,2},{4,7},{5,4},{6,5},{7,6},{8,11},{9,8},{10,9... | collective-permute-start | bytes 147464 | tf_op jit(solution)/shard_map/ppermute | solution.py:376
  95.2 0.5 collective-permute-start.8
  95.8 1.5 %collective-permute-start.11 = (f32[32,7,128]{2,1,0:T(8,128)S(1)}, f32[32,7,128]{2,1,0:T(8,128)S(1)}, u32[]{:S(2)}, u32[]{:S(2)}) collective-permute-start(f32[32,7,128]{2,1,0:T(8,128)S(1)} %slice.11.hot_ref), channel_id=1, source_target_pairs={{0,4},{4,0},{1,5},{5,1},{2,6},{6,2},{3,7},{7,3},{8,12},{12,8},{9,1... | collective-permute-start | bytes 344072 | tf_op jit(solution)/shard_map/ppermute | solution.py:376
  97.3 2.4 %collective-permute-done.9.three_ref = f32[96,128]{1,0:T(8,128)S(1)} collective-permute-done((f32[96,128]{1,0:T(8,128)S(1)}, f32[96,128]{1,0:T(8,128)S(1)}, u32[]{:S(2)}, u32[]{:S(2)}) %collective-permute-start.9) | collective-permute-done | bytes 49184 | tf_op jit(solution)/shard_map/ppermute | solution.py:376
  99.6 0.3 collective-permute-done.8.two_ref
  99.9 1.1 broadcast_in_dim.23
  101.0 6.7 %all-to-all-start.2 = ((f32[32,72,128]{2,1,0:T(8,128)}), f32[32,72,128]{2,1,0:T(8,128)S(1)}, u32[]{:S(2)}, u32[]{:S(2)}) async-start(f32[32,72,128]{2,1,0:T(8,128)} %broadcast_in_dim.23), calls=%async_computation.2 | async-start | bytes 2359296 | tf_op jit(solution)/shard_map/all_to_all | solution.py:361
  107.7 1.7 %blocks.1 = f32[81,1024]{1,0:T(8,128)} custom-call(s32[1,64]{1,0:T(1,128)} %counts_ref.2, f32[96,128]{1,0:T(8,128)S(1)} %collective-permute-done.3.one_ref, f32[96,128]{1,0:T(8,128)S(1)} %collective-permute-done.8.two_ref, f32[96,128]{1,0:T(8,128)S(1)} %collective-permute-done.9.three_ref, f32[96,128]{1,0:T(8,128)S(1)} %collective-permute-done.10.four_ref, ...), custom_call_target="tpu_custom_call" | custom-call | tf_op jit(solution)/shard_map/blocks/pallas_call | solution.py:314
  109.4 13.3 %all-to-all-done.2.rows_ref = f32[32,72,128]{2,1,0:T(8,128)S(1)} async-done(((f32[32,72,128]{2,1,0:T(8,128)}), f32[32,72,128]{2,1,0:T(8,128)S(1)}, u32[]{:S(2)}, u32[]{:S(2)}) %all-to-all-start.2) | async-done | bytes 1179680 | tf_op jit(solution)/shard_map/all_to_all | solution.py:361
  122.8 4.0 %collective-permute-start.12 = (f32[32,72,128]{2,1,0:T(8,128)S(1)}, f32[32,72,128]{2,1,0:T(8,128)S(1)}, u32[]{:S(2)}, u32[]{:S(2)}) collective-permute-start(f32[32,72,128]{2,1,0:T(8,128)S(1)} %all-to-all-done.2.rows_ref), channel_id=1, source_target_pairs={{0,4},{4,0},{1,5},{5,1},{2,6},{6,2},{3,7},{7,3},{8,12},{12,8},{9,1... | collective-permute-start | bytes 3538952 | tf_op jit(solution)/shard_map/ppermute | solution.py:376
  126.8 1.8 %order.2.refs_0_ = f32[9,65536]{1,0:T(8,128)} custom-call(s32[1]{0:T(128)} %bitcast.core_ref, f32[32,72,128]{2,1,0:T(8,128)S(1)} %all-to-all-done.2.rows_ref), custom_call_target="tpu_custom_call" | custom-call | tf_op jit(solution)/shard_map/order/pallas_call | solution.py:346
  128.6 0.6 collective-permute-done.12.rows_ref
  129.2 1.8 %order.3 = f32[9,65536]{1,0:T(8,128)} custom-call(s32[1]{0:T(128)} %bitcast.core_ref, f32[32,72,128]{2,1,0:T(8,128)S(1)} %collective-permute-done.12.rows_ref, f32[9,65536]{1,0:T(8,128)} %order.2.refs_0_), custom_call_target="tpu_custom_call", output_to_operand_aliasing={{}: (2, {})} | custom-call | tf_op jit(solution)/shard_map/order/pallas_call | solution.py:346
  (24 shorter events, 0.6 us)
Async XLA Ops:
  47.5 19.7 %copy-start.1 = (s32[1,64]{1,0:T(1,128)S(1)}, s32[1,64]{1,0:T(1,128)}, u32[]{:S(2)}) copy-start(s32[1,64]{1,0:T(1,128)} %counts_ref.2) | copy-start | bytes 772
  47.5 21.0 %copy-start = (s32[65536]{0:T(1024)S(1)}, s32[65536]{0:T(1024)}, u32[]{:S(2)}) copy-start(s32[65536]{0:T(1024)} %param.9) | copy-start | bytes 786436
  47.5 9.7 %collective-permute-start = (f32[128,128]{1,0:T(8,128)S(1)}, f32[128,128]{1,0:T(8,128)S(1)}, u32[]{:S(2)}, u32[]{:S(2)}) collective-permute-start(f32[128,128]{1,0:T(8,128)S(1)} %get-tuple-element.24), channel_id=1, source_target_pairs={{0,64},{64,128},{128,192},{192,0},{1,65},{65,129},{129,193},{193,1... | collective-permute-start | bytes 196616 | tf_op jit(solution)/shard_map/ppermute | solution.py:376
  50.5 7.0 %collective-permute-start.1 = (f32[128,128]{1,0:T(8,128)S(1)}, f32[128,128]{1,0:T(8,128)S(1)}, u32[]{:S(2)}, u32[]{:S(2)}) collective-permute-start(f32[128,128]{1,0:T(8,128)S(1)} %get-tuple-element.25), channel_id=1, source_target_pairs={{0,128},{64,192},{128,0},{192,64},{1,129},{65,193},{129,1},{193,65... | collective-permute-start | bytes 196616 | tf_op jit(solution)/shard_map/ppermute | solution.py:376
  54.8 5.9 %collective-permute-start.2 = (f32[128,128]{1,0:T(8,128)S(1)}, f32[128,128]{1,0:T(8,128)S(1)}, u32[]{:S(2)}, u32[]{:S(2)}) collective-permute-start(f32[128,128]{1,0:T(8,128)S(1)} %get-tuple-element.26), channel_id=1, source_target_pairs={{0,192},{64,0},{128,64},{192,128},{1,193},{65,1},{129,65},{193,129... | collective-permute-start | bytes 196616 | tf_op jit(solution)/shard_map/ppermute | solution.py:376
  61.6 15.2 %all-to-all-start.1 = ((f32[32,32,128]{2,1,0:T(8,128)}), f32[32,32,128]{2,1,0:T(8,128)S(1)}, u32[]{:S(2)}, u32[]{:S(2)}) async-start(f32[32,32,128]{2,1,0:T(8,128)} %broadcast_in_dim.20), calls=%async_computation.1 | async-start | bytes 1048576 | tf_op jit(solution)/shard_map/all_to_all | solution.py:361
  68.8 0.7 collective-permute-start.3
  79.7 3.8 %collective-permute-start.4 = (f32[72,128]{1,0:T(8,128)S(1)}, f32[72,128]{1,0:T(8,128)S(1)}, u32[]{:S(2)}, u32[]{:S(2)}) collective-permute-start(f32[72,128]{1,0:T(8,128)S(1)} %get-tuple-element.32), channel_id=1, source_target_pairs={{0,4},{4,0},{1,5},{5,1},{2,6},{6,2},{3,7},{7,3},{8,12},{12,8},{9,1... | collective-permute-start | bytes 110600 | tf_op jit(solution)/shard_map/ppermute | solution.py:376
  83.5 11.7 %collective-permute-start.7 = (f32[72,128]{1,0:T(8,128)S(1)}, f32[72,128]{1,0:T(8,128)S(1)}, u32[]{:S(2)}, u32[]{:S(2)}) collective-permute-start(f32[72,128]{1,0:T(8,128)S(1)} %add.52), channel_id=1, source_target_pairs={{0,192},{64,0},{128,64},{192,128},{1,193},{65,1},{129,65},{193,129... | collective-permute-start | bytes 110600 | tf_op jit(solution)/shard_map/ppermute | solution.py:376
  87.4 8.4 %collective-permute-start.6 = (f32[72,128]{1,0:T(8,128)S(1)}, f32[72,128]{1,0:T(8,128)S(1)}, u32[]{:S(2)}, u32[]{:S(2)}) collective-permute-start(f32[72,128]{1,0:T(8,128)S(1)} %add.52), channel_id=1, source_target_pairs={{0,128},{64,192},{128,0},{192,64},{1,129},{65,193},{129,1},{193,65... | collective-permute-start | bytes 110600 | tf_op jit(solution)/shard_map/ppermute | solution.py:376
  90.4 6.9 %collective-permute-start.5 = (f32[72,128]{1,0:T(8,128)S(1)}, f32[72,128]{1,0:T(8,128)S(1)}, u32[]{:S(2)}, u32[]{:S(2)}) collective-permute-start(f32[72,128]{1,0:T(8,128)S(1)} %add.52), channel_id=1, source_target_pairs={{0,64},{64,128},{128,192},{192,0},{1,65},{65,129},{129,193},{193,1... | collective-permute-start | bytes 110600 | tf_op jit(solution)/shard_map/ppermute | solution.py:376
  92.7 4.6 %collective-permute-start.10 = (f32[96,128]{1,0:T(8,128)S(1)}, f32[96,128]{1,0:T(8,128)S(1)}, u32[]{:S(2)}, u32[]{:S(2)}) collective-permute-start(f32[96,128]{1,0:T(8,128)S(1)} %collective-permute-done.3.one_ref), channel_id=1, source_target_pairs={{0,3},{1,0},{2,1},{3,2},{4,7},{5,4},{6,5},{7,6},{8,11},{9,8},{10,9... | collective-permute-start | bytes 147464 | tf_op jit(solution)/shard_map/ppermute | solution.py:376
  95.1 4.5 %collective-permute-start.9 = (f32[96,128]{1,0:T(8,128)S(1)}, f32[96,128]{1,0:T(8,128)S(1)}, u32[]{:S(2)}, u32[]{:S(2)}) collective-permute-start(f32[96,128]{1,0:T(8,128)S(1)} %collective-permute-done.3.one_ref), channel_id=1, source_target_pairs={{0,2},{1,3},{2,0},{3,1},{4,6},{5,7},{6,4},{7,5},{8,10},{9,11},{10,... | collective-permute-start | bytes 147464 | tf_op jit(solution)/shard_map/ppermute | solution.py:376
  95.2 4.7 %collective-permute-start.8 = (f32[96,128]{1,0:T(8,128)S(1)}, f32[96,128]{1,0:T(8,128)S(1)}, u32[]{:S(2)}, u32[]{:S(2)}) collective-permute-start(f32[96,128]{1,0:T(8,128)S(1)} %collective-permute-done.3.one_ref), channel_id=1, source_target_pairs={{0,1},{1,2},{2,3},{3,0},{4,5},{5,6},{6,7},{7,4},{8,9},{9,10},{10,1... | collective-permute-start | bytes 147464 | tf_op jit(solution)/shard_map/ppermute | solution.py:376
  95.8 4.1 %collective-permute-start.11 = (f32[32,7,128]{2,1,0:T(8,128)S(1)}, f32[32,7,128]{2,1,0:T(8,128)S(1)}, u32[]{:S(2)}, u32[]{:S(2)}) collective-permute-start(f32[32,7,128]{2,1,0:T(8,128)S(1)} %slice.11.hot_ref), channel_id=1, source_target_pairs={{0,4},{4,0},{1,5},{5,1},{2,6},{6,2},{3,7},{7,3},{8,12},{12,8},{9,1... | collective-permute-start | bytes 344072 | tf_op jit(solution)/shard_map/ppermute | solution.py:376
  101.0 21.8 %all-to-all-start.2 = ((f32[32,72,128]{2,1,0:T(8,128)}), f32[32,72,128]{2,1,0:T(8,128)S(1)}, u32[]{:S(2)}, u32[]{:S(2)}) async-start(f32[32,72,128]{2,1,0:T(8,128)} %broadcast_in_dim.23), calls=%async_computation.2 | async-start | bytes 2359296 | tf_op jit(solution)/shard_map/all_to_all | solution.py:361
  122.8 6.5 %collective-permute-start.12 = (f32[32,72,128]{2,1,0:T(8,128)S(1)}, f32[32,72,128]{2,1,0:T(8,128)S(1)}, u32[]{:S(2)}, u32[]{:S(2)}) collective-permute-start(f32[32,72,128]{2,1,0:T(8,128)S(1)} %all-to-all-done.2.rows_ref), channel_id=1, source_target_pairs={{0,4},{4,0},{1,5},{5,1},{2,6},{6,2},{3,7},{7,3},{8,12},{12,8},{9,1... | collective-permute-start | bytes 3538952 | tf_op jit(solution)/shard_map/ppermute | solution.py:376

commit v7 on v6

--- a/solution.py
+++ b/solution.py
@@ -226,11 +226,12 @@
             pltpu.VMEM((2 * TERMS * QUARTERS, SPAN), F32),
             pltpu.VMEM((8, LANES), F32),
         ],
+        compiler_params=pltpu.CompilerParams(vmem_limit_bytes=40 << 20),
         cost_estimate=pl.CostEstimate(
             flops=2 * 2 * TERMS * CAM_DEV * 128 * rows // BLOCK, transcendentals=0, bytes_accessed=rows * 512
         ),
         name="sums",
-    )(arrived)
+    )(near(arrived))
 
 
 def place_body(slots_ref, codes_ref, mine_ref, theirs_ref, left_ref, right_ref, acc_ref):
@@ -266,6 +267,10 @@
             for half in range(2):
                 row = (part * 2 + half) * CAMS
                 out_ref[row : row + CAMS, :] = both[:, half * LANES : (half + 1) * LANES]
+    base = ranges * CAMS
+    for source in range(sources):
+        row = base + source * HOT_ROWS
+        theirs_ref[row : row + HOT_ROWS, :] = slots_ref[source, 2 * CAMS : 2 * CAMS + HOT_ROWS, :]
 
 
 def placed(slots, codes, ranges):
@@ -273,7 +278,10 @@
     chunks = slots.shape[0] // 4 + 1
     return pl.pallas_call(
         place_body,
-        out_shape=[pltpu.VMEM((ranges * CAMS, LANES), F32)] * 2,
+        out_shape=[
+            pltpu.VMEM((ranges * CAMS, LANES), F32),
+            pltpu.VMEM((ranges * CAMS + slots.shape[0] * HOT_ROWS, LANES), F32),
+        ],
         in_specs=[VMEM, VMEM],
         out_specs=[VMEM, VMEM],
         scratch_shapes=[
@@ -296,8 +304,9 @@
                 if start >= PAIRS:
                     continue
                 source = group * 4 + lax.rem(part, 2) * 2 + half
-                here = hot_ref[source, : stop - start, :]
-                there = other_ref[source, : stop - start, :]
+                here = hot_ref[source, 2 * CAMS : 2 * CAMS + stop - start, :]
+                row = 2 * CAMS * QUARTERS + source * HOT_ROWS
+                there = other_ref[pl.ds(row, stop - start), :]
                 hot = jnp.where(lax.div(part, 2) == core, here, there)
                 share = share_ref[half * BLOCK_ROWS + start : half * BLOCK_ROWS + stop, :]
                 rows_ref[start:stop, :] = share + jnp.where(own > 0, hot, 0.0)
@@ -402,14 +411,13 @@
     slots, squares = lax.optimization_barrier((slots, squares))
     shares = [squares] + [turned(squares, "x", turn) for turn in range(1, QUARTERS)]
     mine, theirs = placed(slots, codes, 2 * QUARTERS)
-    own_hot = slots[:, 2 * CAMS : 2 * CAMS + HOT_ROWS]
-    other_hot = turned(own_hot, "c", 1)
-    mine = mine + turned(theirs, "c", 1)
+    theirs = turned(theirs, "c", 1)
+    mine = mine + theirs[: mine.shape[0]]
     part = mine
     for turn in range(1, QUARTERS):
         part = part + turned(mine, "zk", turn)
-    part, shares, other_hot = lax.optimization_barrier((part, shares, other_hot))
-    blocks = whole_blocks(bucket_counts, shares, own_hot, other_hot)
+    part, shares = lax.optimization_barrier((part, shares))
+    blocks = whole_blocks(bucket_counts, shares, slots, theirs)
     part = from_all(part, RANGE)
     part, blocks = lax.optimization_barrier((part, blocks))
     other = turned(part, "c", 1)

time: 131 us -> 130 us (level)
  starting transfers between devices: 43.3 us -> 41.4 us
  waiting for transfers between devices: 28.2 us -> 30 us
    ppermute x12 -> x11, starting transfers between devices: 30.3 us -> 28.4 us  [turned(): lax.ppermute(share, axis, [(k, (k + turn) % count) for k in range(count)])]
    ppermute x12 -> x11, waiting for transfers between devices: 7.72 us -> 9.46 us  [turned(): lax.ppermute(share, axis, [(k, (k + turn) % count) for k in range(count)])]
  transfers between devices with their start and end apart: 15 -> 14, of which waited for: 8 -> 10; matrix products, arithmetic and copies ran while one was open for 1% -> 1% of each run, Pallas kernels for 3% -> 3%
where the time goes in v7:
time: 130 us
  starting transfers between devices  41.4 us (32%)
  blocking collectives  34.1 us (26%)
  waiting for transfers between devices  30 us (23%)
  Pallas kernels  19.8 us (15%)
  local copies, waits for them, and re-layouts  2.18 us (2%)
  between operations  1.45 us (1%)
    all_to_all x1, blocking collectives, exchanged(): return lax.all_to_all(pieces, axes, 0, 0, tiled=True)  34.1 us
    ppermute x11, starting transfers between devices, turned(): lax.ppermute(share, axis, [(k, (k + turn) % count) for k in range(count)])  28.4 us
    all_to_all x2, waiting for transfers between devices, exchanged(): return lax.all_to_all(pieces, axes, 0, 0, tiled=True)  20.6 us
    all_to_all x2, starting transfers between devices, exchanged(): return lax.all_to_all(pieces, axes, 0, 0, tiled=True)  12.3 us
    ppermute x11, waiting for transfers between devices, turned(): lax.ppermute(share, axis, [(k, (k + turn) % count) for k in range(count)])  9.46 us
    pallas_call x1, Pallas kernels, camera_sums(): pl.pallas_call(sums_body, grid=(rows // step,), out_shape=[pltpu.VMEM(out...  8.38 us
    pallas_call x2, Pallas kernels, ordered(): pl.pallas_call(order_body, grid_spec=pltpu.PrefetchScalarGridSpec(num_sca...  3.65 us
    pallas_call x1, Pallas kernels, packed(): pl.pallas_call(pack_body, grid=(steps,), out_shape=pltpu.VMEM((targets *...  3.22 us
  transfers between devices with their start and end apart: 14, of which 10 were waited for; matrix products, arithmetic and copies ran while one was open for 1% of the time, Pallas kernels for 3%

profile of v7, /device:TPU:1, one launch (start us, length us, event | category | flops | bytes accessed | tf_op | source)
XLA Modules:
  0.0 129.8 jit_solution(16273444445832800136)
XLA Ops:
  0.6 3.2 %pack.1 = f32[3328,128]{1,0:T(8,128)S(1)} custom-call(s32[1,64]{1,0:T(1,128)} %counts_ref.2, f32[18,32768]{1,0:T(8,128)} %jac_ref.1, f32[2,32768]{1,0:T(2,128)} %res_ref.1, s32[1,32768]{1,0:T(1,128)} %bitcast.12), custom_call_target="tpu_custom_call" | custom-call | tf_op jit(solution)/shard_map/pack/pallas_call | solution.py:139
  3.9 34.1 %all_to_all.15 = f32[64,13,4,128]{3,2,1,0:T(4,128)S(1)} all-to-all(f32[64,13,4,128]{3,2,1,0:T(4,128)S(1)} %bitcast.10), channel_id=1, replica_groups=mesh['zk'=4,'zp'=2,'y'=4,'c'=2,'x'=4] {'zp','y','c','x'}, dimensions={0} | all-to-all | bytes 3407872 | tf_op jit(solution)/shard_map/all_to_all | solution.py:370
  37.9 8.4 %sums.1 = (f32[128,128]{1,0:T(8,128)S(1)}, f32[128,128]{1,0:T(8,128)S(1)}, f32[128,128]{1,0:T(8,128)S(1)}, f32[128,128]{1,0:T(8,128)S(1)}) custom-call(f32[3328,128]{1,0:T(8,128)S(1)} %bitcast.11), custom_call_target="tpu_custom_call" | custom-call | flops 3758096384 | bytes 1703936 | tf_op jit(solution)/shard_map/sums/pallas_call | solution.py:216
  46.3 3.1 %collective-permute-start = (f32[128,128]{1,0:T(8,128)S(1)}, f32[128,128]{1,0:T(8,128)S(1)}, u32[]{:S(2)}, u32[]{:S(2)}) collective-permute-start(f32[128,128]{1,0:T(8,128)S(1)} %get-tuple-element.23), channel_id=1, source_target_pairs={{0,64},{64,128},{128,192},{192,0},{1,65},{65,129},{129,193},{193,1... | collective-permute-start | bytes 196616 | tf_op jit(solution)/shard_map/ppermute | solution.py:385
  49.4 4.2 %collective-permute-start.1 = (f32[128,128]{1,0:T(8,128)S(1)}, f32[128,128]{1,0:T(8,128)S(1)}, u32[]{:S(2)}, u32[]{:S(2)}) collective-permute-start(f32[128,128]{1,0:T(8,128)S(1)} %get-tuple-element.24), channel_id=1, source_target_pairs={{0,128},{64,192},{128,0},{192,64},{1,129},{65,193},{129,1},{193,65... | collective-permute-start | bytes 196616 | tf_op jit(solution)/shard_map/ppermute | solution.py:385
  53.6 2.4 %collective-permute-start.2 = (f32[128,128]{1,0:T(8,128)S(1)}, f32[128,128]{1,0:T(8,128)S(1)}, u32[]{:S(2)}, u32[]{:S(2)}) collective-permute-start(f32[128,128]{1,0:T(8,128)S(1)} %get-tuple-element.25), channel_id=1, source_target_pairs={{0,192},{64,0},{128,64},{192,128},{1,193},{65,1},{129,65},{193,129... | collective-permute-start | bytes 196616 | tf_op jit(solution)/shard_map/ppermute | solution.py:385
  56.0 0.4 collective-permute-done.1
  56.4 3.1 %collective-permute-done.2 = f32[128,128]{1,0:T(8,128)S(1)} collective-permute-done((f32[128,128]{1,0:T(8,128)S(1)}, f32[128,128]{1,0:T(8,128)S(1)}, u32[]{:S(2)}, u32[]{:S(2)}) %collective-permute-start.2) | collective-permute-done | bytes 65568 | tf_op jit(solution)/shard_map/ppermute | solution.py:385
  59.6 0.9 broadcast_in_dim.20
  60.4 5.6 %all-to-all-start.1 = ((f32[32,32,128]{2,1,0:T(8,128)}), f32[32,32,128]{2,1,0:T(8,128)S(1)}, u32[]{:S(2)}, u32[]{:S(2)}) async-start(f32[32,32,128]{2,1,0:T(8,128)} %broadcast_in_dim.20), calls=%async_computation.1 | async-start | bytes 1048576 | tf_op jit(solution)/shard_map/all_to_all | solution.py:370
  66.0 0.7 bitcast_reduce_fusion
  67.7 0.7 collective-permute-start.3
  68.4 7.2 %all-to-all-done.1.slots_ref.hot_ref = f32[32,32,128]{2,1,0:T(8,128)S(1)} async-done(((f32[32,32,128]{2,1,0:T(8,128)}), f32[32,32,128]{2,1,0:T(8,128)S(1)}, u32[]{:S(2)}, u32[]{:S(2)}) %all-to-all-start.1) | async-done | bytes 524320 | tf_op jit(solution)/shard_map/all_to_all | solution.py:370
  75.6 2.9 %place.1 = (f32[72,128]{1,0:T(8,128)S(1)}, f32[296,128]{1,0:T(8,128)S(1)}) custom-call(f32[32,32,128]{2,1,0:T(8,128)S(1)} %all-to-all-done.1.slots_ref.hot_ref, s32[34,2,128]{2,1,0:T(2,128)S(1)} %and_select_fusion.codes_ref), custom_call_target="tpu_custom_call" | custom-call | tf_op jit(solution)/shard_map/place/pallas_call | solution.py:279
  78.6 3.0 %collective-permute-start.4 = (f32[296,128]{1,0:T(8,128)S(1)}, f32[296,128]{1,0:T(8,128)S(1)}, u32[]{:S(2)}, u32[]{:S(2)}) collective-permute-start(f32[296,128]{1,0:T(8,128)S(1)} %get-tuple-element.31), channel_id=1, source_target_pairs={{0,4},{4,0},{1,5},{5,1},{2,6},{6,2},{3,7},{7,3},{8,12},{12,8},{9,1... | collective-permute-start | bytes 454664 | tf_op jit(solution)/shard_map/ppermute | solution.py:385
  81.5 1.0 collective-permute-done.4.other_ref
  82.5 3.8 %collective-permute-start.7 = (f32[72,128]{1,0:T(8,128)S(1)}, f32[72,128]{1,0:T(8,128)S(1)}, u32[]{:S(2)}, u32[]{:S(2)}) collective-permute-start(f32[72,128]{1,0:T(8,128)S(1)} %slice_add_fusion), channel_id=1, source_target_pairs={{0,192},{64,0},{128,64},{192,128},{1,193},{65,1},{129,65},{193,129... | collective-permute-start | bytes 110600 | tf_op jit(solution)/shard_map/ppermute | solution.py:385
  86.4 3.0 %collective-permute-start.6 = (f32[72,128]{1,0:T(8,128)S(1)}, f32[72,128]{1,0:T(8,128)S(1)}, u32[]{:S(2)}, u32[]{:S(2)}) collective-permute-start(f32[72,128]{1,0:T(8,128)S(1)} %slice_add_fusion), channel_id=1, source_target_pairs={{0,128},{64,192},{128,0},{192,64},{1,129},{65,193},{129,1},{193,65... | collective-permute-start | bytes 110600 | tf_op jit(solution)/shard_map/ppermute | solution.py:385
  89.3 2.3 %collective-permute-start.5 = (f32[72,128]{1,0:T(8,128)S(1)}, f32[72,128]{1,0:T(8,128)S(1)}, u32[]{:S(2)}, u32[]{:S(2)}) collective-permute-start(f32[72,128]{1,0:T(8,128)S(1)} %slice_add_fusion), channel_id=1, source_target_pairs={{0,64},{64,128},{128,192},{192,0},{1,65},{65,129},{129,193},{193,1... | collective-permute-start | bytes 110600 | tf_op jit(solution)/shard_map/ppermute | solution.py:385
  91.6 2.1 %collective-permute-start.10 = (f32[96,128]{1,0:T(8,128)S(1)}, f32[96,128]{1,0:T(8,128)S(1)}, u32[]{:S(2)}, u32[]{:S(2)}) collective-permute-start(f32[96,128]{1,0:T(8,128)S(1)} %collective-permute-done.3.one_ref), channel_id=1, source_target_pairs={{0,3},{1,0},{2,1},{3,2},{4,7},{5,4},{6,5},{7,6},{8,11},{9,8},{10,9... | collective-permute-start | bytes 147464 | tf_op jit(solution)/shard_map/ppermute | solution.py:385
  93.9 0.4 collective-permute-start.8
  94.6 0.3 collective-permute-done.10.four_ref
  94.9 3.4 %collective-permute-done.9.three_ref = f32[96,128]{1,0:T(8,128)S(1)} collective-permute-done((f32[96,128]{1,0:T(8,128)S(1)}, f32[96,128]{1,0:T(8,128)S(1)}, u32[]{:S(2)}, u32[]{:S(2)}) %collective-permute-start.9) | collective-permute-done | bytes 49184 | tf_op jit(solution)/shard_map/ppermute | solution.py:385
  98.3 0.3 collective-permute-done.8.two_ref
  98.6 1.1 broadcast_in_dim.23
  99.7 6.7 %all-to-all-start.2 = ((f32[32,72,128]{2,1,0:T(8,128)}), f32[32,72,128]{2,1,0:T(8,128)S(1)}, u32[]{:S(2)}, u32[]{:S(2)}) async-start(f32[32,72,128]{2,1,0:T(8,128)} %broadcast_in_dim.23), calls=%async_computation.2 | async-start | bytes 2359296 | tf_op jit(solution)/shard_map/all_to_all | solution.py:370
  106.4 1.7 %blocks.1 = f32[81,1024]{1,0:T(8,128)} custom-call(s32[1,64]{1,0:T(1,128)} %counts_ref.2, f32[96,128]{1,0:T(8,128)S(1)} %collective-permute-done.3.one_ref, f32[96,128]{1,0:T(8,128)S(1)} %collective-permute-done.8.two_ref, f32[96,128]{1,0:T(8,128)S(1)} %collective-permute-done.9.three_ref, f32[96,128]{1,0:T(8,128)S(1)} %collective-permute-done.10.four_ref, ...), custom_call_target="tpu_custom_call" | custom-call | tf_op jit(solution)/shard_map/blocks/pallas_call | solution.py:323
  108.1 13.4 %all-to-all-done.2.rows_ref = f32[32,72,128]{2,1,0:T(8,128)S(1)} async-done(((f32[32,72,128]{2,1,0:T(8,128)}), f32[32,72,128]{2,1,0:T(8,128)S(1)}, u32[]{:S(2)}, u32[]{:S(2)}) %all-to-all-start.2) | async-done | bytes 1179680 | tf_op jit(solution)/shard_map/all_to_all | solution.py:370
  121.5 4.0 %collective-permute-start.11 = (f32[32,72,128]{2,1,0:T(8,128)S(1)}, f32[32,72,128]{2,1,0:T(8,128)S(1)}, u32[]{:S(2)}, u32[]{:S(2)}) collective-permute-start(f32[32,72,128]{2,1,0:T(8,128)S(1)} %all-to-all-done.2.rows_ref), channel_id=1, source_target_pairs={{0,4},{4,0},{1,5},{5,1},{2,6},{6,2},{3,7},{7,3},{8,12},{12,8},{9,1... | collective-permute-start | bytes 3538952 | tf_op jit(solution)/shard_map/ppermute | solution.py:385
  125.5 1.8 %order.2.refs_0_ = f32[9,65536]{1,0:T(8,128)} custom-call(s32[1]{0:T(128)} %bitcast.core_ref, f32[32,72,128]{2,1,0:T(8,128)S(1)} %all-to-all-done.2.rows_ref), custom_call_target="tpu_custom_call" | custom-call | tf_op jit(solution)/shard_map/order/pallas_call | solution.py:355
  127.3 0.6 collective-permute-done.11.rows_ref
  128.0 1.8 %order.3 = f32[9,65536]{1,0:T(8,128)} custom-call(s32[1]{0:T(128)} %bitcast.core_ref, f32[32,72,128]{2,1,0:T(8,128)S(1)} %collective-permute-done.11.rows_ref, f32[9,65536]{1,0:T(8,128)} %order.2.refs_0_), custom_call_target="tpu_custom_call", output_to_operand_aliasing={{}: (2, {})} | custom-call | tf_op jit(solution)/shard_map/order/pallas_call | solution.py:355
  (21 shorter events, 0.8 us)
Async XLA Ops:
  46.3 19.7 %copy-start.1 = (s32[1,64]{1,0:T(1,128)S(1)}, s32[1,64]{1,0:T(1,128)}, u32[]{:S(2)}) copy-start(s32[1,64]{1,0:T(1,128)} %counts_ref.2) | copy-start | bytes 772
  46.3 21.0 %copy-start = (s32[65536]{0:T(1024)S(1)}, s32[65536]{0:T(1024)}, u32[]{:S(2)}) copy-start(s32[65536]{0:T(1024)} %param.9) | copy-start | bytes 786436
  46.3 9.7 %collective-permute-start = (f32[128,128]{1,0:T(8,128)S(1)}, f32[128,128]{1,0:T(8,128)S(1)}, u32[]{:S(2)}, u32[]{:S(2)}) collective-permute-start(f32[128,128]{1,0:T(8,128)S(1)} %get-tuple-element.23), channel_id=1, source_target_pairs={{0,64},{64,128},{128,192},{192,0},{1,65},{65,129},{129,193},{193,1... | collective-permute-start | bytes 196616 | tf_op jit(solution)/shard_map/ppermute | solution.py:385
  49.4 7.0 %collective-permute-start.1 = (f32[128,128]{1,0:T(8,128)S(1)}, f32[128,128]{1,0:T(8,128)S(1)}, u32[]{:S(2)}, u32[]{:S(2)}) collective-permute-start(f32[128,128]{1,0:T(8,128)S(1)} %get-tuple-element.24), channel_id=1, source_target_pairs={{0,128},{64,192},{128,0},{192,64},{1,129},{65,193},{129,1},{193,65... | collective-permute-start | bytes 196616 | tf_op jit(solution)/shard_map/ppermute | solution.py:385
  53.6 5.9 %collective-permute-start.2 = (f32[128,128]{1,0:T(8,128)S(1)}, f32[128,128]{1,0:T(8,128)S(1)}, u32[]{:S(2)}, u32[]{:S(2)}) collective-permute-start(f32[128,128]{1,0:T(8,128)S(1)} %get-tuple-element.25), channel_id=1, source_target_pairs={{0,192},{64,0},{128,64},{192,128},{1,193},{65,1},{129,65},{193,129... | collective-permute-start | bytes 196616 | tf_op jit(solution)/shard_map/ppermute | solution.py:385
  60.4 15.2 %all-to-all-start.1 = ((f32[32,32,128]{2,1,0:T(8,128)}), f32[32,32,128]{2,1,0:T(8,128)S(1)}, u32[]{:S(2)}, u32[]{:S(2)}) async-start(f32[32,32,128]{2,1,0:T(8,128)} %broadcast_in_dim.20), calls=%async_computation.1 | async-start | bytes 1048576 | tf_op jit(solution)/shard_map/all_to_all | solution.py:370
  67.7 0.7 collective-permute-start.3
  78.6 4.0 %collective-permute-start.4 = (f32[296,128]{1,0:T(8,128)S(1)}, f32[296,128]{1,0:T(8,128)S(1)}, u32[]{:S(2)}, u32[]{:S(2)}) collective-permute-start(f32[296,128]{1,0:T(8,128)S(1)} %get-tuple-element.31), channel_id=1, source_target_pairs={{0,4},{4,0},{1,5},{5,1},{2,6},{6,2},{3,7},{7,3},{8,12},{12,8},{9,1... | collective-permute-start | bytes 454664 | tf_op jit(solution)/shard_map/ppermute | solution.py:385
  82.5 11.4 %collective-permute-start.7 = (f32[72,128]{1,0:T(8,128)S(1)}, f32[72,128]{1,0:T(8,128)S(1)}, u32[]{:S(2)}, u32[]{:S(2)}) collective-permute-start(f32[72,128]{1,0:T(8,128)S(1)} %slice_add_fusion), channel_id=1, source_target_pairs={{0,192},{64,0},{128,64},{192,128},{1,193},{65,1},{129,65},{193,129... | collective-permute-start | bytes 110600 | tf_op jit(solution)/shard_map/ppermute | solution.py:385
  86.4 8.0 %collective-permute-start.6 = (f32[72,128]{1,0:T(8,128)S(1)}, f32[72,128]{1,0:T(8,128)S(1)}, u32[]{:S(2)}, u32[]{:S(2)}) collective-permute-start(f32[72,128]{1,0:T(8,128)S(1)} %slice_add_fusion), channel_id=1, source_target_pairs={{0,128},{64,192},{128,0},{192,64},{1,129},{65,193},{129,1},{193,65... | collective-permute-start | bytes 110600 | tf_op jit(solution)/shard_map/ppermute | solution.py:385
  89.3 5.3 %collective-permute-start.5 = (f32[72,128]{1,0:T(8,128)S(1)}, f32[72,128]{1,0:T(8,128)S(1)}, u32[]{:S(2)}, u32[]{:S(2)}) collective-permute-start(f32[72,128]{1,0:T(8,128)S(1)} %slice_add_fusion), channel_id=1, source_target_pairs={{0,64},{64,128},{128,192},{192,0},{1,65},{65,129},{129,193},{193,1... | collective-permute-start | bytes 110600 | tf_op jit(solution)/shard_map/ppermute | solution.py:385
  91.6 3.3 %collective-permute-start.10 = (f32[96,128]{1,0:T(8,128)S(1)}, f32[96,128]{1,0:T(8,128)S(1)}, u32[]{:S(2)}, u32[]{:S(2)}) collective-permute-start(f32[96,128]{1,0:T(8,128)S(1)} %collective-permute-done.3.one_ref), channel_id=1, source_target_pairs={{0,3},{1,0},{2,1},{3,2},{4,7},{5,4},{6,5},{7,6},{8,11},{9,8},{10,9... | collective-permute-start | bytes 147464 | tf_op jit(solution)/shard_map/ppermute | solution.py:385
  93.8 4.5 %collective-permute-start.9 = (f32[96,128]{1,0:T(8,128)S(1)}, f32[96,128]{1,0:T(8,128)S(1)}, u32[]{:S(2)}, u32[]{:S(2)}) collective-permute-start(f32[96,128]{1,0:T(8,128)S(1)} %collective-permute-done.3.one_ref), channel_id=1, source_target_pairs={{0,2},{1,3},{2,0},{3,1},{4,6},{5,7},{6,4},{7,5},{8,10},{9,11},{10,... | collective-permute-start | bytes 147464 | tf_op jit(solution)/shard_map/ppermute | solution.py:385
  93.9 4.7 %collective-permute-start.8 = (f32[96,128]{1,0:T(8,128)S(1)}, f32[96,128]{1,0:T(8,128)S(1)}, u32[]{:S(2)}, u32[]{:S(2)}) collective-permute-start(f32[96,128]{1,0:T(8,128)S(1)} %collective-permute-done.3.one_ref), channel_id=1, source_target_pairs={{0,1},{1,2},{2,3},{3,0},{4,5},{5,6},{6,7},{7,4},{8,9},{9,10},{10,1... | collective-permute-start | bytes 147464 | tf_op jit(solution)/shard_map/ppermute | solution.py:385
  99.7 21.8 %all-to-all-start.2 = ((f32[32,72,128]{2,1,0:T(8,128)}), f32[32,72,128]{2,1,0:T(8,128)S(1)}, u32[]{:S(2)}, u32[]{:S(2)}) async-start(f32[32,72,128]{2,1,0:T(8,128)} %broadcast_in_dim.23), calls=%async_computation.2 | async-start | bytes 2359296 | tf_op jit(solution)/shard_map/all_to_all | solution.py:370
  121.5 6.5 %collective-permute-start.11 = (f32[32,72,128]{2,1,0:T(8,128)S(1)}, f32[32,72,128]{2,1,0:T(8,128)S(1)}, u32[]{:S(2)}, u32[]{:S(2)}) collective-permute-start(f32[32,72,128]{2,1,0:T(8,128)S(1)} %all-to-all-done.2.rows_ref), channel_id=1, source_target_pairs={{0,4},{4,0},{1,5},{5,1},{2,6},{6,2},{3,7},{7,3},{8,12},{12,8},{9,1... | collective-permute-start | bytes 3538952 | tf_op jit(solution)/shard_map/ppermute | solution.py:385

commit v8 on v7

--- a/solution.py
+++ b/solution.py
@@ -5,6 +5,7 @@
 from jax.experimental.pallas import tpu as pltpu
 from jax.sharding import Mesh
 from jax.sharding import PartitionSpec as P
+
 
 CAM_DEV = 1024
 HALF = 256
@@ -409,16 +410,18 @@
     squares = to_owner(share[GRAD_ROWS:])
     slots = from_all(share[:GRAD_ROWS], RANGE)
     slots, squares = lax.optimization_barrier((slots, squares))
-    shares = [squares] + [turned(squares, "x", turn) for turn in range(1, QUARTERS)]
+    shares = [squares]
+    for turn in range(1, QUARTERS):
+        shares.append(turned(squares, "x", turn))
     mine, theirs = placed(slots, codes, 2 * QUARTERS)
     theirs = turned(theirs, "c", 1)
     mine = mine + theirs[: mine.shape[0]]
     part = mine
     for turn in range(1, QUARTERS):
         part = part + turned(mine, "zk", turn)
-    part, shares = lax.optimization_barrier((part, shares))
     blocks = whole_blocks(bucket_counts, shares, slots, theirs)
-    part = from_all(part, RANGE)
+    spread = jnp.broadcast_to(part[None], (targets // 2, *part.shape))
+    part = exchanged(spread, RANGE)
     part, blocks = lax.optimization_barrier((part, blocks))
     other = turned(part, "c", 1)
     core = core.reshape(1)

time: 130 us -> 130 us (level)
  starting transfers between devices: 41.4 us -> 45.3 us
  waiting for transfers between devices: 30 us -> 26.4 us
    all_to_all x2, waiting for transfers between devices: 20.6 us -> 7.22 us  [exchanged(): return lax.all_to_all(pieces, axes, 0, 0, tiled=True)]
    ppermute x11, waiting for transfers between devices: 9.46 us -> 19.2 us  [turned(): lax.ppermute(share, axis, [(k, (k + turn) % count) for k in range(count)])]
    all_to_all x2, starting transfers between devices: 12.3 us -> 15 us  [exchanged(): return lax.all_to_all(pieces, axes, 0, 0, tiled=True)]
  transfers between devices with their start and end apart: 14 -> 14, of which waited for: 10 -> 9; matrix products, arithmetic and copies ran while one was open for 1% -> 1% of each run, Pallas kernels for 3% -> 3%
where the time goes in v8:
time: 130 us
  starting transfers between devices  45.3 us (35%)
  blocking collectives  34.1 us (26%)
  waiting for transfers between devices  26.4 us (20%)
  Pallas kernels  19.8 us (15%)
  local copies, waits for them, and re-layouts  2.18 us (2%)
  between operations  1.45 us (1%)
    all_to_all x1, blocking collectives, exchanged(): return lax.all_to_all(pieces, axes, 0, 0, tiled=True)  34.1 us
    ppermute x11, starting transfers between devices, turned(): lax.ppermute(share, axis, [(k, (k + turn) % count) for k in range(count)])  29.7 us
    ppermute x11, waiting for transfers between devices, turned(): lax.ppermute(share, axis, [(k, (k + turn) % count) for k in range(count)])  19.2 us
    all_to_all x2, starting transfers between devices, exchanged(): return lax.all_to_all(pieces, axes, 0, 0, tiled=True)  15 us
    pallas_call x1, Pallas kernels, camera_sums(): pl.pallas_call(sums_body, grid=(rows // step,), out_shape=[pltpu.VMEM(out...  8.38 us
    all_to_all x2, waiting for transfers between devices, exchanged(): return lax.all_to_all(pieces, axes, 0, 0, tiled=True)  7.22 us
    pallas_call x2, Pallas kernels, ordered(): pl.pallas_call(order_body, grid_spec=pltpu.PrefetchScalarGridSpec(num_sca...  3.65 us
    pallas_call x1, Pallas kernels, packed(): pl.pallas_call(pack_body, grid=(steps,), out_shape=pltpu.VMEM((targets *...  3.22 us
  transfers between devices with their start and end apart: 14, of which 9 were waited for; matrix products, arithmetic and copies ran while one was open for 1% of the time, Pallas kernels for 3%

profile of v8, /device:TPU:1, one launch (start us, length us, event | category | flops | bytes accessed | tf_op | source)
XLA Modules:
  0.0 130.0 jit_solution(3119991170649715867)
XLA Ops:
  0.6 3.2 %pack.1 = f32[3328,128]{1,0:T(8,128)S(1)} custom-call(s32[1,64]{1,0:T(1,128)} %counts_ref.2, f32[18,32768]{1,0:T(8,128)} %jac_ref.1, f32[2,32768]{1,0:T(2,128)} %res_ref.1, s32[1,32768]{1,0:T(1,128)} %bitcast.12), custom_call_target="tpu_custom_call" | custom-call | tf_op jit(solution)/shard_map/pack/pallas_call | solution.py:140
  3.9 34.1 %all_to_all.15 = f32[64,13,4,128]{3,2,1,0:T(4,128)S(1)} all-to-all(f32[64,13,4,128]{3,2,1,0:T(4,128)S(1)} %bitcast.10), channel_id=1, replica_groups=mesh['zk'=4,'zp'=2,'y'=4,'c'=2,'x'=4] {'zp','y','c','x'}, dimensions={0} | all-to-all | bytes 3407872 | tf_op jit(solution)/shard_map/all_to_all | solution.py:371
  37.9 8.4 %sums.1 = (f32[128,128]{1,0:T(8,128)S(1)}, f32[128,128]{1,0:T(8,128)S(1)}, f32[128,128]{1,0:T(8,128)S(1)}, f32[128,128]{1,0:T(8,128)S(1)}) custom-call(f32[3328,128]{1,0:T(8,128)S(1)} %bitcast.11), custom_call_target="tpu_custom_call" | custom-call | flops 3758096384 | bytes 1703936 | tf_op jit(solution)/shard_map/sums/pallas_call | solution.py:217
  46.3 3.1 %collective-permute-start = (f32[128,128]{1,0:T(8,128)S(1)}, f32[128,128]{1,0:T(8,128)S(1)}, u32[]{:S(2)}, u32[]{:S(2)}) collective-permute-start(f32[128,128]{1,0:T(8,128)S(1)} %get-tuple-element.18), channel_id=1, source_target_pairs={{0,64},{64,128},{128,192},{192,0},{1,65},{65,129},{129,193},{193,1... | collective-permute-start | bytes 196616 | tf_op jit(solution)/shard_map/ppermute | solution.py:386
  49.4 4.2 %collective-permute-start.1 = (f32[128,128]{1,0:T(8,128)S(1)}, f32[128,128]{1,0:T(8,128)S(1)}, u32[]{:S(2)}, u32[]{:S(2)}) collective-permute-start(f32[128,128]{1,0:T(8,128)S(1)} %get-tuple-element.19), channel_id=1, source_target_pairs={{0,128},{64,192},{128,0},{192,64},{1,129},{65,193},{129,1},{193,65... | collective-permute-start | bytes 196616 | tf_op jit(solution)/shard_map/ppermute | solution.py:386
  53.6 2.4 %collective-permute-start.2 = (f32[128,128]{1,0:T(8,128)S(1)}, f32[128,128]{1,0:T(8,128)S(1)}, u32[]{:S(2)}, u32[]{:S(2)}) collective-permute-start(f32[128,128]{1,0:T(8,128)S(1)} %get-tuple-element.20), channel_id=1, source_target_pairs={{0,192},{64,0},{128,64},{192,128},{1,193},{65,1},{129,65},{193,129... | collective-permute-start | bytes 196616 | tf_op jit(solution)/shard_map/ppermute | solution.py:386
  56.4 3.1 %collective-permute-done.2 = f32[128,128]{1,0:T(8,128)S(1)} collective-permute-done((f32[128,128]{1,0:T(8,128)S(1)}, f32[128,128]{1,0:T(8,128)S(1)}, u32[]{:S(2)}, u32[]{:S(2)}) %collective-permute-start.2) | collective-permute-done | bytes 65568 | tf_op jit(solution)/shard_map/ppermute | solution.py:386
  59.6 0.9 broadcast_in_dim.20
  60.4 5.6 %all-to-all-start.1 = ((f32[32,32,128]{2,1,0:T(8,128)}), f32[32,32,128]{2,1,0:T(8,128)S(1)}, u32[]{:S(2)}, u32[]{:S(2)}) async-start(f32[32,32,128]{2,1,0:T(8,128)} %broadcast_in_dim.20), calls=%async_computation.1 | async-start | bytes 1048576 | tf_op jit(solution)/shard_map/all_to_all | solution.py:371
  66.0 0.7 bitcast_reduce_fusion
  67.7 0.7 collective-permute-start.3
  68.4 7.2 %all-to-all-done.1.slots_ref.hot_ref = f32[32,32,128]{2,1,0:T(8,128)S(1)} async-done(((f32[32,32,128]{2,1,0:T(8,128)}), f32[32,32,128]{2,1,0:T(8,128)S(1)}, u32[]{:S(2)}, u32[]{:S(2)}) %all-to-all-start.1) | async-done | bytes 524320 | tf_op jit(solution)/shard_map/all_to_all | solution.py:371
  75.6 2.9 %place.1 = (f32[72,128]{1,0:T(8,128)S(1)}, f32[296,128]{1,0:T(8,128)S(1)}) custom-call(f32[32,32,128]{2,1,0:T(8,128)S(1)} %all-to-all-done.1.slots_ref.hot_ref, s32[34,2,128]{2,1,0:T(2,128)S(1)} %and_select_fusion.codes_ref), custom_call_target="tpu_custom_call" | custom-call | tf_op jit(solution)/shard_map/place/pallas_call | solution.py:280
  78.6 3.0 %collective-permute-start.4 = (f32[296,128]{1,0:T(8,128)S(1)}, f32[296,128]{1,0:T(8,128)S(1)}, u32[]{:S(2)}, u32[]{:S(2)}) collective-permute-start(f32[296,128]{1,0:T(8,128)S(1)} %get-tuple-element.26), channel_id=1, source_target_pairs={{0,4},{4,0},{1,5},{5,1},{2,6},{6,2},{3,7},{7,3},{8,12},{12,8},{9,1... | collective-permute-start | bytes 454664 | tf_op jit(solution)/shard_map/ppermute | solution.py:386
  81.5 1.0 collective-permute-done.4.other_ref
  82.5 3.8 %collective-permute-start.7 = (f32[72,128]{1,0:T(8,128)S(1)}, f32[72,128]{1,0:T(8,128)S(1)}, u32[]{:S(2)}, u32[]{:S(2)}) collective-permute-start(f32[72,128]{1,0:T(8,128)S(1)} %slice_add_fusion), channel_id=1, source_target_pairs={{0,192},{64,0},{128,64},{192,128},{1,193},{65,1},{129,65},{193,129... | collective-permute-start | bytes 110600 | tf_op jit(solution)/shard_map/ppermute | solution.py:386
  86.4 3.0 %collective-permute-start.6 = (f32[72,128]{1,0:T(8,128)S(1)}, f32[72,128]{1,0:T(8,128)S(1)}, u32[]{:S(2)}, u32[]{:S(2)}) collective-permute-start(f32[72,128]{1,0:T(8,128)S(1)} %slice_add_fusion), channel_id=1, source_target_pairs={{0,128},{64,192},{128,0},{192,64},{1,129},{65,193},{129,1},{193,65... | collective-permute-start | bytes 110600 | tf_op jit(solution)/shard_map/ppermute | solution.py:386
  89.3 2.3 %collective-permute-start.5 = (f32[72,128]{1,0:T(8,128)S(1)}, f32[72,128]{1,0:T(8,128)S(1)}, u32[]{:S(2)}, u32[]{:S(2)}) collective-permute-start(f32[72,128]{1,0:T(8,128)S(1)} %slice_add_fusion), channel_id=1, source_target_pairs={{0,64},{64,128},{128,192},{192,0},{1,65},{65,129},{129,193},{193,1... | collective-permute-start | bytes 110600 | tf_op jit(solution)/shard_map/ppermute | solution.py:386
  91.6 1.4 %collective-permute-done.6 = f32[72,128]{1,0:T(8,128)S(1)} collective-permute-done((f32[72,128]{1,0:T(8,128)S(1)}, f32[72,128]{1,0:T(8,128)S(1)}, u32[]{:S(2)}, u32[]{:S(2)}) %collective-permute-start.6) | collective-permute-done | bytes 36896 | tf_op jit(solution)/shard_map/ppermute | solution.py:386
  93.1 1.5 %collective-permute-done.5 = f32[72,128]{1,0:T(8,128)S(1)} collective-permute-done((f32[72,128]{1,0:T(8,128)S(1)}, f32[72,128]{1,0:T(8,128)S(1)}, u32[]{:S(2)}, u32[]{:S(2)}) %collective-permute-start.5) | collective-permute-done | bytes 36896 | tf_op jit(solution)/shard_map/ppermute | solution.py:386
  94.6 1.1 broadcast_in_dim.23
  95.7 9.4 %all-to-all-start.2 = ((f32[32,72,128]{2,1,0:T(8,128)}), f32[32,72,128]{2,1,0:T(8,128)S(1)}, u32[]{:S(2)}, u32[]{:S(2)}) async-start(f32[32,72,128]{2,1,0:T(8,128)} %broadcast_in_dim.23), calls=%async_computation.2 | async-start | bytes 2359296 | tf_op jit(solution)/shard_map/all_to_all | solution.py:371
  105.2 2.7 %collective-permute-start.10 = (f32[96,128]{1,0:T(8,128)S(1)}, f32[96,128]{1,0:T(8,128)S(1)}, u32[]{:S(2)}, u32[]{:S(2)}) collective-permute-start(f32[96,128]{1,0:T(8,128)S(1)} %collective-permute-done.3.one_ref), channel_id=1, source_target_pairs={{0,3},{1,0},{2,1},{3,2},{4,7},{5,4},{6,5},{7,6},{8,11},{9,8},{10,9... | collective-permute-start | bytes 147464 | tf_op jit(solution)/shard_map/ppermute | solution.py:386
  107.9 0.6 collective-permute-start.9
  108.4 0.6 collective-permute-start.8
  109.0 9.0 %collective-permute-done.10.four_ref = f32[96,128]{1,0:T(8,128)S(1)} collective-permute-done((f32[96,128]{1,0:T(8,128)S(1)}, f32[96,128]{1,0:T(8,128)S(1)}, u32[]{:S(2)}, u32[]{:S(2)}) %collective-permute-start.10) | collective-permute-done | bytes 49184 | tf_op jit(solution)/shard_map/ppermute | solution.py:386
  118.0 1.9 %collective-permute-done.9.three_ref = f32[96,128]{1,0:T(8,128)S(1)} collective-permute-done((f32[96,128]{1,0:T(8,128)S(1)}, f32[96,128]{1,0:T(8,128)S(1)}, u32[]{:S(2)}, u32[]{:S(2)}) %collective-permute-start.9) | collective-permute-done | bytes 49184 | tf_op jit(solution)/shard_map/ppermute | solution.py:386
  120.0 1.7 %blocks.1 = f32[81,1024]{1,0:T(8,128)} custom-call(s32[1,64]{1,0:T(1,128)} %counts_ref.2, f32[96,128]{1,0:T(8,128)S(1)} %collective-permute-done.3.one_ref, f32[96,128]{1,0:T(8,128)S(1)} %collective-permute-done.8.two_ref, f32[96,128]{1,0:T(8,128)S(1)} %collective-permute-done.9.three_ref, f32[96,128]{1,0:T(8,128)S(1)} %collective-permute-done.10.four_ref, ...), custom_call_target="tpu_custom_call" | custom-call | tf_op jit(solution)/shard_map/blocks/pallas_call | solution.py:324
  121.6 4.1 %collective-permute-start.11 = (f32[32,72,128]{2,1,0:T(8,128)S(1)}, f32[32,72,128]{2,1,0:T(8,128)S(1)}, u32[]{:S(2)}, u32[]{:S(2)}) collective-permute-start(f32[32,72,128]{2,1,0:T(8,128)S(1)} %all-to-all-done.2.rows_ref), channel_id=1, source_target_pairs={{0,4},{4,0},{1,5},{5,1},{2,6},{6,2},{3,7},{7,3},{8,12},{12,8},{9,1... | collective-permute-start | bytes 3538952 | tf_op jit(solution)/shard_map/ppermute | solution.py:386
  125.7 1.8 %order.2.refs_0_ = f32[9,65536]{1,0:T(8,128)} custom-call(s32[1]{0:T(128)} %bitcast.core_ref, f32[32,72,128]{2,1,0:T(8,128)S(1)} %all-to-all-done.2.rows_ref), custom_call_target="tpu_custom_call" | custom-call | tf_op jit(solution)/shard_map/order/pallas_call | solution.py:356
  127.6 0.6 collective-permute-done.11.rows_ref
  128.2 1.8 %order.3 = f32[9,65536]{1,0:T(8,128)} custom-call(s32[1]{0:T(128)} %bitcast.core_ref, f32[32,72,128]{2,1,0:T(8,128)S(1)} %collective-permute-done.11.rows_ref, f32[9,65536]{1,0:T(8,128)} %order.2.refs_0_), custom_call_target="tpu_custom_call", output_to_operand_aliasing={{}: (2, {})} | custom-call | tf_op jit(solution)/shard_map/order/pallas_call | solution.py:356
  (21 shorter events, 0.8 us)
Async XLA Ops:
  46.3 19.7 %copy-start.1 = (s32[1,64]{1,0:T(1,128)S(1)}, s32[1,64]{1,0:T(1,128)}, u32[]{:S(2)}) copy-start(s32[1,64]{1,0:T(1,128)} %counts_ref.2) | copy-start | bytes 772
  46.3 21.0 %copy-start = (s32[65536]{0:T(1024)S(1)}, s32[65536]{0:T(1024)}, u32[]{:S(2)}) copy-start(s32[65536]{0:T(1024)} %param.9) | copy-start | bytes 786436
  46.3 9.7 %collective-permute-start = (f32[128,128]{1,0:T(8,128)S(1)}, f32[128,128]{1,0:T(8,128)S(1)}, u32[]{:S(2)}, u32[]{:S(2)}) collective-permute-start(f32[128,128]{1,0:T(8,128)S(1)} %get-tuple-element.18), channel_id=1, source_target_pairs={{0,64},{64,128},{128,192},{192,0},{1,65},{65,129},{129,193},{193,1... | collective-permute-start | bytes 196616 | tf_op jit(solution)/shard_map/ppermute | solution.py:386
  49.4 7.0 %collective-permute-start.1 = (f32[128,128]{1,0:T(8,128)S(1)}, f32[128,128]{1,0:T(8,128)S(1)}, u32[]{:S(2)}, u32[]{:S(2)}) collective-permute-start(f32[128,128]{1,0:T(8,128)S(1)} %get-tuple-element.19), channel_id=1, source_target_pairs={{0,128},{64,192},{128,0},{192,64},{1,129},{65,193},{129,1},{193,65... | collective-permute-start | bytes 196616 | tf_op jit(solution)/shard_map/ppermute | solution.py:386
  53.6 5.9 %collective-permute-start.2 = (f32[128,128]{1,0:T(8,128)S(1)}, f32[128,128]{1,0:T(8,128)S(1)}, u32[]{:S(2)}, u32[]{:S(2)}) collective-permute-start(f32[128,128]{1,0:T(8,128)S(1)} %get-tuple-element.20), channel_id=1, source_target_pairs={{0,192},{64,0},{128,64},{192,128},{1,193},{65,1},{129,65},{193,129... | collective-permute-start | bytes 196616 | tf_op jit(solution)/shard_map/ppermute | solution.py:386
  60.4 15.2 %all-to-all-start.1 = ((f32[32,32,128]{2,1,0:T(8,128)}), f32[32,32,128]{2,1,0:T(8,128)S(1)}, u32[]{:S(2)}, u32[]{:S(2)}) async-start(f32[32,32,128]{2,1,0:T(8,128)} %broadcast_in_dim.20), calls=%async_computation.1 | async-start | bytes 1048576 | tf_op jit(solution)/shard_map/all_to_all | solution.py:371
  67.7 0.7 collective-permute-start.3
  78.6 4.0 %collective-permute-start.4 = (f32[296,128]{1,0:T(8,128)S(1)}, f32[296,128]{1,0:T(8,128)S(1)}, u32[]{:S(2)}, u32[]{:S(2)}) collective-permute-start(f32[296,128]{1,0:T(8,128)S(1)} %get-tuple-element.26), channel_id=1, source_target_pairs={{0,4},{4,0},{1,5},{5,1},{2,6},{6,2},{3,7},{7,3},{8,12},{12,8},{9,1... | collective-permute-start | bytes 454664 | tf_op jit(solution)/shard_map/ppermute | solution.py:386
  82.5 9.1 %collective-permute-start.7 = (f32[72,128]{1,0:T(8,128)S(1)}, f32[72,128]{1,0:T(8,128)S(1)}, u32[]{:S(2)}, u32[]{:S(2)}) collective-permute-start(f32[72,128]{1,0:T(8,128)S(1)} %slice_add_fusion), channel_id=1, source_target_pairs={{0,192},{64,0},{128,64},{192,128},{1,193},{65,1},{129,65},{193,129... | collective-permute-start | bytes 110600 | tf_op jit(solution)/shard_map/ppermute | solution.py:386
  86.4 6.7 %collective-permute-start.6 = (f32[72,128]{1,0:T(8,128)S(1)}, f32[72,128]{1,0:T(8,128)S(1)}, u32[]{:S(2)}, u32[]{:S(2)}) collective-permute-start(f32[72,128]{1,0:T(8,128)S(1)} %slice_add_fusion), channel_id=1, source_target_pairs={{0,128},{64,192},{128,0},{192,64},{1,129},{65,193},{129,1},{193,65... | collective-permute-start | bytes 110600 | tf_op jit(solution)/shard_map/ppermute | solution.py:386
  89.3 5.3 %collective-permute-start.5 = (f32[72,128]{1,0:T(8,128)S(1)}, f32[72,128]{1,0:T(8,128)S(1)}, u32[]{:S(2)}, u32[]{:S(2)}) collective-permute-start(f32[72,128]{1,0:T(8,128)S(1)} %slice_add_fusion), channel_id=1, source_target_pairs={{0,64},{64,128},{128,192},{192,0},{1,65},{65,129},{129,193},{193,1... | collective-permute-start | bytes 110600 | tf_op jit(solution)/shard_map/ppermute | solution.py:386
  95.7 25.9 %all-to-all-start.2 = ((f32[32,72,128]{2,1,0:T(8,128)}), f32[32,72,128]{2,1,0:T(8,128)S(1)}, u32[]{:S(2)}, u32[]{:S(2)}) async-start(f32[32,72,128]{2,1,0:T(8,128)} %broadcast_in_dim.23), calls=%async_computation.2 | async-start | bytes 2359296 | tf_op jit(solution)/shard_map/all_to_all | solution.py:371
  105.2 12.9 %collective-permute-start.10 = (f32[96,128]{1,0:T(8,128)S(1)}, f32[96,128]{1,0:T(8,128)S(1)}, u32[]{:S(2)}, u32[]{:S(2)}) collective-permute-start(f32[96,128]{1,0:T(8,128)S(1)} %collective-permute-done.3.one_ref), channel_id=1, source_target_pairs={{0,3},{1,0},{2,1},{3,2},{4,7},{5,4},{6,5},{7,6},{8,11},{9,8},{10,9... | collective-permute-start | bytes 147464 | tf_op jit(solution)/shard_map/ppermute | solution.py:386
  107.9 12.1 %collective-permute-start.9 = (f32[96,128]{1,0:T(8,128)S(1)}, f32[96,128]{1,0:T(8,128)S(1)}, u32[]{:S(2)}, u32[]{:S(2)}) collective-permute-start(f32[96,128]{1,0:T(8,128)S(1)} %collective-permute-done.3.one_ref), channel_id=1, source_target_pairs={{0,2},{1,3},{2,0},{3,1},{4,6},{5,7},{6,4},{7,5},{8,10},{9,11},{10,... | collective-permute-start | bytes 147464 | tf_op jit(solution)/shard_map/ppermute | solution.py:386
  108.4 11.5 %collective-permute-start.8 = (f32[96,128]{1,0:T(8,128)S(1)}, f32[96,128]{1,0:T(8,128)S(1)}, u32[]{:S(2)}, u32[]{:S(2)}) collective-permute-start(f32[96,128]{1,0:T(8,128)S(1)} %collective-permute-done.3.one_ref), channel_id=1, source_target_pairs={{0,1},{1,2},{2,3},{3,0},{4,5},{5,6},{6,7},{7,4},{8,9},{9,10},{10,1... | collective-permute-start | bytes 147464 | tf_op jit(solution)/shard_map/ppermute | solution.py:386
  121.6 6.6 %collective-permute-start.11 = (f32[32,72,128]{2,1,0:T(8,128)S(1)}, f32[32,72,128]{2,1,0:T(8,128)S(1)}, u32[]{:S(2)}, u32[]{:S(2)}) collective-permute-start(f32[32,72,128]{2,1,0:T(8,128)S(1)} %all-to-all-done.2.rows_ref), channel_id=1, source_target_pairs={{0,4},{4,0},{1,5},{5,1},{2,6},{6,2},{3,7},{7,3},{8,12},{12,8},{9,1... | collective-permute-start | bytes 3538952 | tf_op jit(solution)/shard_map/ppermute | solution.py:386
